TPU v7x, 32 devices: a whole 2x2x4 slice. The times are simulated.
32 devices in a mesh: group: 4 (over y, x), dev: 8 (over z, core).
Axes of the slice: x: 2, y: 2, z: 4, core: 2. Of those that a mesh axis runs over, the one named last changes fastest.
Arguments:
- node_feats: bfloat16 [8192, 1024], P(('group', 'dev')), may hold values from -60 to 60
- w_gcn: bfloat16 [1024, 1024], replicated, may hold values from -0.1875 to 0.1875
- adj_tiles: bfloat16 [64, 16, 128, 128], P(('group', 'dev')), may hold values from -0.125 to 0.125
- neighbor_blocks: int32 [64, 16], P(('group', 'dev')), may hold values from 0 to 21, all different within a row
- inner_rows: int32 [32, 8, 256], P(('group', 'dev')), may hold values from 0 to 255
- outer_rows: int32 [32, 4, 128], P(('group', 'dev')), may hold values from 0 to 255
- w_qkv: bfloat16 [1024, 3072], replicated, may hold values from -0.1875 to 0.1875
- key_blocks: int32 [64, 16], P('group'), may hold values from 0 to 15, all different within a row
- key_counts: int32 [64], P('group'), may hold values from 1 to 16
- w_out: bfloat16 [1024, 1024], replicated, may hold values from -0.1875 to 0.1875
- w_up: bfloat16 [1024, 2048], replicated, may hold values from -0.1875 to 0.1875
- w_down: bfloat16 [2048, 1024], replicated, may hold values from -0.125 to 0.125
Outputs:
- layer_out: bfloat16 [8192, 1024], P(('group', 'dev'))
Inputs may be any that keep to these rules, and one draw needn't show every extreme that they name: `inner_rows`: row numbers of the sending device. `outer_rows`: row numbers of the sending device. `neighbor_blocks`: table block numbers; the 16 entries of a row differ. `key_blocks`: the 16 entries of a row differ.
All inputs are finite; a program needn't handle non-finite values.
Results may differ from a plain program's by a relative error of at most 0.012.
The roundings to bfloat16 on the way count: a program that leaves them out, or rounds other values in their place, can miss the bound.
Values may be sent and summed in bfloat16 or wider, within the bound.
No kernel may reach another device: no remote copies, remote signals or barrier semaphores. Data moves between devices by JAX's collectives and lax.ppermute only.
A program may use at most 128 MiB of HBM per device.

v0:
```python
import jax
import jax.numpy as jnp
from jax import lax
from jax.sharding import PartitionSpec as P

H = 32


def layer_norm(values):
    average = jnp.mean(values, axis=-1, keepdims=True)
    centered = values - average
    variance = jnp.mean(centered * centered, axis=-1, keepdims=True)
    return centered / jnp.sqrt(variance + 1e-05)


def per_device(
    node_feats,
    w_gcn,
    adj_tiles,
    neighbor_blocks,
    inner_rows,
    outer_rows,
    w_qkv,
    key_blocks,
    key_counts,
    w_out,
    w_up,
    w_down,
):
    row_count = node_feats.shape[0]
    width = node_feats.shape[1]
    block_rows = adj_tiles.shape[-1]
    peers = lax.axis_size("dev")
    clusters = lax.axis_size("group")
    head_size = width // H
    local_heads = H // peers
    head_cols = local_heads * head_size
    gcn_rows = jnp.dot(node_feats, w_gcn, preferred_element_type=jnp.float32).astype(jnp.bfloat16)
    qkv_split = jnp.einsum(
        "rd,dtph->pthr",
        node_feats,
        w_qkv.reshape(width, 3, peers, head_cols),
        preferred_element_type=jnp.float32,
    ).astype(jnp.bfloat16)
    whole_rows, whole_lists = (
        lax.all_gather(gcn_rows, "dev", axis=0, tiled=True),
        lax.all_gather(inner_rows, "dev", axis=0, tiled=True),
    )
    chosen_lists = lax.dynamic_index_in_dim(
        whole_lists, lax.axis_index("dev"), axis=1, keepdims=False
    )
    inner_index = (jnp.arange(peers, dtype=jnp.int32)[:, None] * row_count + chosen_lists).reshape(
        -1
    )
    inner_part = whole_rows[inner_index]
    far_rows, far_lists = (
        lax.all_gather(gcn_rows, "group", axis=0, tiled=True),
        lax.all_gather(outer_rows, "group", axis=0, tiled=True),
    )
    chosen_far = lax.dynamic_index_in_dim(
        far_lists, lax.axis_index("group"), axis=1, keepdims=False
    )
    outer_index = (jnp.arange(clusters, dtype=jnp.int32)[:, None] * row_count + chosen_far).reshape(
        -1
    )
    outer_part = far_rows[outer_index]
    head_parts = lax.all_to_all(qkv_split, "dev", split_axis=0, concat_axis=3, tiled=True)
    table = jnp.concatenate([gcn_rows, inner_part, outer_part], axis=0)
    table_count = table.shape[0] // block_rows
    selector = (
        neighbor_blocks[:, :, None] == jnp.arange(table_count, dtype=jnp.int32)[None, None, :]
    ).astype(jnp.bfloat16)
    spread = jnp.einsum(
        "bst,bsij->bitj", selector, adj_tiles, preferred_element_type=jnp.float32
    ).astype(jnp.bfloat16)
    agg = jnp.dot(
        spread.reshape(row_count, table_count * block_rows),
        table,
        preferred_element_type=jnp.float32,
    )
    features = node_feats.astype(jnp.float32)
    local_branch = layer_norm(features + agg)
    group_rows = row_count * peers
    block_total = group_rows // block_rows
    per_step = 8
    steps_total = block_total // per_step
    head_parts = head_parts.reshape(3, local_heads, head_size, block_total, block_rows)
    query_part = (
        head_parts[0]
        .reshape(local_heads, head_size, steps_total, per_step, block_rows)
        .transpose(2, 0, 1, 3, 4)
    )
    key_value = head_parts[1:3]
    scale = 1.0 / head_size**0.5
    slot_count = key_blocks.shape[1]

    def attend(inputs):
        picks, counts, queries = inputs
        picker = (
            picks[:, :, None] == jnp.arange(block_total, dtype=jnp.int32)[None, None, :]
        ).astype(jnp.bfloat16)
        picked = jnp.einsum(
            "qst,kletj->kleqsj", picker, key_value, preferred_element_type=jnp.float32
        ).astype(jnp.bfloat16)
        keys_here = picked[0]
        values_here = picked[1]
        scores = (
            jnp.einsum("leqi,leqsj->qlisj", queries, keys_here, preferred_element_type=jnp.float32)
            * scale
        )
        live = jnp.arange(slot_count, dtype=jnp.int32)[None, :] < counts[:, None]
        scores = jnp.where(live[:, None, None, :, None], scores, -jnp.inf)
        highest = jnp.max(scores, axis=(3, 4), keepdims=True)
        expos = jnp.exp(scores - highest)
        totals = jnp.sum(expos, axis=(3, 4), keepdims=True)
        probs = (expos / totals).astype(jnp.bfloat16)
        mixed = jnp.einsum(
            "qlisj,leqsj->leqi", probs, values_here, preferred_element_type=jnp.float32
        )
        return mixed.astype(jnp.bfloat16)

    attended = lax.map(
        attend,
        (
            key_blocks.reshape(steps_total, per_step, slot_count),
            key_counts.reshape(steps_total, per_step),
            query_part,
        ),
    )
    attended = attended.transpose(1, 2, 0, 3, 4).reshape(head_cols, group_rows)
    returned = lax.all_to_all(attended, "dev", split_axis=1, concat_axis=0, tiled=True)
    projected = lax.dot_general(
        returned, w_out, (((0,), (0,)), ((), ())), preferred_element_type=jnp.float32
    )
    attn_branch = layer_norm(features + projected)
    summed = local_branch + attn_branch
    summed_in = summed.astype(jnp.bfloat16)
    activated = jax.nn.gelu(jnp.dot(summed_in, w_up, preferred_element_type=jnp.float32)).astype(
        jnp.bfloat16
    )
    layer_out = layer_norm(summed + jnp.dot(activated, w_down, preferred_element_type=jnp.float32))
    return layer_out.astype(jnp.bfloat16)


def solution(mesh):
    placed = (
        P(("group", "dev"), None),
        P(),
        P(("group", "dev"), None, None, None),
        P(("group", "dev"), None),
        P(("group", "dev"), None, None),
        P(("group", "dev"), None, None),
        P(),
        P("group", None),
        P("group"),
        P(),
        P(),
        P(),
    )
    return jax.shard_map(
        per_device, mesh=mesh, in_specs=placed, out_specs=P(("group", "dev"), None), check_vma=False
    )
```

profile of v0, /device:TPU:0, one launch (start us, length us, event | category | flops | bytes accessed | tf_op | source)
XLA Modules:
  0.0 267.3 jit_solution(1727776612422304538)
XLA Ops:
  6.5 0.0 copy-start
  6.5 3.4 %convolution_convert_fusion.2 = bf16[256,1024]{1,0:T(8,128)(2,1)} fusion(bf16[256,1024]{1,0:T(8,128)(2,1)} %param.14, bf16[1024,1024]{1,0:T(8,128)(2,1)} %param.15), kind=kOutput, calls=%fused_computation.52 | convolution fusion | flops 537133056 | bytes 3145728 | tf_op jit(solution)/shard_map/dot_general | solution.py:38
  9.9 0.0 all-gather.5.cloned.1.call-update
  10.0 0.0 copy-start.4
  10.0 8.7 %copy.49 = bf16[1024,3072]{0,1:T(8,128)(2,1)} copy(bf16[1024,3072]{1,0:T(8,128)(2,1)} %param.20) | data formatting | bytes 12582912 | tf_op jit(solution)/shard_map/reshape | solution.py:42
  18.7 0.0 copy-done.4
  18.7 5.0 %fusion.46 = bf16[8,3,128,256]{3,2,0,1:T(8,128)(2,1)S(1)} fusion(bf16[1024,3,8,128]{0,3,2,1:T(8,128)(2,1)} %bitcast.118, bf16[256,1024]{1,0:T(8,128)(2,1)S(1)} %copy-done.4), kind=kOutput, calls=%fused_computation.46 | convolution fusion | flops 1611399168 | bytes 8388608 | tf_op jit(solution)/shard_map/rd,dtph->pthr/dot_general | solution.py:39
  23.7 0.0 copy-start.12
  23.7 0.0 copy-start.10
  23.7 0.0 copy-start.9
  23.7 1.3 copy.35
  25.0 6.2 %all-to-all-start = ((bf16[8,3,128,256]{3,2,1,0:T(8,128)(2,1)}), bf16[8,3,128,256]{3,2,1,0:T(8,128)(2,1)}, u32[]{:S(2)}, u32[]{:S(2)}) async-start(bf16[8,3,128,256]{3,2,1,0:T(8,128)(2,1)} %copy.35), calls=%async_computation | async-start | bytes 3145728 | tf_op jit(solution)/shard_map/all_to_all | solution.py:67
  31.2 0.0 all-gather.3.cloned.1.call-start
  31.2 0.7 all-gather.3.cloned.1.call-update
  31.9 0.1 reshape.158
  32.0 0.1 broadcast_bitcast_fusion
  32.1 0.6 copy.52
  32.7 8.4 %all_gather.15 = s32[4,4,128]{2,1,0:T(4,128)S(1)} all-gather(s32[1,4,128]{2,1,0:T(4,128)S(1)} %copy-done.10), channel_id=1, replica_groups=mesh['group'=4,'dev'=8] {'group'}, dimensions={0}, use_global_device_ids=true | all-gather | bytes 10240 | tf_op jit(solution)/shard_map/all_gather | solution.py:58
  41.1 53.9 %all_gather.13 = s32[8,8,256]{2,1,0:T(8,128)S(1)} all-gather(s32[1,8,256]{2,1,0:T(8,128)S(1)} %copy-done.9), channel_id=1, replica_groups=mesh['group'=4,'dev'=8] {'dev'}, dimensions={0}, use_global_device_ids=true | all-gather | bytes 73728 | tf_op jit(solution)/shard_map/all_gather | solution.py:47
  95.0 0.1 add.124
  95.0 0.6 pad_clamp_fusion
  95.6 0.6 constant_dynamic-slice_fusion.2
  96.2 0.0 all-to-all-done
  96.2 1.3 slice.25
  97.5 0.0 copy-start.5
  97.5 1.9 slice.26
  99.4 0.6 copy.36
  100.0 1.4 slice.17
  101.4 1.3 copy.37
  102.7 1.0 reshape_squeeze.3
  103.7 0.0 copy-done.5
  103.7 98.9 %while.10 = (s32[]{:T(128)}, bf16[2,4,32,8,128]{4,2,3,1,0:T(8,128)(2,1)}, s32[2,8,16]{2,1,0:T(8,128)S(1)}, bf16[2,4,32,16,128]{4,3,2,1,0:T(8,128)(2,1)}, s32[2,8...) while((s32[]{:T(128)}, bf16[2,4,32,8,128]{4,2,3,1,0:T(8,128)(2,1)}, ...), condition=%wide.region_5.6_spmd, body=%wide.region_2.5_spmd.sunk | while | flops 1312942208 | bytes 138496240 | solution.py:122
  103.7 3.6 %convert_bitcast_fusion.2 = bf16[2,4,32,8,16,128]{5,4,2,1,0,3:T(8,128)(2,1)S(1)} fusion(bf16[2,4,32,16,128]{4,3,2,1,0:T(8,128)(2,1)} %get-tuple-element.136, s32[8,16]{1,0:T(8,128)S(1)} %dynamic-slice_bitcast_fusion.2), kind=kOutput, calls=%fused_computation.9.clone.1 | convolution fusion | flops 138414080 | bytes 9437696 | tf_op jit(solution)/shard_map/while/body/eval_jaxpr/qst,kletj->kleqsj/dot_general | solution.py:102
  107.3 1.5 slice_bitcast_fusion.3
  108.9 0.1 iota_compare_fusion.4
  109.0 15.2 %fusion.108 = (f32[8,4,128]{2,1,0:T(4,128)S(1)}, f32[8,4,128,16,128]{2,4,3,1,0:T(8,128)}) fusion(pred[8,16]{1,0:T(8,128)(4,1)S(1)} %iota_compare_fusion.4, bf16[4,32,8,16,128]{4,3,1,0,2:T(8,128)(2,1)S(1)} %get-tuple-element.116, bf16[1,4,32,8,128]{4,3,0,2,1:T(8,128)(2,1)S(1)} %constant_dynamic-slice_fusion.4), kind=kOutput, calls=%fused_computation.5.clone.1 | convolution fusion | flops 562032640 | bytes 38027392 | tf_op jit(solution)/shard_map/while/body/eval_jaxpr/leqi,leqsj->qlisj/dot_general | solution.py:108
  124.2 14.3 %fusion.109 = f32[8,4,128]{2,1,0:T(4,128)S(1)} fusion(f32[8,4,128,16,128]{2,4,3,1,0:T(8,128)} %get-tuple-element.117, f32[8,4,128]{2,1,0:T(4,128)S(1)} %get-tuple-element.118, pred[8,16]{1,0:T(8,128)(4,1)S(1)} %iota_compare_fusion.4), kind=kLoop, calls=%fused_computation.6.clone.1 | loop fusion | flops 33550336 | bytes 33587328 | tf_op jit(solution)/shard_map/while/body/eval_jaxpr/reduce_sum | solution.py:115
  138.5 14.7 %fusion.110 = bf16[2,4,32,8,128]{4,2,3,1,0:T(8,128)(2,1)} fusion(bf16[2,4,32,8,128]{4,2,3,1,0:T(8,128)(2,1)} %get-tuple-element.127, s32[]{:T(128)S(6)} %copy.102, bf16[4,32,8,16,128]{4,3,1,0,2:T(8,128)(2,1)S(1)} %get-tuple-element.115, f32[8,4,128,16,128]{2,4,3,1,0:T(8,128)} %get-tuple-element.117, f32[8,4,128]{2,1,0:T(4,128)S(1)} %fusion.109, ...), kind=kOutput, calls=%fused_computation.18.clone.1 | convolution fusion | flops 578945024 | bytes 38043780 | tf_op jit(solution)/shard_map/while/body/eval_jaxpr/qlisj,leqsj->leqi/dot_general | solution.py:117
  153.2 3.6 %convert_bitcast_fusion.2 = bf16[2,4,32,8,16,128]{5,4,2,1,0,3:T(8,128)(2,1)S(1)} fusion(bf16[2,4,32,16,128]{4,3,2,1,0:T(8,128)(2,1)} %get-tuple-element.136, s32[8,16]{1,0:T(8,128)S(1)} %dynamic-slice_bitcast_fusion.2), kind=kOutput, calls=%fused_computation.9.clone.1 | convolution fusion | flops 138414080 | bytes 9437696 | tf_op jit(solution)/shard_map/while/body/eval_jaxpr/qst,kletj->kleqsj/dot_general | solution.py:102
  156.8 1.5 slice_bitcast_fusion.3
  158.3 0.1 iota_compare_fusion.4
  158.4 0.0 copy-done.1
  158.4 15.2 %fusion.108 = (f32[8,4,128]{2,1,0:T(4,128)S(1)}, f32[8,4,128,16,128]{2,4,3,1,0:T(8,128)}) fusion(pred[8,16]{1,0:T(8,128)(4,1)S(1)} %iota_compare_fusion.4, bf16[4,32,8,16,128]{4,3,1,0,2:T(8,128)(2,1)S(1)} %get-tuple-element.116, bf16[1,4,32,8,128]{4,3,0,2,1:T(8,128)(2,1)S(1)} %constant_dynamic-slice_fusion.4), kind=kOutput, calls=%fused_computation.5.clone.1 | convolution fusion | flops 562032640 | bytes 38027392 | tf_op jit(solution)/shard_map/while/body/eval_jaxpr/leqi,leqsj->qlisj/dot_general | solution.py:108
  173.6 14.3 %fusion.109 = f32[8,4,128]{2,1,0:T(4,128)S(1)} fusion(f32[8,4,128,16,128]{2,4,3,1,0:T(8,128)} %get-tuple-element.117, f32[8,4,128]{2,1,0:T(4,128)S(1)} %get-tuple-element.118, pred[8,16]{1,0:T(8,128)(4,1)S(1)} %iota_compare_fusion.4), kind=kLoop, calls=%fused_computation.6.clone.1 | loop fusion | flops 33550336 | bytes 33587328 | tf_op jit(solution)/shard_map/while/body/eval_jaxpr/reduce_sum | solution.py:115
  187.9 14.7 %fusion.110 = bf16[2,4,32,8,128]{4,2,3,1,0:T(8,128)(2,1)} fusion(bf16[2,4,32,8,128]{4,2,3,1,0:T(8,128)(2,1)} %get-tuple-element.127, s32[]{:T(128)S(6)} %copy.102, bf16[4,32,8,16,128]{4,3,1,0,2:T(8,128)(2,1)S(1)} %get-tuple-element.115, f32[8,4,128,16,128]{2,4,3,1,0:T(8,128)} %get-tuple-element.117, f32[8,4,128]{2,1,0:T(4,128)S(1)} %fusion.109, ...), kind=kOutput, calls=%fused_computation.18.clone.1 | convolution fusion | flops 578945024 | bytes 38043780 | tf_op jit(solution)/shard_map/while/body/eval_jaxpr/qlisj,leqsj->leqi/dot_general | solution.py:117
  202.6 1.3 copy.39
  203.9 0.2 all_to_all.28
  204.1 0.9 copy.40
  205.0 5.7 %all-to-all-start.1 = ((bf16[128,8,256]{2,0,1:T(8,128)(2,1)}), bf16[128,8,256]{2,0,1:T(8,128)(2,1)S(1)}, u32[]{:S(2)}, u32[]{:S(2)}) async-start(bf16[128,8,256]{2,0,1:T(8,128)(2,1)} %copy.40), calls=%async_computation.1 | async-start | bytes 1048576 | tf_op jit(solution)/shard_map/all_to_all | solution.py:131
  210.7 0.0 copy-done.7
  210.7 3.3 %convolution_convert_fusion.1 = bf16[2,22,128,128]{3,1,2,0:T(8,128)(2,1)} fusion(bf16[2,16,128,128]{3,2,1,0:T(8,128)(2,1)} %param.16, s32[2,16]{1,0:T(2,128)S(1)} %copy-done.11), kind=kOutput, calls=%fused_computation.45 | convolution fusion | flops 23790272 | bytes 2490496 | tf_op jit(solution)/shard_map/bst,bsij->bitj/dot_general | solution.py:73
  214.1 5.4 %gather_fusion.1 = bf16[512,1024]{1,0:T(8,128)(2,1)} fusion(bf16[1024,1024]{1,0:T(8,128)(2,1)} %all-gather.5.cloned.1.call-done, s32[1024]{0:T(1024)S(1)} %copy-done.8), kind=kCustom, calls=%fused_computation.1 | custom fusion | bytes 2099200 | tf_op jit(solution)/shard_map/gather | solution.py:66
  219.4 6.6 %all-to-all-done.1 = bf16[128,8,256]{2,0,1:T(8,128)(2,1)S(1)} async-done(((bf16[128,8,256]{2,0,1:T(8,128)(2,1)}), bf16[128,8,256]{2,0,1:T(8,128)(2,1)S(1)}, u32[]{:S(2)}, u32[]{:S(2)}) %all-to-all-start.1) | async-done | bytes 524320 | tf_op jit(solution)/shard_map/all_to_all | solution.py:131
  226.0 0.8 copy-done.2
  226.8 2.0 fusion.83
  228.8 0.3 multiply_reduce_fusion.1
  229.1 0.0 all-gather.3.cloned.1.call-done
  229.1 13.7 %gather_fusion = bf16[2048,1024]{1,0:T(8,128)(2,1)} fusion(bf16[2048,1024]{1,0:T(8,128)(2,1)} %all-gather.3.cloned.1.call-done, s32[2048]{0:T(1024)S(1)} %broadcast_clamp_fusion), kind=kCustom, calls=%fused_computation | custom fusion | bytes 8396800 | tf_op jit(solution)/shard_map/gather | solution.py:55
  242.8 4.9 %fusion.84 = (f32[256]{0:T(256)S(1)}, f32[256,1024]{1,0:T(8,128)S(1)}) fusion(bf16[512,1024]{1,0:T(8,128)(2,1)} %gather_fusion.1, bf16[2048,1024]{1,0:T(8,128)(2,1)} %gather_fusion, bf16[256,1024]{1,0:T(8,128)(2,1)} %convolution_convert_fusion.2, bf16[32,8,22,128]{3,2,1,0:T(8,128)(2,1)} %bitcast.120, bf16[256,1024]{1,0:T(8,128)(2,1)} %param.14), kind=kOutput, calls=%fused_computation.94 | convolution fusion | flops 1494482688 | bytes 8782848 | tf_op jit(solution)/shard_map/dot_general | solution.py:76
  247.7 1.0 copy-done.3
  248.7 0.2 multiply_reduce_fusion.2
  248.9 7.9 %fusion.85 = (f32[256]{0:T(256)S(1)}, f32[256,1024]{1,0:T(8,128)}) fusion(bf16[2048,1024]{1,0:T(8,128)(2,1)} %param.25, bf16[1024,2048]{1,0:T(8,128)(2,1)} %param.24, f32[256,1024]{1,0:T(8,128)S(1)} %get-tuple-element.67, f32[256,1024]{1,0:T(8,128)} %copy-done.3, f32[256]{0:T(256)S(1)} %get-tuple-element.72, f32[256]{0:T(256)S(1)} %broadcast_multiply_fusion.1, ...), kind=kOutput, calls=%fused_computation.95 | convolution fusion | flops 2155609856 | bytes 11539456 | tf_op jit(solution)/shard_map/dot_general | solution.py:141
  256.8 1.5 multiply_reduce_fusion
  258.3 2.2 divide_convert_fusion.1
  (35 shorter events, 0.2 us)
Async XLA Ops:
  6.5 220.3 %copy-start = (bf16[1024,1024]{1,0:T(8,128)(2,1)S(1)}, bf16[1024,1024]{1,0:T(8,128)(2,1)}, u32[]{:S(2)}) copy-start(bf16[1024,1024]{1,0:T(8,128)(2,1)} %param.23) | copy-start | bytes 6291460
  6.5 207.5 %all-gather.5.cloned.1.call-start = ((), (), s32[]{:S(2)}) async-start(), calls=%async_computation.3 | async-start | bytes 2621440 | tf_op jit(solution)/shard_map/all_gather | solution.py:57
  10.0 8.7 %copy-start.4 = (bf16[256,1024]{1,0:T(8,128)(2,1)S(1)}, bf16[256,1024]{1,0:T(8,128)(2,1)}, u32[]{:S(2)}) copy-start(bf16[256,1024]{1,0:T(8,128)(2,1)} %param.14) | copy-start | bytes 1572868
  23.7 8.2 %copy-start.12 = (s32[16]{0:T(128)S(1)}, s32[16]{0:T(128)}, u32[]{:S(2)}) copy-start(s32[16]{0:T(128)} %param.22) | copy-start | bytes 196
  23.7 9.0 %copy-start.10 = (s32[1,4,128]{2,1,0:T(4,128)S(1)}, s32[1,4,128]{2,1,0:T(4,128)}, u32[]{:S(2)}) copy-start(s32[1,4,128]{2,1,0:T(4,128)} %param.19) | copy-start | bytes 6148
  23.7 17.4 %copy-start.9 = (s32[1,8,256]{2,1,0:T(8,128)S(1)}, s32[1,8,256]{2,1,0:T(8,128)}, u32[]{:S(2)}) copy-start(s32[1,8,256]{2,1,0:T(8,128)} %param.18) | copy-start | bytes 24580
  25.0 71.2 %all-to-all-start = ((bf16[8,3,128,256]{3,2,1,0:T(8,128)(2,1)}), bf16[8,3,128,256]{3,2,1,0:T(8,128)(2,1)}, u32[]{:S(2)}, u32[]{:S(2)}) async-start(bf16[8,3,128,256]{3,2,1,0:T(8,128)(2,1)} %copy.35), calls=%async_computation | async-start | bytes 3145728 | tf_op jit(solution)/shard_map/all_to_all | solution.py:67
  31.2 198.0 %all-gather.3.cloned.1.call-start = ((), (), s32[]{:S(2)}) async-start(), calls=%async_computation.2 | async-start | bytes 4718592 | tf_op jit(solution)/shard_map/all_gather | solution.py:46
  97.5 6.2 %copy-start.5 = (s32[16,16]{1,0:T(8,128)S(1)}, s32[16,16]{1,0:T(8,128)}, u32[]{:S(2)}) copy-start(s32[16,16]{1,0:T(8,128)} %param.21) | copy-start | bytes 3076
  107.3 1.6 copy-start.1
  156.8 1.6 copy-start.1
  202.6 8.1 %copy-start.6 = (s32[1,1,8,256]{3,1,2,0:T(1,128)S(1)}, s32[1,1,8,256]{3,1,2,0:T(1,128)}, u32[]{:S(2)}) copy-start(s32[1,1,8,256]{3,1,2,0:T(1,128)} %copy.52) | copy-start | bytes 24580
  202.6 8.1 %copy-start.7 = (s32[8,1,256]{2,1,0:T(1,128)S(1)}, s32[8,1,256]{2,1,0:T(1,128)}, u32[]{:S(2)}) copy-start(s32[8,1,256]{2,1,0:T(1,128)} %constant_dynamic-slice_fusion.2) | copy-start | bytes 24580
  202.6 8.1 %copy-start.11 = (s32[2,16]{1,0:T(2,128)S(1)}, s32[2,16]{1,0:T(2,128)}, u32[]{:S(2)}) copy-start(s32[2,16]{1,0:T(2,128)} %param.17) | copy-start | bytes 388
  202.6 11.5 %copy-start.8 = (s32[1024]{0:T(1024)S(1)}, s32[1024]{0:T(1024)}, u32[]{:S(2)}) copy-start(s32[1024]{0:T(1024)} %pad_clamp_fusion) | copy-start | bytes 12292
  205.0 21.0 %all-to-all-start.1 = ((bf16[128,8,256]{2,0,1:T(8,128)(2,1)}), bf16[128,8,256]{2,0,1:T(8,128)(2,1)S(1)}, u32[]{:S(2)}, u32[]{:S(2)}) async-start(bf16[128,8,256]{2,0,1:T(8,128)(2,1)} %copy.40), calls=%async_computation.1 | async-start | bytes 1048576 | tf_op jit(solution)/shard_map/all_to_all | solution.py:131
  226.0 0.8 copy-start.2
  247.7 1.0 copy-start.3
Sparse Core Ops, SparseCore 0:
  10.1 37.9 all-gather.4
  49.7 55.0 all-gather.2
where the time goes:
time: 269 us; the launch traced here: 267 us
  matrix products  93.5 us (35%)
  blocking collectives  62.2 us (23%)
  local copies, waits for them, and re-layouts  45.2 us (17%)
  other arithmetic  33.6 us (12%)
  between operations  13.6 us (5%)
  starting transfers between devices  11.9 us (4%)
  waiting for transfers between devices  7.31 us (3%)
    all_gather x1, blocking collectives, per_device(): lax.all_gather(inner_rows, 'dev', axis=0, tiled=True)  53.9 us
    dot_general x2, matrix products, attend(): jnp.einsum('leqi,leqsj->qlisj', queries, keys_here, preferred_element_typ...  30.4 us
    dot_general x2, matrix products, attend(): jnp.einsum('qlisj,leqsj->leqi', probs, values_here, preferred_element_typ...  29.3 us
    reduce_sum x2, other arithmetic, attend(): totals = jnp.sum(expos, axis=(3, 4), keepdims=True)  28.6 us
    gather x1, local copies, waits for them, and re-layouts, per_device(): inner_part = whole_rows[inner_index]  13.7 us
    reshape x1, local copies, waits for them, and re-layouts, per_device(): w_qkv.reshape(width, 3, peers, head_cols)  8.68 us
    all_gather x1, blocking collectives, per_device(): lax.all_gather(outer_rows, 'group', axis=0, tiled=True)  8.39 us
    dot_general x1, matrix products, per_device(): jnp.dot(activated, w_down, preferred_element_type=jnp.float32)  7.85 us
  transfers between devices with their start and end apart: 4, of which 1 were waited for; matrix products, arithmetic and copies ran while one was open for 51% of the time, Pallas kernels for 0%

commit v1 on v0

--- a/solution.py
+++ b/solution.py
@@ -1,9 +1,16 @@
+import functools
+import math
+
 import jax
 import jax.numpy as jnp
 from jax import lax
+from jax.experimental import pallas as pl
+from jax.experimental.pallas import tpu as pltpu
 from jax.sharding import PartitionSpec as P
 
 H = 32
+LOW = -1e30
+CORES = 2
 
 
 def layer_norm(values):
@@ -13,7 +20,7 @@
     return centered / jnp.sqrt(variance + 1e-05)
 
 
-def per_device(
+def gathered_plan(
     node_feats,
     w_gcn,
     adj_tiles,
@@ -142,6 +149,459 @@
     return layer_out.astype(jnp.bfloat16)
 
 
+BF = jnp.bfloat16
+F32 = jnp.float32
+SMEM = pl.BlockSpec(memory_space=pltpu.SMEM)
+VMEM = pl.BlockSpec(memory_space=pltpu.VMEM)
+
+
+def mm(a, b, dims):
+    return lax.dot_general(a, b, (dims, ((), ())), preferred_element_type=F32)
+
+
+def attend_kernel(first, sources, rows, block, heads_step, scale, *refs):
+    info, key_blocks, key_counts, *refs = refs
+    if first:
+        own, partner, wq, wk, wv, qt_ref, max_ref, sum_ref, acc_ref, live_ref = refs
+        pieces = [own]
+    else:
+        pieces = refs[:sources]
+        wk, wv, qt_in, max_in, sum_in, acc_in, max_ref, sum_ref, acc_ref, live_ref = refs[sources:]
+    per_dev = rows // block
+    slots = key_blocks.shape[1]
+    chip = info[0]
+    width_step = wk.shape[1]
+    head = width_step // heads_step
+    packed = 128 // head
+    queries = CORES * rows
+
+    @pl.when(pl.program_id(0) == 0)
+    def _():
+        for p in range(len(pieces)):
+            for j in range(per_dev):
+                wanted = info[1 + p] * per_dev + j
+                for i in range(CORES * per_dev):
+                    at = info[8 + i]
+                    count = key_counts[at]
+                    hit = jnp.int32(0)
+                    for s in range(slots):
+                        hit = jnp.where((key_blocks[at, s] == wanted) & (s < count), 1, hit)
+                    live_ref[(p * per_dev + j) * CORES * per_dev + i] = hit
+
+    if first:
+        q_own = mm(own[0:rows, :], wq[...], ((1,), (0,))).astype(BF)
+        q_par = mm(partner[0:rows, :], wq[...], ((1,), (0,))).astype(BF)
+        qt_ref[:, 0:rows] = q_own.T
+        qt_ref[:, rows:queries] = q_par.T
+        max_ref[...] = jnp.full(max_ref.shape, LOW, F32)
+        sum_ref[...] = jnp.zeros(sum_ref.shape, F32)
+        acc_ref[...] = jnp.zeros(acc_ref.shape, F32)
+        qt = qt_ref
+    else:
+        max_ref[...] = max_in[...]
+        sum_ref[...] = sum_in[...]
+        acc_ref[...] = acc_in[...]
+        qt = qt_in
+    belongs = lax.broadcasted_iota(jnp.int32, (128, queries), 0) // head
+
+    for p, piece in enumerate(pieces):
+
+        @pl.when(info[1 + sources + p] != 0)
+        def _(p=p, piece=piece):
+            x = piece[0:rows, :]
+            keys = mm(x, wk[...], ((1,), (0,))).astype(BF)
+            values = mm(x, wv[...], ((1,), (0,))).astype(BF).T
+            alive = []
+            for j in range(per_dev):
+                base = (p * per_dev + j) * CORES * per_dev
+                alive.append(
+                    jnp.concatenate(
+                        [
+                            jnp.full((1, block), live_ref[base + i], jnp.int32)
+                            for i in range(CORES * per_dev)
+                        ],
+                        axis=1,
+                    )
+                    != 0
+                )
+            ones = jnp.ones((16, rows), BF)
+            for h in range(heads_step):
+                lane = (h // packed) * 128
+                q_head = jnp.where(belongs == h % packed, qt[lane : lane + 128, :], 0).astype(BF)
+                scores = mm(keys[:, lane : lane + 128], q_head, ((1,), (0,)))
+                parts = [scores[j * block : (j + 1) * block] for j in range(per_dev)]
+                top = max_ref[h : h + 1, :]
+                new_top = top
+                for j in range(per_dev):
+                    peak = jnp.max(parts[j], axis=0, keepdims=True) * scale
+                    new_top = jnp.maximum(new_top, jnp.where(alive[j], peak, LOW))
+                probs = jnp.concatenate(
+                    [
+                        jnp.exp2(parts[j] * scale - jnp.where(alive[j], new_top, -LOW))
+                        for j in range(per_dev)
+                    ],
+                    axis=0,
+                ).astype(BF)
+                left = jnp.concatenate([values[h * head : (h + 1) * head, :], ones], axis=0)
+                mixed = mm(left, probs, ((1,), (0,)))
+                fade = jnp.exp2(top - new_top)
+                max_ref[h : h + 1, :] = new_top
+                sum_ref[h : h + 1, :] = sum_ref[h : h + 1, :] * fade + mixed[head : head + 1, :]
+                at = slice(h * head, (h + 1) * head)
+                acc_ref[at, :] = acc_ref[at, :] * fade + mixed[0:head, :]
+
+
+def attend_call(first, pieces, state, info, key_blocks, key_counts, w_qkv, rows, block, name):
+    width = pieces[0].shape[1]
+    head = width // H
+    step = 256
+    groups = width // step
+    heads_step = step // head
+    queries = CORES * rows
+    whole = lambda a: pl.BlockSpec(a.shape, lambda g: (0,) * a.ndim)
+    weight = lambda part: pl.BlockSpec((width, step), lambda g, part=part: (0, part * groups + g))
+    tall = pl.BlockSpec((step, queries), lambda g: (g, 0))
+    small = pl.BlockSpec((heads_step, queries), lambda g: (g, 0))
+    shapes = [
+        jax.ShapeDtypeStruct((H, queries), F32),
+        jax.ShapeDtypeStruct((H, queries), F32),
+        jax.ShapeDtypeStruct((width, queries), F32),
+    ]
+    count = 1 if first else len(pieces)
+    scale = math.log2(math.e) / math.sqrt(head)
+    kernel = functools.partial(attend_kernel, first, count, rows, block, heads_step, scale)
+    if first:
+        in_specs = [SMEM] * 3 + [whole(p) for p in pieces] + [weight(0), weight(1), weight(2)]
+        out_specs = [tall, small, small, tall]
+        out_shape = [jax.ShapeDtypeStruct((width, queries), BF)] + shapes
+        args = [info, key_blocks, key_counts, *pieces, w_qkv, w_qkv, w_qkv]
+        aliases = {}
+    else:
+        qt, top, total, acc = state
+        in_specs = (
+            [SMEM] * 3 + [whole(p) for p in pieces] + [weight(1), weight(2), tall, small, small, tall]
+        )
+        out_specs = [small, small, tall]
+        out_shape = shapes
+        args = [info, key_blocks, key_counts, *pieces, w_qkv, w_qkv, qt, top, total, acc]
+        at = 3 + len(pieces) + 3
+        aliases = {at: 0, at + 1: 1, at + 2: 2}
+    flops = count * (2 * rows * width * 2 * width + 4 * rows * queries * width * 4)
+    out = pl.pallas_call(
+        kernel,
+        grid=(groups,),
+        in_specs=in_specs,
+        out_specs=out_specs,
+        out_shape=out_shape,
+        scratch_shapes=[pltpu.SMEM((count * (rows // block) * CORES * (rows // block),), jnp.int32)],
+        input_output_aliases=aliases,
+        cost_estimate=pl.CostEstimate(
+            flops=flops, transcendentals=count * H * rows * queries, bytes_accessed=4 << 20
+        ),
+        name=name,
+    )(*args)
+    if first:
+        return tuple(out)
+    return (state[0], *out)
+
+
+def pick_row(tile, at):
+    rows = lax.broadcasted_iota(jnp.int32, tile.shape, 0)
+    return jnp.sum(jnp.where(rows == at, tile.astype(F32), 0.0), axis=0, keepdims=True)
+
+
+def add_pieces(info, base, pieces, spread, y_own, y_par, rows, slot, block, blocks_of):
+    numbers = lax.broadcasted_iota(jnp.int32, (rows, slot), 0).astype(F32)
+    for p, piece in enumerate(pieces):
+
+        @pl.when(info[base + len(pieces) + p] != 0)
+        def _(p=p, piece=piece):
+            lists = piece[rows:, 0:slot]
+            for dest, target in ((0, y_own), (1, y_par)):
+                row = pick_row(lists, info[6 + dest])
+                chosen = jnp.where(numbers == row, 1.0, 0.0).astype(BF)
+                mix = jnp.zeros((rows, rows), F32)
+                for j in range(slot // block):
+                    tile = spread(dest, p, j)
+                    mix = mix + mm(tile, chosen[:, j * block : (j + 1) * block], ((1,), (1,)))
+                target[...] += mm(mix.astype(BF), piece[0:rows, :], ((1,), (0,)))
+
+
+def gather_kernel(count, far_count, rows, slot, far_slot, block, *refs):
+    info, nb_own, nb_par, own, adj_own, adj_par, *refs = refs
+    pieces = refs[:count]
+    far = refs[count : count + far_count]
+    y_own, y_par, spread = refs[count + far_count :]
+    spread[...] = jnp.zeros(spread.shape, BF)
+    per_dev, tiles = adj_own.shape[0], adj_own.shape[1]
+    for dest, (adj, nb) in enumerate(((adj_own, nb_own), (adj_par, nb_par))):
+        for b in range(per_dev):
+            for s in range(tiles):
+                spread[dest, nb[b, s], b * block : (b + 1) * block, :] = adj[b, s]
+    total = jnp.zeros(y_own.shape, F32)
+    for j in range(rows // block):
+        total = total + mm(spread[0, j], own[j * block : (j + 1) * block, :], ((1,), (0,)))
+    first_far = rows // block + info[5] * (slot // block)
+    for f in range(far_count):
+        for j in range(far_slot // block):
+            source = info[10 + 2 * count + f]
+            tile = spread[0, first_far + source * (far_slot // block) + j]
+            total = total + mm(tile, far[f][j * block : (j + 1) * block, :], ((1,), (0,)))
+    y_own[...] = total
+    y_par[...] = jnp.zeros(y_par.shape, F32)
+
+    def tile_of(dest, p, j):
+        return spread[dest, rows // block + info[10 + p] * (slot // block) + j]
+
+    add_pieces(info, 10, pieces, tile_of, y_own, y_par, rows, slot, block, None)
+
+
+def gather_more_kernel(count, rows, slot, block, *refs):
+    info, *refs = refs
+    pieces = refs[:count]
+    tiles = refs[count : 2 * count]
+    own_in, par_in, y_own, y_par = refs[2 * count :]
+    y_own[...] = own_in[...]
+    y_par[...] = par_in[...]
+
+    def tile_of(dest, p, j):
+        return tiles[p][dest, j]
+
+    add_pieces(info, 10, pieces, tile_of, y_own, y_par, rows, slot, block, None)
+
+
+def local_kernel(x, y_own, y_got, w, out):
+    mixed = (y_own[...] + y_got[...]).astype(BF)
+    agg = mm(mixed, w[...], ((1,), (0,)))
+    out[...] = layer_norm(x[...].astype(F32) + agg)
+
+
+def tail_kernel(rows, x, local, top, total, acc, got, got_stats, w_out, w_up, w_down, out, wo, wu, wd, sems):
+    loads = [
+        pltpu.make_async_copy(src, dst, sems.at[i])
+        for i, (src, dst) in enumerate(((w_out, wo), (w_up, wu), (w_down, wd)))
+    ]
+    for load in loads:
+        load.start()
+    heads = top.shape[0]
+    width = acc.shape[0]
+    head = width // heads
+    top_a = top[:, 0:rows]
+    top_b = got_stats[0:heads, :]
+    peak = jnp.maximum(top_a, top_b)
+    fade_a = jnp.exp2(top_a - peak)
+    fade_b = jnp.exp2(top_b - peak)
+    whole = total[:, 0:rows] * fade_a + got_stats[heads : 2 * heads, :] * fade_b
+    fade_a = fade_a / whole
+    fade_b = fade_b / whole
+    pieces = []
+    for h in range(heads):
+        at = slice(h * head, (h + 1) * head)
+        pieces.append(
+            (
+                acc[at, 0:rows] * fade_a[h : h + 1, :]
+                + got[at, :].astype(F32) * fade_b[h : h + 1, :]
+            ).astype(BF)
+        )
+    attended = jnp.concatenate(pieces, axis=0)
+    loads[0].wait()
+    projected = mm(attended, wo[...], ((0,), (0,)))
+    summed = local[...] + layer_norm(x[...].astype(F32) + projected)
+    loads[1].wait()
+    activated = jax.nn.gelu(mm(summed.astype(BF), wu[...], ((1,), (0,)))).astype(BF)
+    loads[2].wait()
+    out[...] = layer_norm(summed + mm(activated, wd[...], ((1,), (0,)))).astype(BF)
+
+
+def line_plan(
+    node_feats,
+    w_gcn,
+    adj_tiles,
+    neighbor_blocks,
+    inner_rows,
+    outer_rows,
+    w_qkv,
+    key_blocks,
+    key_counts,
+    w_out,
+    w_up,
+    w_down,
+):
+    rows, width = node_feats.shape
+    block = adj_tiles.shape[-1]
+    per_dev = rows // block
+    peers = lax.axis_size("dev")
+    clusters = lax.axis_size("group")
+    chips = peers // CORES
+    slot = inner_rows.shape[-1]
+    far_slot = outer_rows.shape[-1]
+    me = lax.axis_index("dev")
+    cluster = lax.axis_index("group")
+    core = me % CORES
+    mate = me + 1 - 2 * core
+
+    swap = [(CORES * c + k, CORES * c + 1 - k) for c in range(chips) for k in range(CORES)]
+
+    def hop(value, step, far):
+        pairs = []
+        for c in range(chips):
+            to = c + step
+            if 0 <= to < chips and 0 <= to - step * far < chips:
+                pairs += [(CORES * c + k, CORES * to + k) for k in range(CORES)]
+        return lax.ppermute(value, "dev", pairs)
+
+    lists = jnp.pad(inner_rows[0].astype(BF), ((0, 0), (0, width - slot)))
+    piece = jnp.concatenate([node_feats, lists], axis=0)
+    left, right = hop(piece, 1, 1), hop(piece, -1, 1)
+    mate_piece = lax.ppermute(piece, "dev", swap)
+    mate_adj = lax.ppermute(adj_tiles, "dev", swap)
+    mate_nb = lax.ppermute(neighbor_blocks, "dev", swap)
+
+    numbers = jnp.arange(rows, dtype=jnp.int32)
+    chosen = (outer_rows[0].reshape(-1)[:, None] == numbers[None, :]).astype(BF)
+    picked = jnp.dot(chosen, node_feats, preferred_element_type=F32).astype(BF)
+    picked = picked.reshape(clusters, far_slot, width)
+    far = [lax.dynamic_index_in_dim(picked, cluster, 0, keepdims=False)]
+    far_from = [cluster]
+    for s in range(1, clusters):
+        if clusters & (clusters - 1) == 0:
+            pairs = [(c, c ^ s) for c in range(clusters)]
+            to, source = cluster ^ s, cluster ^ s
+        else:
+            pairs = [(c, (c + s) % clusters) for c in range(clusters)]
+            to, source = (cluster + s) % clusters, (cluster - s) % clusters
+        sent = lax.dynamic_index_in_dim(picked, to, 0, keepdims=False)
+        far.append(lax.ppermute(sent, "group", pairs))
+        far_from.append(source)
+
+    blocks_at = [me * per_dev + b for b in range(per_dev)] + [mate * per_dev + b for b in range(per_dev)]
+
+    def info_of(sources):
+        flags = [(s >= 0) & (s < peers) for s in sources]
+        clipped = [jnp.clip(s, 0, peers - 1) for s in sources]
+        return clipped, flags
+
+    def pack(entries):
+        return jnp.stack([jnp.asarray(e).astype(jnp.int32) for e in entries])
+
+    def attend_info(sources):
+        clipped, flags = info_of(sources)
+        entries = [me // CORES, *clipped, *flags]
+        entries += [0] * (8 - len(entries)) + blocks_at
+        return pack(entries)
+
+    def gather_info(sources):
+        clipped, flags = info_of(sources)
+        return pack([0, 0, 0, 0, 0, peers, me, mate, 0, 0, *clipped, *flags, *far_from])
+
+    state = attend_call(
+        True, [piece, mate_piece], None, attend_info([me]), key_blocks, key_counts, w_qkv, rows, block, "attend0"
+    )
+    arrived, origin = [piece], [me]
+    for step in range(1, chips):
+        pair, sources = [left, right], [me - CORES * step, me + CORES * step]
+        if step + 1 < chips:
+            left, right = hop(left, 1, step + 1), hop(right, -1, step + 1)
+        if step + 1 == chips:
+            sums = gather_call(
+                arrived, gather_info(origin), node_feats, adj_tiles, mate_adj, neighbor_blocks, mate_nb,
+                far, rows, slot, far_slot, block,
+            )
+            sums = gather_more_call(pair, gather_info(sources), sums, rows, slot, block)
+            y_got = lax.ppermute(sums[1], "dev", swap)
+        state = attend_call(
+            False, pair, state, attend_info(sources), key_blocks, key_counts, w_qkv, rows, block, f"attend{step}"
+        )
+        arrived += pair
+        origin += sources
+    _, top, total, acc = state
+    got = lax.ppermute(acc[:, rows:], "dev", swap)
+    stats = jnp.concatenate([top[:, rows:], total[:, rows:]], axis=0)
+    got_stats = lax.ppermute(stats, "dev", swap)
+    local = pl.pallas_call(
+        local_kernel,
+        in_specs=[VMEM] * 4,
+        out_specs=VMEM,
+        out_shape=jax.ShapeDtypeStruct((rows, width), F32),
+        cost_estimate=pl.CostEstimate(flops=2 * rows * width * width, transcendentals=0, bytes_accessed=4 << 20),
+        name="local",
+    )(node_feats, sums[0], y_got, w_gcn)
+    hbm = pl.BlockSpec(memory_space=pl.ANY)
+    return pl.pallas_call(
+        functools.partial(tail_kernel, rows),
+        in_specs=[VMEM] * 7 + [hbm] * 3,
+        out_specs=VMEM,
+        out_shape=jax.ShapeDtypeStruct((rows, width), BF),
+        scratch_shapes=[
+            pltpu.VMEM(w_out.shape, BF),
+            pltpu.VMEM(w_up.shape, BF),
+            pltpu.VMEM(w_down.shape, BF),
+            pltpu.SemaphoreType.DMA((3,)),
+        ],
+        cost_estimate=pl.CostEstimate(
+            flops=2 * rows * width * (width + 2 * w_up.shape[1]), transcendentals=0, bytes_accessed=12 << 20
+        ),
+        name="tail",
+    )(node_feats, local, top, total, acc, got, got_stats, w_out, w_up, w_down)
+
+
+def gather_call(
+    pieces, info, own, adj_own, adj_par, nb_own, nb_par, far, rows, slot, far_slot, block
+):
+    width = own.shape[1]
+    table_blocks = rows // block + (int(lax.axis_size("dev")) * slot + len(far) * far_slot) // block
+    y = jax.ShapeDtypeStruct((rows, width), F32)
+    spread = jax.ShapeDtypeStruct((CORES, table_blocks, rows, block), BF)
+    return pl.pallas_call(
+        functools.partial(gather_kernel, len(pieces), len(far), rows, slot, far_slot, block),
+        in_specs=[SMEM] * 3 + [VMEM] * (3 + len(pieces) + len(far)),
+        out_specs=[VMEM] * 3,
+        out_shape=[y, y, spread],
+        cost_estimate=pl.CostEstimate(
+            flops=2 * rows * rows * width * (2 * len(pieces)), transcendentals=0, bytes_accessed=8 << 20
+        ),
+        name="gather",
+    )(info, nb_own, nb_par, own, adj_own, adj_par, *pieces, *far)
+
+
+def gather_more_call(pieces, info, sums, rows, slot, block):
+    y_own, y_par, spread = sums
+    each = slot // block
+    count = len(pieces)
+    base = rows // block // each
+    tile = [
+        pl.BlockSpec(
+            (CORES, each, rows, block), lambda i, info, p=p: (0, base + info[10 + p], 0, 0)
+        )
+        for p in range(count)
+    ]
+    whole = lambda a: pl.BlockSpec(a.shape, lambda i, info: (0,) * a.ndim)
+    out = pl.pallas_call(
+        functools.partial(gather_more_kernel, count, rows, slot, block),
+        grid_spec=pltpu.PrefetchScalarGridSpec(
+            num_scalar_prefetch=1,
+            grid=(1,),
+            in_specs=[whole(p) for p in pieces] + tile + [whole(y_own), whole(y_par)],
+            out_specs=[whole(y_own), whole(y_par)],
+        ),
+        out_shape=[jax.ShapeDtypeStruct(y_own.shape, F32)] * 2,
+        input_output_aliases={1 + 2 * count: 0, 2 + 2 * count: 1},
+        cost_estimate=pl.CostEstimate(
+            flops=4 * rows * rows * y_own.shape[1] * count, transcendentals=0, bytes_accessed=4 << 20
+        ),
+        name="gather_more",
+    )(info, *pieces, *([spread] * count), y_own, y_par)
+    return out
+
+
+def per_device(*args):
+    inner, feats, tiles = args[4], args[0], args[2]
+    whole_slots = inner.shape[-1] == feats.shape[0] and feats.shape[0] <= 256
+    if whole_slots and lax.axis_size("dev") % CORES == 0 and inner.shape[-1] % tiles.shape[-1] == 0:
+        return line_plan(*args)
+    return gathered_plan(*args)
+
+
 def solution(mesh):
     placed = (
         P(("group", "dev"), None),

time: 269 us -> 133 us (0.49)
  the two profiles are of different devices: /device:TPU:0 before, /device:TPU:17 now
where the time goes in v1:
time: 133 us
  Pallas kernels  97.9 us (74%)
  starting transfers between devices  20.3 us (15%)
  local copies, waits for them, and re-layouts  10.5 us (8%)
  other arithmetic  1.78 us (1%)
  matrix products  1.54 us (1%)
    pallas_call x4, Pallas kernels, attend_call(): pl.pallas_call(kernel, grid=(groups,), in_specs=in_specs, out_specs=out_s...  69.8 us
    ppermute x6, starting transfers between devices, hop(): return lax.ppermute(value, 'dev', pairs)  13.4 us
    pallas_call x1, Pallas kernels, gather_call(): pl.pallas_call(functools.partial(gather_kernel, len(pieces), len(far), ro...  10.1 us
    pallas_call x1, Pallas kernels, line_plan(): pl.pallas_call(functools.partial(tail_kernel, rows), in_specs=[VMEM] * 7...  9.25 us
    unnamed x26, local copies, waits for them, and re-layouts  4.7 us
    pallas_call x1, Pallas kernels, gather_more_call(): pl.pallas_call(functools.partial(gather_more_kernel, count, rows, slot, b...  4.42 us
    pallas_call x1, Pallas kernels, line_plan(): pl.pallas_call(local_kernel, in_specs=[VMEM] * 4, out_specs=VMEM, out_sha...  4.38 us
    another operation x6, local copies, waits for them, and re-layouts, pack(): return jnp.stack([jnp.asarray(e).astype(jnp.int32) for e in entries])  3.6 us
  transfers between devices with their start and end apart: 15, of which 0 were waited for; matrix products, arithmetic and copies ran while one was open for 6% of the time, Pallas kernels for 64%

profile of v1, /device:TPU:17, one launch (start us, length us, event | category | flops | bytes accessed | tf_op | source)
XLA Modules:
  0.0 132.6 jit_solution(16038985384098718604)
XLA Ops:
  0.0 0.7 convert_bitcast_fusion
  0.7 1.1 fusion.1.refs_6_.refs_3_
  1.8 0.0 copy-start
  1.8 0.7 collective-permute-start.12
  2.5 3.2 %collective-permute-start = (bf16[264,1024]{1,0:T(8,128)(2,1)S(1)}, bf16[264,1024]{1,0:T(8,128)(2,1)}, u32[]{:S(2)}, u32[]{:S(2)}) collective-permute-start(bf16[264,1024]{1,0:T(8,128)(2,1)S(1)} %fusion.1.refs_6_.refs_3_), channel_id=1, source_target_pairs={{0,2},{1,3},{2,4},{3,5},{4,6},{5,7},{8,10},{9,11},{10,12},{11,13},... | collective-permute-start | bytes 1622024 | tf_op jit(solution)/shard_map/ppermute | solution.py:451
  5.7 2.1 %collective-permute-start.3 = (bf16[264,1024]{1,0:T(8,128)(2,1)S(1)}, bf16[264,1024]{1,0:T(8,128)(2,1)}, u32[]{:S(2)}, u32[]{:S(2)}) collective-permute-start(bf16[264,1024]{1,0:T(8,128)(2,1)S(1)} %fusion.1.refs_6_.refs_3_), channel_id=1, source_target_pairs={{2,0},{3,1},{4,2},{5,3},{6,4},{7,5},{10,8},{11,9},{12,10},{13,11},... | collective-permute-start | bytes 1622024 | tf_op jit(solution)/shard_map/ppermute | solution.py:451
  7.8 0.7 collective-permute-start.6
  8.5 0.1 collective-permute-start.7
  8.6 1.5 %convolution_convert_fusion = bf16[512,1024]{1,0:T(8,128)(2,1)S(1)} fusion(bf16[256,1024]{1,0:T(8,128)(2,1)} %x.5, s32[512]{0:T(512)} %bitcast.39), kind=kOutput, calls=%fused_computation | convolution fusion | flops 269090816 | bytes 1574912 | tf_op jit(solution)/shard_map/dot_general | solution.py:462
  10.2 0.6 stack.184.refs_0_
  10.8 0.6 stack.183.refs_0_
  11.4 0.6 stack.185.refs_0_
  12.0 0.6 stack.161.refs_0_
  12.6 0.6 stack.177.refs_0_
  13.2 0.6 stack.186.refs_0_
  13.8 0.9 dynamic-slice_bitcast_fusion
  14.7 0.0 collective-permute-done.12.refs_4_
  14.7 1.2 collective-permute-start.8
  15.9 0.0 copy-done
  15.9 0.0 copy-done.4
  15.9 18.1 %attend0.1 = (bf16[1024,512]{1,0:T(8,128)(2,1)}, f32[32,512]{1,0:T(8,128)}, f32[32,512]{1,0:T(8,128)}, f32[1024,512]{1,0:T(8,128)}) custom-call(s32[12]{0:T(128)} %stack.184.refs_0_, s32[16,16]{1,0:T(8,128)} %refs_1_.9, s32[16]{0:T(128)} %refs_2_.7, bf16[264,1024]{1,0:T(8,128)(2,1)} %copy-done, bf16[264,1024]{1,0:T(8,128)(2,1)} %copy-done.4, ...), custom_call_target="tpu_custom_call" | custom-call | flops 3221225472 | bytes 4194304 | tf_op jit(solution)/shard_map/attend0/pallas_call | solution.py:290
  34.0 0.0 collective-permute-done.6.refs_2_
  34.0 0.0 copy-start.12
  34.0 1.3 collective-permute-start.9
  35.3 0.0 collective-permute-done.8.refs_12_
  35.3 0.7 collective-permute-start.10
  36.0 0.0 collective-permute-done.refs_7_.refs_3_
  36.0 3.9 %collective-permute-start.1 = (bf16[264,1024]{1,0:T(8,128)(2,1)}, bf16[264,1024]{1,0:T(8,128)(2,1)S(1)}, u32[]{:S(2)}, u32[]{:S(2)}) collective-permute-start(bf16[264,1024]{1,0:T(8,128)(2,1)} %collective-permute-done.refs_7_.refs_3_), channel_id=1, source_target_pairs={{2,4},{3,5},{4,6},{5,7},{10,12},{11,13},{12,14},{13,15},{18,20},{1... | collective-permute-start | bytes 1622024 | tf_op jit(solution)/shard_map/ppermute | solution.py:451
  39.9 0.0 collective-permute-done.3.refs_8_.refs_4_
  39.9 2.2 %collective-permute-start.4 = (bf16[264,1024]{1,0:T(8,128)(2,1)}, bf16[264,1024]{1,0:T(8,128)(2,1)}, u32[]{:S(2)}, u32[]{:S(2)}) collective-permute-start(bf16[264,1024]{1,0:T(8,128)(2,1)} %collective-permute-done.3.refs_8_.refs_4_), channel_id=1, source_target_pairs={{2,0},{3,1},{4,2},{5,3},{10,8},{11,9},{12,10},{13,11},{18,16},{19,... | collective-permute-start | bytes 1622024 | tf_op jit(solution)/shard_map/ppermute | solution.py:451
  42.2 29.2 %attend1.1 = (f32[32,512]{1,0:T(8,128)}, f32[32,512]{1,0:T(8,128)}, f32[1024,512]{1,0:T(8,128)}) custom-call(s32[12]{0:T(128)} %stack.186.refs_0_, s32[16,16]{1,0:T(8,128)} %refs_1_.9, s32[16]{0:T(128)} %refs_2_.7, bf16[264,1024]{1,0:T(8,128)(2,1)} %collective-permute-done.refs_7_.refs_3_, ...), custom_call_target="tpu_custom_call", output_to_operand_aliasing={{0}: (8, {}), {1}: (9, {}), {2}: (10, {})} | custom-call | flops 6442450944 | bytes 4194304 | tf_op jit(solution)/shard_map/attend1/pallas_call | solution.py:290
  71.4 0.0 copy-done.12
  71.4 0.0 collective-permute-done.1.refs_9_.refs_3_
  71.4 1.3 collective-permute-start.2
  72.7 0.0 collective-permute-done.4.refs_10_.refs_4_
  72.7 0.7 collective-permute-start.5
  73.4 0.0 collective-permute-done.9.refs_13_
  73.5 0.0 collective-permute-done.10.refs_14_
  73.5 0.0 collective-permute-done.7.refs_5_
  73.5 0.0 copy-start.1
  73.5 0.0 copy-done.6
  73.5 1.0 copy-done.1
  74.5 10.1 %gather.1 = (f32[256,1024]{1,0:T(8,128)}, f32[256,1024]{1,0:T(8,128)}, bf16[2,22,256,128]{3,2,1,0:T(8,128)(2,1)}) custom-call(s32[24]{0:T(128)} %stack.177.refs_0_, s32[2,16]{1,0:T(2,128)} %refs_1_.5, s32[2,16]{1,0:T(2,128)} %copy-done.12, bf16[256,1024]{1,0:T(8,128)(2,1)} %x.5, bf16[2,16,128,128]{3,2,1,0:T(8,128)(2,1)} %refs_4_.1, ...), custom_call_target="tpu_custom_call" | custom-call | flops 1342177280 | bytes 8388608 | tf_op jit(solution)/shard_map/gather/pallas_call | solution.py:555
  84.6 16.5 %attend2.1 = (f32[32,512]{1,0:T(8,128)}, f32[32,512]{1,0:T(8,128)}, f32[1024,512]{1,0:T(8,128)}) custom-call(s32[12]{0:T(128)} %stack.185.refs_0_, s32[16,16]{1,0:T(8,128)} %refs_1_.9, s32[16]{0:T(128)} %refs_2_.7, bf16[264,1024]{1,0:T(8,128)(2,1)} %copy-done.6, ...), custom_call_target="tpu_custom_call", output_to_operand_aliasing={{0}: (8, {}), {1}: (9, {}), {2}: (10, {})} | custom-call | flops 6442450944 | bytes 4194304 | tf_op jit(solution)/shard_map/attend2/pallas_call | solution.py:290
  101.1 0.0 collective-permute-done.2.refs_1_.refs_3_
  101.1 0.0 collective-permute-done.5.refs_2_.refs_4_
  101.1 0.0 copy-start.7
  101.1 0.8 copy-done.5
  102.0 0.2 copy-done.7
  102.2 4.4 %gather_more.1 = (f32[256,1024]{1,0:T(8,128)}, f32[256,1024]{1,0:T(8,128)}) custom-call(s32[18]{0:T(128)} %stack.161.refs_0_, bf16[264,1024]{1,0:T(8,128)(2,1)} %copy-done.5, bf16[264,1024]{1,0:T(8,128)(2,1)} %copy-done.7, bf16[2,22,256,128]{3,2,1,0:T(8,128)(2,1)} %get-tuple-element.23.refs_3_.refs_4_, ...), custom_call_target="tpu_custom_call", output_to_operand_aliasing={{0}: (5, {}), {1}: (6, {})} | custom-call | flops 536870912 | bytes 4194304 | tf_op jit(solution)/shard_map/gather_more/pallas_call | solution.py:579
  106.6 1.5 %collective-permute-start.11 = (f32[256,1024]{1,0:T(8,128)}, f32[256,1024]{1,0:T(8,128)S(1)}, u32[]{:S(2)}, u32[]{:S(2)}) collective-permute-start(f32[256,1024]{1,0:T(8,128)} %get-tuple-element.27), channel_id=1, source_target_pairs={{0,1},{1,0},{2,3},{3,2},{4,5},{5,4},{6,7},{7,6},{8,9},{9,8},{10,11... | collective-permute-start | bytes 3145736 | tf_op jit(solution)/shard_map/ppermute | solution.py:511
  108.2 6.0 %attend3.1 = (f32[32,512]{1,0:T(8,128)}, f32[32,512]{1,0:T(8,128)}, f32[1024,512]{1,0:T(8,128)}) custom-call(s32[12]{0:T(128)} %stack.183.refs_0_, s32[16,16]{1,0:T(8,128)} %refs_1_.9, s32[16]{0:T(128)} %refs_2_.7, bf16[264,1024]{1,0:T(8,128)(2,1)} %copy-done.5, ...), custom_call_target="tpu_custom_call", output_to_operand_aliasing={{0}: (8, {}), {1}: (9, {}), {2}: (10, {})} | custom-call | flops 6442450944 | bytes 4194304 | tf_op jit(solution)/shard_map/attend3/pallas_call | solution.py:290
  114.2 1.3 %slice.9 = f32[1024,256]{1,0:T(8,128)S(1)} slice(f32[1024,512]{1,0:T(8,128)} %get-tuple-element.40.acc), slice={[0:1024], [256:512]} | slice | bytes 2097152 | tf_op jit(solution)/shard_map/slice | solution.py:518
  115.5 0.1 collective-permute-start.13
  115.6 0.0 copy-done.9
  115.6 0.5 collective-permute-start.14
  116.2 0.0 collective-permute-done.11.y_got
  116.2 1.0 copy-done.2
  117.2 4.4 %local.1 = f32[256,1024]{1,0:T(8,128)} custom-call(bf16[256,1024]{1,0:T(8,128)(2,1)} %x.5, f32[256,1024]{1,0:T(8,128)} %get-tuple-element.26.y_own, f32[256,1024]{1,0:T(8,128)} %copy-done.2, bf16[1024,1024]{1,0:T(8,128)(2,1)} %w.1), custom_call_target="tpu_custom_call" | custom-call | flops 536870912 | bytes 4194304 | tf_op jit(solution)/shard_map/local/pallas_call | solution.py:521
  121.6 0.0 collective-permute-done.14.got_stats
  121.6 0.0 collective-permute-done.13.got
  121.6 0.6 copy-done.11
  122.2 1.0 copy-done.3
  123.2 9.2 %tail.1 = bf16[256,1024]{1,0:T(8,128)(2,1)} custom-call(bf16[256,1024]{1,0:T(8,128)(2,1)} %x.5, f32[256,1024]{1,0:T(8,128)} %local.1, f32[32,512]{1,0:T(8,128)} %get-tuple-element.38.top, f32[32,512]{1,0:T(8,128)} %get-tuple-element.39.total, f32[1024,512]{1,0:T(8,128)} %get-tuple-element.40.acc, f32[1024,256]{1,0:T(8,128)} %copy-done.3, ...), custom_call_target="tpu_custom_call" | custom-call | flops 2684354560 | bytes 12582912 | tf_op jit(solution)/shard_map/tail/pallas_call | solution.py:530
  (16 shorter events, 0.0 us)
Async XLA Ops:
  1.8 14.1 %copy-start = (bf16[264,1024]{1,0:T(8,128)(2,1)}, bf16[264,1024]{1,0:T(8,128)(2,1)S(1)}, u32[]{:S(2)}) copy-start(bf16[264,1024]{1,0:T(8,128)(2,1)S(1)} %fusion.1.refs_6_.refs_3_) | copy-start | bytes 1622020
  1.8 12.9 %collective-permute-start.12 = (bf16[264,1024]{1,0:T(8,128)(2,1)S(1)}, bf16[264,1024]{1,0:T(8,128)(2,1)S(1)}, u32[]{:S(2)}, u32[]{:S(2)}) collective-permute-start(bf16[264,1024]{1,0:T(8,128)(2,1)S(1)} %fusion.1.refs_6_.refs_3_), channel_id=1, source_target_pairs={{0,1},{1,0},{2,3},{3,2},{4,5},{5,4},{6,7},{7,6},{8,9},{9,8},{10,11... | collective-permute-start | bytes 1622024 | tf_op jit(solution)/shard_map/ppermute | solution.py:456
  2.5 33.5 %collective-permute-start = (bf16[264,1024]{1,0:T(8,128)(2,1)S(1)}, bf16[264,1024]{1,0:T(8,128)(2,1)}, u32[]{:S(2)}, u32[]{:S(2)}) collective-permute-start(bf16[264,1024]{1,0:T(8,128)(2,1)S(1)} %fusion.1.refs_6_.refs_3_), channel_id=1, source_target_pairs={{0,2},{1,3},{2,4},{3,5},{4,6},{5,7},{8,10},{9,11},{10,12},{11,13},... | collective-permute-start | bytes 1622024 | tf_op jit(solution)/shard_map/ppermute | solution.py:451
  5.7 34.2 %collective-permute-start.3 = (bf16[264,1024]{1,0:T(8,128)(2,1)S(1)}, bf16[264,1024]{1,0:T(8,128)(2,1)}, u32[]{:S(2)}, u32[]{:S(2)}) collective-permute-start(bf16[264,1024]{1,0:T(8,128)(2,1)S(1)} %fusion.1.refs_6_.refs_3_), channel_id=1, source_target_pairs={{2,0},{3,1},{4,2},{5,3},{6,4},{7,5},{10,8},{11,9},{12,10},{13,11},... | collective-permute-start | bytes 1622024 | tf_op jit(solution)/shard_map/ppermute | solution.py:451
  7.8 26.2 %collective-permute-start.6 = (s32[2,16]{1,0:T(2,128)}, s32[2,16]{1,0:T(2,128)S(1)}, u32[]{:S(2)}, u32[]{:S(2)}) collective-permute-start(s32[2,16]{1,0:T(2,128)} %refs_1_.5), channel_id=1, source_target_pairs={{0,1},{1,0},{2,3},{3,2},{4,5},{5,4},{6,7},{7,6},{8,9},{9,8},{10,11... | collective-permute-start | bytes 392 | tf_op jit(solution)/shard_map/ppermute | solution.py:458
  8.5 65.0 %collective-permute-start.7 = (bf16[2,16,128,128]{3,2,1,0:T(8,128)(2,1)}, bf16[2,16,128,128]{3,2,1,0:T(8,128)(2,1)S(1)}, u32[]{:S(2)}, u32[]{:S(2)}) collective-permute-start(bf16[2,16,128,128]{3,2,1,0:T(8,128)(2,1)} %refs_4_.1), channel_id=1, source_target_pairs={{0,1},{1,0},{2,3},{3,2},{4,5},{5,4},{6,7},{7,6},{8,9},{9,8},{10,11... | collective-permute-start | bytes 3145736 | tf_op jit(solution)/shard_map/ppermute | solution.py:457
  14.7 1.2 copy-start.4
  14.7 20.6 %collective-permute-start.8 = (bf16[128,1024]{1,0:T(8,128)(2,1)}, bf16[128,1024]{1,0:T(8,128)(2,1)S(1)}, u32[]{:S(2)}, u32[]{:S(2)}) collective-permute-start(bf16[128,1024]{1,0:T(8,128)(2,1)} %get-tuple-element.43), channel_id=1, source_target_pairs={{0,8},{8,0},{16,24},{24,16},{1,9},{9,1},{17,25},{25,17},{2,10},{10... | collective-permute-start | bytes 786440 | tf_op jit(solution)/shard_map/ppermute | solution.py:474
  34.0 37.4 %copy-start.12 = (s32[2,16]{1,0:T(2,128)}, s32[2,16]{1,0:T(2,128)S(1)}, u32[]{:S(2)}) copy-start(s32[2,16]{1,0:T(2,128)S(1)} %collective-permute-done.6.refs_2_) | copy-start | bytes 388
  34.0 39.4 %collective-permute-start.9 = (bf16[128,1024]{1,0:T(8,128)(2,1)}, bf16[128,1024]{1,0:T(8,128)(2,1)}, u32[]{:S(2)}, u32[]{:S(2)}) collective-permute-start(bf16[128,1024]{1,0:T(8,128)(2,1)} %get-tuple-element.42), channel_id=1, source_target_pairs={{0,16},{8,24},{16,0},{24,8},{1,17},{9,25},{17,1},{25,9},{2,18},{10... | collective-permute-start | bytes 786440 | tf_op jit(solution)/shard_map/ppermute | solution.py:474
  35.3 36.1 %copy-start.8 = (bf16[128,1024]{1,0:T(8,128)(2,1)}, bf16[128,1024]{1,0:T(8,128)(2,1)S(1)}, u32[]{:S(2)}) copy-start(bf16[128,1024]{1,0:T(8,128)(2,1)S(1)} %collective-permute-done.8.refs_12_) | copy-start | bytes 786436
  35.3 38.1 %collective-permute-start.10 = (bf16[128,1024]{1,0:T(8,128)(2,1)S(1)}, bf16[128,1024]{1,0:T(8,128)(2,1)}, u32[]{:S(2)}, u32[]{:S(2)}) collective-permute-start(bf16[128,1024]{1,0:T(8,128)(2,1)S(1)} %get-tuple-element.41), channel_id=1, source_target_pairs={{0,24},{8,16},{16,8},{24,0},{1,25},{9,17},{17,9},{25,1},{2,26},{10... | collective-permute-start | bytes 786440 | tf_op jit(solution)/shard_map/ppermute | solution.py:474
  36.0 35.3 %collective-permute-start.1 = (bf16[264,1024]{1,0:T(8,128)(2,1)}, bf16[264,1024]{1,0:T(8,128)(2,1)S(1)}, u32[]{:S(2)}, u32[]{:S(2)}) collective-permute-start(bf16[264,1024]{1,0:T(8,128)(2,1)} %collective-permute-done.refs_7_.refs_3_), channel_id=1, source_target_pairs={{2,4},{3,5},{4,6},{5,7},{10,12},{11,13},{12,14},{13,15},{18,20},{1... | collective-permute-start | bytes 1622024 | tf_op jit(solution)/shard_map/ppermute | solution.py:451
  39.9 32.8 %collective-permute-start.4 = (bf16[264,1024]{1,0:T(8,128)(2,1)}, bf16[264,1024]{1,0:T(8,128)(2,1)}, u32[]{:S(2)}, u32[]{:S(2)}) collective-permute-start(bf16[264,1024]{1,0:T(8,128)(2,1)} %collective-permute-done.3.refs_8_.refs_4_), channel_id=1, source_target_pairs={{2,0},{3,1},{4,2},{5,3},{10,8},{11,9},{12,10},{13,11},{18,16},{19,... | collective-permute-start | bytes 1622024 | tf_op jit(solution)/shard_map/ppermute | solution.py:451
  71.4 2.1 %copy-start.6 = (bf16[264,1024]{1,0:T(8,128)(2,1)}, bf16[264,1024]{1,0:T(8,128)(2,1)S(1)}, u32[]{:S(2)}) copy-start(bf16[264,1024]{1,0:T(8,128)(2,1)S(1)} %collective-permute-done.1.refs_9_.refs_3_) | copy-start | bytes 1622020
  71.4 29.7 %collective-permute-start.2 = (bf16[264,1024]{1,0:T(8,128)(2,1)S(1)}, bf16[264,1024]{1,0:T(8,128)(2,1)S(1)}, u32[]{:S(2)}, u32[]{:S(2)}) collective-permute-start(bf16[264,1024]{1,0:T(8,128)(2,1)S(1)} %collective-permute-done.1.refs_9_.refs_3_), channel_id=1, source_target_pairs={{4,6},{5,7},{12,14},{13,15},{20,22},{21,23},{28,30},{29,31}} | collective-permute-start | bytes 1622024 | tf_op jit(solution)/shard_map/ppermute | solution.py:451
  72.7 28.4 %collective-permute-start.5 = (bf16[264,1024]{1,0:T(8,128)(2,1)}, bf16[264,1024]{1,0:T(8,128)(2,1)S(1)}, u32[]{:S(2)}, u32[]{:S(2)}) collective-permute-start(bf16[264,1024]{1,0:T(8,128)(2,1)} %collective-permute-done.4.refs_10_.refs_4_), channel_id=1, source_target_pairs={{2,0},{3,1},{10,8},{11,9},{18,16},{19,17},{26,24},{27,25}} | collective-permute-start | bytes 1622024 | tf_op jit(solution)/shard_map/ppermute | solution.py:451
  73.5 1.0 copy-start.1
  101.1 0.8 copy-start.5
  101.1 1.1 copy-start.7
  106.6 9.6 %collective-permute-start.11 = (f32[256,1024]{1,0:T(8,128)}, f32[256,1024]{1,0:T(8,128)S(1)}, u32[]{:S(2)}, u32[]{:S(2)}) collective-permute-start(f32[256,1024]{1,0:T(8,128)} %get-tuple-element.27), channel_id=1, source_target_pairs={{0,1},{1,0},{2,3},{3,2},{4,5},{5,4},{6,7},{7,6},{8,9},{9,8},{10,11... | collective-permute-start | bytes 3145736 | tf_op jit(solution)/shard_map/ppermute | solution.py:511
  114.2 1.4 %copy-start.10 = (f32[32,512]{1,0:T(8,128)S(1)}, f32[32,512]{1,0:T(8,128)}, u32[]{:S(2)}) copy-start(f32[32,512]{1,0:T(8,128)} %get-tuple-element.39.total) | copy-start | bytes 196612
  114.2 1.4 %copy-start.9 = (f32[32,512]{1,0:T(8,128)S(1)}, f32[32,512]{1,0:T(8,128)}, u32[]{:S(2)}) copy-start(f32[32,512]{1,0:T(8,128)} %get-tuple-element.38.top) | copy-start | bytes 196612
  115.5 6.1 %collective-permute-start.13 = (f32[1024,256]{1,0:T(8,128)S(1)}, f32[1024,256]{1,0:T(8,128)S(1)}, u32[]{:S(2)}, u32[]{:S(2)}) collective-permute-start(f32[1024,256]{1,0:T(8,128)S(1)} %slice.9), channel_id=1, source_target_pairs={{0,1},{1,0},{2,3},{3,2},{4,5},{5,4},{6,7},{7,6},{8,9},{9,8},{10,11... | collective-permute-start | bytes 3145736 | tf_op jit(solution)/shard_map/ppermute | solution.py:518
  115.6 5.9 %collective-permute-start.14 = (f32[64,256]{1,0:T(8,128)S(1)}, f32[64,256]{1,0:T(8,128)S(1)}, u32[]{:S(2)}, u32[]{:S(2)}) collective-permute-start(f32[64,256]{1,0:T(8,128)S(1)} %pad_maximum_fusion), channel_id=1, source_target_pairs={{0,1},{1,0},{2,3},{3,2},{4,5},{5,4},{6,7},{7,6},{8,9},{9,8},{10,11... | collective-permute-start | bytes 196616 | tf_op jit(solution)/shard_map/ppermute | solution.py:520
  116.2 1.0 copy-start.2
  121.6 0.6 copy-start.11
  122.2 1.0 copy-start.3

commit v2 on v0

--- a/solution.py
+++ b/solution.py
@@ -1,9 +1,16 @@
+import functools
+import math
+
 import jax
 import jax.numpy as jnp
 from jax import lax
+from jax.experimental import pallas as pl
+from jax.experimental.pallas import tpu as pltpu
 from jax.sharding import PartitionSpec as P
 
 H = 32
+LOW = -1e30
+CORES = 2
 
 
 def layer_norm(values):
@@ -13,7 +20,7 @@
     return centered / jnp.sqrt(variance + 1e-05)
 
 
-def per_device(
+def gathered_plan(
     node_feats,
     w_gcn,
     adj_tiles,
@@ -142,6 +149,461 @@
     return layer_out.astype(jnp.bfloat16)
 
 
+BF = jnp.bfloat16
+F32 = jnp.float32
+SMEM = pl.BlockSpec(memory_space=pltpu.SMEM)
+VMEM = pl.BlockSpec(memory_space=pltpu.VMEM)
+GROUP_COLS = 256
+DEPTH = 3
+
+
+def mm(a, b, dims=((1,), (0,))):
+    return lax.dot_general(a, b, (dims, ((), ())), preferred_element_type=F32)
+
+
+def grant(mib):
+    return pltpu.CompilerParams(vmem_limit_bytes=mib << 20)
+
+
+def sources_of(step, me, peers):
+    left, right = me - CORES * step, me + CORES * step
+    return left, right, left >= 0, right < peers
+
+
+def attend_kernel(mode, step, rows, block, peers, where, live, *refs):
+    first, last, both = mode
+    if first:
+        own, mate_piece, w, qt_ref, max_ref, sum_ref, acc_ref, score_ref, prob_ref = refs
+    else:
+        left_piece, right_piece, w, qt_ref, max_in, sum_in, acc_in, *refs = refs
+        if last:
+            send_ref, *refs = refs
+        max_ref, sum_ref, acc_ref, score_ref, prob_ref = refs
+    width = w.shape[0]
+    head = width // H
+    heads_step = GROUP_COLS // head
+    per_dev = rows // block
+    queries = CORES * rows
+    scale = math.log2(math.e) / math.sqrt(head)
+    me = where[0]
+    mate = me + 1 - 2 * (me % CORES)
+    if first:
+        source, needed = me, None
+    else:
+        left, right, has_left, has_right = sources_of(step, me, peers)
+        if both:
+            source, needed = right, has_left & has_right
+        else:
+            source, needed = jnp.where(has_left, left, right), has_left | has_right
+
+    def run():
+        if first:
+            x = own[0:rows, :]
+        elif both:
+            x = right_piece[0:rows, :]
+        else:
+            x = jnp.where(has_left, left_piece[0:rows, :], right_piece[0:rows, :])
+        query_blocks = [dev * per_dev + b for dev in (me, mate) for b in range(per_dev)]
+        alive = []
+        for j in range(per_dev):
+            bit = source * per_dev + j
+            flags = [jnp.full((1, block), (live[q] >> bit) & 1, jnp.int32) for q in query_blocks]
+            alive.append(jnp.concatenate(flags, axis=1) != 0)
+        ones = jnp.ones((16, rows), BF)
+
+        def group(g, carry):
+            cols = pl.multiple_of(g * GROUP_COLS, GROUP_COLS)
+            heads_at = pl.multiple_of(g * heads_step, heads_step)
+
+            def weight(part):
+                return w[:, pl.ds(pl.multiple_of(part * width + cols, GROUP_COLS), GROUP_COLS)]
+
+            if first:
+                wq = weight(0)
+                qt_ref[pl.ds(cols, GROUP_COLS), 0:rows] = mm(x, wq).astype(BF).T
+                mate_q = mm(mate_piece[0:rows, :], wq).astype(BF)
+                qt_ref[pl.ds(cols, GROUP_COLS), rows:queries] = mate_q.T
+                tops = jnp.full((heads_step, queries), LOW, F32)
+                sums = jnp.zeros((heads_step, queries), F32)
+            else:
+                tops = max_in[pl.ds(heads_at, heads_step), :]
+                sums = sum_in[pl.ds(heads_at, heads_step), :]
+            keys = mm(x, weight(1)).astype(BF)
+            values = mm(x, weight(2)).astype(BF).T
+            new_tops, new_sums = [], []
+
+            def score(h):
+                q = qt_ref[pl.ds(cols + h * head, head), :]
+                score_ref[h % DEPTH] = mm(keys[:, h * head : (h + 1) * head], q)
+
+            def soften(h):
+                parts = [score_ref[h % DEPTH, j * block : (j + 1) * block, :] for j in range(per_dev)]
+                top = tops[h : h + 1, :]
+                for j in range(per_dev):
+                    peak = jnp.max(parts[j], axis=0, keepdims=True) * scale
+                    top = jnp.maximum(top, jnp.where(alive[j], peak, LOW))
+                for j in range(per_dev):
+                    shift = jnp.where(alive[j], top, -LOW)
+                    prob_ref[h % 2, j * block : (j + 1) * block, :] = jnp.exp2(parts[j] * scale - shift).astype(BF)
+                new_tops.append(top)
+
+            def mix(h):
+                stacked = jnp.concatenate([values[h * head : (h + 1) * head, :], ones], axis=0)
+                mixed = mm(stacked, prob_ref[h % 2])
+                at = pl.ds(cols + h * head, head)
+                if first:
+                    new_sums.append(mixed[head : head + 1, :])
+                    acc_ref[at, :] = mixed[0:head, :]
+                else:
+                    fade = jnp.exp2(tops[h : h + 1, :] - new_tops[h])
+                    new_sums.append(sums[h : h + 1, :] * fade + mixed[head : head + 1, :])
+                    acc_ref[at, :] = acc_in[at, :] * fade + mixed[0:head, :]
+
+            for h in range(DEPTH - 1):
+                score(h)
+            for h in range(heads_step):
+                if h + DEPTH - 1 < heads_step:
+                    score(h + DEPTH - 1)
+                soften(h)
+                if h > 0:
+                    mix(h - 1)
+            mix(heads_step - 1)
+            max_ref[pl.ds(heads_at, heads_step), :] = jnp.concatenate(new_tops, axis=0)
+            sum_ref[pl.ds(heads_at, heads_step), :] = jnp.concatenate(new_sums, axis=0)
+            return carry
+
+        lax.fori_loop(0, width // GROUP_COLS, group, 0)
+
+    if needed is None:
+        run()
+    else:
+        pl.when(needed)(run)
+
+        @pl.when(jnp.logical_not(needed))
+        def _():
+            max_ref[...] = max_in[...]
+            sum_ref[...] = sum_in[...]
+            acc_ref[...] = acc_in[...]
+
+    if last:
+        send_ref[0:width, :] = acc_ref[:, rows:queries]
+        send_ref[width : width + H, :] = max_ref[:, rows:queries]
+        send_ref[width + H : width + 2 * H, :] = sum_ref[:, rows:queries]
+
+
+def attend_call(mode, step, pieces, state, where, live, w_qkv, rows, block, peers):
+    first, last, both = mode
+    width = w_qkv.shape[0]
+    queries = CORES * rows
+    stats = jax.ShapeDtypeStruct((H, queries), F32)
+    out_shape = [stats, stats, jax.ShapeDtypeStruct((width, queries), F32)]
+    args = [where, live, *pieces, w_qkv]
+    aliases = {}
+    if first:
+        out_shape = [jax.ShapeDtypeStruct((width, queries), BF), *out_shape]
+    else:
+        args += state
+        extra = 1 if last else 0
+        aliases = {6: extra, 7: extra + 1, 8: extra + 2}
+    if last:
+        out_shape = [jax.ShapeDtypeStruct((width + 2 * H, rows), F32), *out_shape]
+    out = pl.pallas_call(
+        functools.partial(attend_kernel, mode, step, rows, block, peers),
+        in_specs=[SMEM, SMEM] + [VMEM] * (len(args) - 2),
+        out_specs=[VMEM] * len(out_shape),
+        out_shape=out_shape,
+        scratch_shapes=[pltpu.VMEM((DEPTH, rows, queries), F32), pltpu.VMEM((2, rows, queries), BF)],
+        input_output_aliases=aliases,
+        compiler_params=grant(24),
+        cost_estimate=pl.CostEstimate(
+            flops=4 * rows * width * width + 16 * rows * queries * width,
+            transcendentals=H * rows * queries,
+            bytes_accessed=4 << 20,
+        ),
+        name=f"attend{step}{'b' if both else ''}",
+    )(*args)
+    if first:
+        return list(out)
+    if last:
+        return out
+    return [state[0], *out]
+
+
+def pick_row(tile, at):
+    rows = lax.broadcasted_iota(jnp.int32, tile.shape, 0)
+    return jnp.sum(jnp.where(rows == at, tile.astype(F32), 0.0), axis=0, keepdims=True)
+
+
+def add_piece(piece_lists, piece_rows, dests, tile, y_own, y_mate, rows, slot, block):
+    numbers = lax.broadcasted_iota(jnp.int32, (rows, slot), 0).astype(F32)
+    mixes = []
+    for dest in range(CORES):
+        chosen = jnp.where(numbers == pick_row(piece_lists, dests[dest]), 1.0, 0.0).astype(BF)
+        left = jnp.concatenate([tile(dest, j) for j in range(slot // block)], axis=1)
+        mixes.append(mm(left, chosen, ((1,), (1,))).astype(BF))
+    both = mm(jnp.concatenate(mixes, axis=0), piece_rows)
+    y_own[...] += both[0:rows, :]
+    y_mate[...] += both[rows:, :]
+
+
+def add_arrived(step, where, left_piece, right_piece, spread, y_own, y_mate, rows, slot, block, peers):
+    me = where[0]
+    mate = me + 1 - 2 * (me % CORES)
+    left, right, has_left, has_right = sources_of(step, me, peers)
+
+    def add(source, piece):
+        at = rows // block + source * (slot // block)
+        add_piece(
+            piece[rows:, 0:slot], piece[0:rows, :], (me, mate), lambda dest, j: spread[dest, at + j],
+            y_own, y_mate, rows, slot, block,
+        )
+
+    pl.when(has_left)(lambda: add(left, left_piece))
+    pl.when(has_right)(lambda: add(right, right_piece))
+
+
+def gather_kernel(steps, far_count, rows, slot, far_slot, block, peers, where, nb_own, nb_mate, *refs):
+    own, adj_own, adj_mate, *refs = refs
+    arrived = refs[: 2 * steps]
+    far = refs[2 * steps : 2 * steps + far_count]
+    y_own, y_mate, spread = refs[2 * steps + far_count :]
+    me, cluster = where[0], where[1]
+    mate = me + 1 - 2 * (me % CORES)
+    spread[...] = jnp.zeros(spread.shape, BF)
+    per_dev, tiles = adj_own.shape[0], adj_own.shape[1]
+    for dest, (adj, nb) in enumerate(((adj_own, nb_own), (adj_mate, nb_mate))):
+        for b in range(per_dev):
+            for s in range(tiles):
+                spread[dest, nb[b, s], b * block : (b + 1) * block, :] = adj[b, s]
+    mine = jnp.concatenate([spread[0, j] for j in range(per_dev)], axis=1)
+    y_own[...] = mm(mine, own[0:rows, :])
+    y_mate[...] = jnp.zeros(y_mate.shape, F32)
+    base = rows // block
+    add_piece(
+        own[rows:, 0:slot], own[0:rows, :], (me, mate),
+        lambda dest, j: spread[dest, base + me * (slot // block) + j],
+        y_own, y_mate, rows, slot, block,
+    )
+    first_far = base + peers * (slot // block)
+    tiles_far = []
+    for f in range(far_count):
+        source = far_source(f, cluster, far_count)
+        for j in range(far_slot // block):
+            tiles_far.append(spread[0, first_far + source * (far_slot // block) + j])
+    y_own[...] += mm(jnp.concatenate(tiles_far, axis=1), jnp.concatenate([r[...] for r in far], axis=0))
+    for t in range(steps):
+        add_arrived(
+            t + 1, where, arrived[2 * t], arrived[2 * t + 1], spread, y_own, y_mate, rows, slot, block, peers
+        )
+
+
+def gather_more_kernel(step, rows, slot, block, peers, where, left, right, spread, own_in, mate_in, y_own, y_mate):
+    y_own[...] = own_in[...]
+    y_mate[...] = mate_in[...]
+    add_arrived(step, where, left, right, spread, y_own, y_mate, rows, slot, block, peers)
+
+
+def far_source(step, cluster, clusters):
+    if clusters & (clusters - 1) == 0:
+        return cluster ^ step
+    return (cluster - step) % clusters
+
+
+def far_target(step, cluster, clusters):
+    if clusters & (clusters - 1) == 0:
+        return cluster ^ step
+    return (cluster + step) % clusters
+
+
+def pick_kernel(clusters, where, lists, x, *outs):
+    rows = x.shape[0]
+    numbers = lax.broadcasted_iota(jnp.int32, (rows, lists.shape[-1]), 0)
+    for step, out in enumerate(outs):
+        row = lists[0, pl.ds(far_target(step, where[1], clusters), 1), :]
+        chosen = jnp.where(numbers == row, 1.0, 0.0).astype(BF)
+        out[...] = mm(chosen, x[...], ((0,), (0,))).astype(BF)
+
+
+def local_kernel(x, y_own, y_got, w, out):
+    mixed = (y_own[...] + y_got[...]).astype(BF)
+    agg = mm(mixed, w[...])
+    out[...] = layer_norm(x[...].astype(F32) + agg)
+
+
+def tail_kernel(rows, x, local, top, total, acc, got, w_out, w_up, w_down, out):
+    heads = top.shape[0]
+    width = acc.shape[0]
+    head = width // heads
+    top_a = top[:, 0:rows]
+    top_b = got[width : width + heads, :]
+    peak = jnp.maximum(top_a, top_b)
+    fade_a = jnp.exp2(top_a - peak)
+    fade_b = jnp.exp2(top_b - peak)
+    whole = total[:, 0:rows] * fade_a + got[width + heads :, :] * fade_b
+    fade_a = fade_a / whole
+    fade_b = fade_b / whole
+    pieces = []
+    for h in range(heads):
+        at = slice(h * head, (h + 1) * head)
+        pieces.append((acc[at, 0:rows] * fade_a[h : h + 1, :] + got[at, :] * fade_b[h : h + 1, :]).astype(BF))
+    attended = jnp.concatenate(pieces, axis=0)
+    projected = mm(attended, w_out[...], ((0,), (0,)))
+    summed = local[...] + layer_norm(x[...].astype(F32) + projected)
+    activated = jax.nn.gelu(mm(summed.astype(BF), w_up[...])).astype(BF)
+    out[...] = layer_norm(summed + mm(activated, w_down[...])).astype(BF)
+
+
+def line_plan(
+    node_feats,
+    w_gcn,
+    adj_tiles,
+    neighbor_blocks,
+    inner_rows,
+    outer_rows,
+    w_qkv,
+    key_blocks,
+    key_counts,
+    w_out,
+    w_up,
+    w_down,
+):
+    rows, width = node_feats.shape
+    block = adj_tiles.shape[-1]
+    peers = lax.axis_size("dev")
+    clusters = lax.axis_size("group")
+    chips = peers // CORES
+    slot = inner_rows.shape[-1]
+    far_slot = outer_rows.shape[-1]
+    cluster = lax.axis_index("group")
+    where = jnp.stack([lax.axis_index("dev"), cluster]).astype(jnp.int32)
+    swap = [(CORES * c + k, CORES * c + 1 - k) for c in range(chips) for k in range(CORES)]
+
+    def hop(value, step, far):
+        pairs = []
+        for c in range(chips):
+            to = c + step
+            if 0 <= to < chips and 0 <= to - step * far < chips:
+                pairs += [(CORES * c + k, CORES * to + k) for k in range(CORES)]
+        return lax.ppermute(value, "dev", pairs)
+
+    lists = jnp.pad(inner_rows[0].astype(BF), ((0, 0), (0, width - slot)))
+    piece = jnp.concatenate([node_feats, lists], axis=0)
+    left, right = hop(piece, 1, 1), hop(piece, -1, 1)
+    mate_piece = lax.ppermute(piece, "dev", swap)
+    mate_adj = lax.ppermute(adj_tiles, "dev", swap)
+    mate_nb = lax.ppermute(neighbor_blocks, "dev", swap)
+
+    picked = pl.pallas_call(
+        functools.partial(pick_kernel, clusters),
+        in_specs=[SMEM, VMEM, VMEM],
+        out_specs=[VMEM] * clusters,
+        out_shape=[jax.ShapeDtypeStruct((far_slot, width), BF)] * clusters,
+        compiler_params=grant(8),
+        cost_estimate=pl.CostEstimate(
+            flops=2 * rows * clusters * far_slot * width, transcendentals=0, bytes_accessed=1 << 20
+        ),
+        name="pick",
+    )(where, outer_rows, node_feats)
+    far = [picked[0]]
+    for s in range(1, clusters):
+        pairs = [(c, far_target(s, c, clusters)) for c in range(clusters)]
+        far.append(lax.ppermute(picked[s], "group", pairs))
+
+    slots = jnp.arange(key_blocks.shape[1], dtype=jnp.int32)[None, :]
+    live = jnp.sum(jnp.where(slots < key_counts[:, None], jnp.left_shift(1, key_blocks), 0), axis=1)
+    live = live.astype(jnp.int32)
+
+    attend = lambda mode, step, pieces, state: attend_call(
+        mode, step, pieces, state, where, live, w_qkv, rows, block, peers
+    )
+    state = attend((True, False, False), 0, [piece, mate_piece], None)
+    arrived = []
+    for step in range(1, chips):
+        pair = [left, right]
+        final = step + 1 == chips
+        if final:
+            sums = gather_call(
+                where, neighbor_blocks, mate_nb, piece, adj_tiles, mate_adj, arrived, far, rows, slot, far_slot, block, peers
+            )
+            sums = gather_more_call(step, where, pair, sums, rows, slot, block, peers)
+            y_got = lax.ppermute(sums[1], "dev", swap)
+        else:
+            left, right = hop(left, 1, step + 1), hop(right, -1, step + 1)
+        two = 2 * step <= chips - 1
+        state = attend((False, final and not two, False), step, pair, state)
+        if two:
+            state = attend((False, final, True), step, pair, state)
+        arrived += pair
+    send, top, total, acc = state
+    got = lax.ppermute(send, "dev", swap)
+    local = pl.pallas_call(
+        local_kernel,
+        in_specs=[VMEM] * 4,
+        out_specs=VMEM,
+        out_shape=jax.ShapeDtypeStruct((rows, width), F32),
+        compiler_params=grant(16),
+        cost_estimate=pl.CostEstimate(flops=2 * rows * width * width, transcendentals=0, bytes_accessed=4 << 20),
+        name="local",
+    )(node_feats, sums[0], y_got, w_gcn)
+    return pl.pallas_call(
+        functools.partial(tail_kernel, rows),
+        in_specs=[VMEM] * 9,
+        out_specs=VMEM,
+        out_shape=jax.ShapeDtypeStruct((rows, width), BF),
+        compiler_params=grant(32),
+        cost_estimate=pl.CostEstimate(
+            flops=2 * rows * width * (width + 2 * w_up.shape[1]), transcendentals=0, bytes_accessed=12 << 20
+        ),
+        name="tail",
+    )(node_feats, local, top, total, acc, got, w_out, w_up, w_down)
+
+
+def gather_call(
+    where, nb_own, nb_mate, own, adj_own, adj_mate, arrived, far, rows, slot, far_slot, block, peers
+):
+    width = own.shape[1]
+    table_blocks = (rows + peers * slot + len(far) * far_slot) // block
+    y = jax.ShapeDtypeStruct((rows, width), F32)
+    spread = jax.ShapeDtypeStruct((CORES, table_blocks, rows, block), BF)
+    steps = len(arrived) // 2
+    return pl.pallas_call(
+        functools.partial(gather_kernel, steps, len(far), rows, slot, far_slot, block, peers),
+        in_specs=[SMEM] * 3 + [VMEM] * (3 + len(arrived) + len(far)),
+        out_specs=[VMEM] * 3,
+        out_shape=[y, y, spread],
+        compiler_params=grant(24),
+        cost_estimate=pl.CostEstimate(
+            flops=4 * rows * rows * width * (2 + steps), transcendentals=0, bytes_accessed=8 << 20
+        ),
+        name="gather",
+    )(where, nb_own, nb_mate, own, adj_own, adj_mate, *arrived, *far)
+
+
+def gather_more_call(step, where, pair, sums, rows, slot, block, peers):
+    y_own, y_mate, spread = sums
+    return pl.pallas_call(
+        functools.partial(gather_more_kernel, step, rows, slot, block, peers),
+        in_specs=[SMEM] + [VMEM] * 5,
+        out_specs=[VMEM] * 2,
+        out_shape=[jax.ShapeDtypeStruct(y_own.shape, F32)] * 2,
+        input_output_aliases={4: 0, 5: 1},
+        compiler_params=grant(16),
+        cost_estimate=pl.CostEstimate(
+            flops=4 * rows * rows * y_own.shape[1], transcendentals=0, bytes_accessed=4 << 20
+        ),
+        name="gather_more",
+    )(where, *pair, spread, y_own, y_mate)
+
+
+def per_device(*args):
+    inner, feats, tiles = args[4], args[0], args[2]
+    whole_slots = inner.shape[-1] == feats.shape[0] and feats.shape[0] <= 256
+    whole_slots = whole_slots and args[8].shape[0] <= 31
+    if whole_slots and lax.axis_size("dev") % CORES == 0 and inner.shape[-1] % tiles.shape[-1] == 0:
+        return line_plan(*args)
+    return gathered_plan(*args)
+
+
 def solution(mesh):
     placed = (
         P(("group", "dev"), None),

time: 269 us -> 85.4 us (0.32)
  matrix products: 93.5 us -> 0 us
  blocking collectives: 62.2 us -> 0 us
  Pallas kernels: 0 us -> 42.8 us
  local copies, waits for them, and re-layouts: 45.2 us -> 5.71 us
  other arithmetic: 33.6 us -> 2.7 us
  between operations: 13.6 us -> 0.29 us
  waiting for transfers between devices: 7.31 us -> 17.5 us
  starting transfers between devices: 11.9 us -> 16 us
    dot_general x12 -> x0, matrix products: 93.5 us -> none  [the longest x2 30.4 us: attend(): jnp.einsum('leqi,leqsj->qlisj', queries, keys_here, preferred_element_typ...]
    all_gather x2 -> x0, blocking collectives: 62.2 us -> none  [the longest x1 53.9 us: per_device(): lax.all_gather(inner_rows, 'dev', axis=0, tiled=True)]
    pallas_call x0 -> x10, Pallas kernels: none -> 42.8 us  [the longest x5 31.5 us: attend_call(): pl.pallas_call(functools.partial(attend_kernel, mode, step, rows, block,...]
    reduce_sum x5 -> x1, other arithmetic: 30.6 us -> 0.84 us  [line_plan(): jnp.sum(jnp.where(slots < key_counts[:, None], jnp.left_shift(1, key_bloc...]
    gather x2 -> x0, local copies, waits for them, and re-layouts: 19 us -> none  [the longest x1 13.7 us: per_device(): inner_part = whole_rows[inner_index]]
    ppermute x0 -> x14, waiting for transfers between devices: none -> 17.5 us  [the longest x6 8.52 us: hop(): return lax.ppermute(value, 'dev', pairs)]
    ppermute x0 -> x14, starting transfers between devices: none -> 16 us  [the longest x6 10.2 us: hop(): return lax.ppermute(value, 'dev', pairs)]
    all_to_all x2 -> x0, starting transfers between devices: 11.9 us -> none  [the longest x1 6.16 us: per_device(): lax.all_to_all(qkv_split, 'dev', split_axis=0, concat_axis=3, tiled=True)]
  transfers between devices with their start and end apart: 4 -> 14, of which waited for: 1 -> 4; matrix products, arithmetic and copies ran while one was open for 51% -> 1% of each run, Pallas kernels for 0% -> 36%
where the time goes in v2:
time: 85.4 us; the launch traced here: 85 us
  Pallas kernels  42.8 us (50%)
  waiting for transfers between devices  17.5 us (20%)
  starting transfers between devices  16 us (19%)
  local copies, waits for them, and re-layouts  5.71 us (7%)
  other arithmetic  2.7 us (3%)
    pallas_call x5, Pallas kernels, attend_call(): pl.pallas_call(functools.partial(attend_kernel, mode, step, rows, block,...  31.5 us
    ppermute x6, starting transfers between devices, hop(): return lax.ppermute(value, 'dev', pairs)  10.2 us
    ppermute x6, waiting for transfers between devices, hop(): return lax.ppermute(value, 'dev', pairs)  8.52 us
    ppermute x3, waiting for transfers between devices, line_plan(): far.append(lax.ppermute(picked[s], 'group', pairs))  6.7 us
    unnamed x22, local copies, waits for them, and re-layouts  5.71 us
    pallas_call x1, Pallas kernels, line_plan(): pl.pallas_call(functools.partial(tail_kernel, rows), in_specs=[VMEM] * 9,...  4.57 us
    ppermute x3, starting transfers between devices, line_plan(): far.append(lax.ppermute(picked[s], 'group', pairs))  4.51 us
    pallas_call x1, Pallas kernels, gather_call(): pl.pallas_call(functools.partial(gather_kernel, steps, len(far), rows, sl...  3.28 us
  transfers between devices with their start and end apart: 14, of which 4 were waited for; matrix products, arithmetic and copies ran while one was open for 1% of the time, Pallas kernels for 36%

profile of v2, /device:TPU:0, one launch (start us, length us, event | category | flops | bytes accessed | tf_op | source)
XLA Modules:
  0.0 85.0 jit_solution(12751571936888824185)
XLA Ops:
  0.0 0.0 copy-start.10
  0.0 0.7 convert_bitcast_fusion
  0.7 1.1 %fusion.1.refs_0_ = bf16[264,1024]{1,0:T(8,128)(2,1)S(1)} fusion(bf16[8,256]{1,0:T(8,128)(2,1)S(1)} %convert_bitcast_fusion, bf16[256,1024]{1,0:T(8,128)(2,1)} %x.7), kind=kLoop, calls=%fused_computation.2 | loop fusion | flops 1622016 | bytes 1069056 | tf_op jit(solution)/shard_map/concatenate | solution.py:490
  1.8 5.0 %collective-permute-start = (bf16[264,1024]{1,0:T(8,128)(2,1)S(1)}, bf16[264,1024]{1,0:T(8,128)(2,1)S(1)}, u32[]{:S(2)}, u32[]{:S(2)}) collective-permute-start(bf16[264,1024]{1,0:T(8,128)(2,1)S(1)} %fusion.1.refs_0_), channel_id=1, source_target_pairs={{0,2},{1,3},{2,4},{3,5},{4,6},{5,7},{8,10},{9,11},{10,12},{11,13},... | collective-permute-start | bytes 1622024 | tf_op jit(solution)/shard_map/ppermute | solution.py:487
  6.8 1.3 %collective-permute-start.3 = (bf16[264,1024]{1,0:T(8,128)(2,1)S(1)}, bf16[264,1024]{1,0:T(8,128)(2,1)S(1)}, u32[]{:S(2)}, u32[]{:S(2)}) collective-permute-start(bf16[264,1024]{1,0:T(8,128)(2,1)S(1)} %fusion.1.refs_0_), channel_id=1, source_target_pairs={{2,0},{3,1},{4,2},{5,3},{6,4},{7,5},{10,8},{11,9},{12,10},{13,11},... | collective-permute-start | bytes 1622024 | tf_op jit(solution)/shard_map/ppermute | solution.py:487
  8.1 0.1 collective-permute-start.12
  8.2 0.5 collective-permute-start.6
  8.7 0.1 collective-permute-start.7
  8.7 0.1 pad_add_fusion.where
  8.8 0.0 copy-start
  8.8 1.0 %copy-done = bf16[256,1024]{1,0:T(8,128)(2,1)S(1)} copy-done((bf16[256,1024]{1,0:T(8,128)(2,1)S(1)}, bf16[256,1024]{1,0:T(8,128)(2,1)}, u32[]{:S(2)}) %copy-start) | copy-done | bytes 524312
  9.9 0.0 copy-start.9
  9.9 0.7 copy-done.9
  10.5 1.0 %pick.1 = (bf16[128,1024]{1,0:T(8,128)(2,1)S(1)}, bf16[128,1024]{1,0:T(8,128)(2,1)S(1)}, bf16[128,1024]{1,0:T(8,128)(2,1)S(1)}, bf16[128,1024]{1,0:T(8,128)(2,1)S(1)}) custom-call(s32[2]{0:T(128)S(1)} %pad_add_fusion.where, s32[1,4,128]{2,1,0:T(4,128)S(1)} %copy-done.9, bf16[256,1024]{1,0:T(8,128)(2,1)S(1)} %copy-done), custom_call_target="tpu_custom_call" | custom-call | flops 268435456 | bytes 1048576 | tf_op jit(solution)/shard_map/pick/pallas_call | solution.py:496
  11.6 0.0 copy-done.10
  11.6 0.8 select_reduce_fusion.live
  12.4 5.9 %collective-permute-done.refs_3_.refs_0_ = bf16[264,1024]{1,0:T(8,128)(2,1)S(1)} collective-permute-done((bf16[264,1024]{1,0:T(8,128)(2,1)S(1)}, bf16[264,1024]{1,0:T(8,128)(2,1)S(1)}, u32[]{:S(2)}, u32[]{:S(2)}) %collective-permute-start) | collective-permute-done | bytes 540704 | tf_op jit(solution)/shard_map/ppermute | solution.py:487
  18.3 1.5 %collective-permute-start.8 = (bf16[128,1024]{1,0:T(8,128)(2,1)S(1)}, bf16[128,1024]{1,0:T(8,128)(2,1)S(1)}, u32[]{:S(2)}, u32[]{:S(2)}) collective-permute-start(bf16[128,1024]{1,0:T(8,128)(2,1)S(1)} %get-tuple-element.32), channel_id=1, source_target_pairs={{0,8},{8,0},{16,24},{24,16},{1,9},{9,1},{17,25},{25,17},{2,10},{10... | collective-permute-start | bytes 786440 | tf_op jit(solution)/shard_map/ppermute | solution.py:510
  19.8 2.7 %collective-permute-done.3.refs_4_.refs_1_ = bf16[264,1024]{1,0:T(8,128)(2,1)S(1)} collective-permute-done((bf16[264,1024]{1,0:T(8,128)(2,1)S(1)}, bf16[264,1024]{1,0:T(8,128)(2,1)S(1)}, u32[]{:S(2)}, u32[]{:S(2)}) %collective-permute-start.3) | collective-permute-done | bytes 540704 | tf_op jit(solution)/shard_map/ppermute | solution.py:487
  22.4 0.7 collective-permute-start.1
  23.1 0.0 collective-permute-done.12.refs_1_
  23.1 1.3 %collective-permute-start.4 = (bf16[264,1024]{1,0:T(8,128)(2,1)S(1)}, bf16[264,1024]{1,0:T(8,128)(2,1)S(1)}, u32[]{:S(2)}, u32[]{:S(2)}) collective-permute-start(bf16[264,1024]{1,0:T(8,128)(2,1)S(1)} %collective-permute-done.3.refs_4_.refs_1_), channel_id=1, source_target_pairs={{2,0},{3,1},{4,2},{5,3},{10,8},{11,9},{12,10},{13,11},{18,16},{19,... | collective-permute-start | bytes 1622024 | tf_op jit(solution)/shard_map/ppermute | solution.py:487
  24.4 0.0 copy-start.8
  24.4 2.8 %copy-done.8 = bf16[1024,3072]{1,0:T(8,128)(2,1)S(1)} copy-done((bf16[1024,3072]{1,0:T(8,128)(2,1)S(1)}, bf16[1024,3072]{1,0:T(8,128)(2,1)}, u32[]{:S(2)}) %copy-start.8) | copy-done | bytes 6291480
  27.2 8.3 %attend0.1 = (bf16[1024,512]{1,0:T(8,128)(2,1)S(1)}, f32[32,512]{1,0:T(8,128)S(1)}, f32[32,512]{1,0:T(8,128)S(1)}, f32[1024,512]{1,0:T(8,128)S(1)}) custom-call(s32[2]{0:T(128)S(1)} %pad_add_fusion.where, s32[16]{0:T(128)S(1)} %select_reduce_fusion.live, bf16[264,1024]{1,0:T(8,128)(2,1)S(1)} %fusion.1.refs_0_, ...), custom_call_target="tpu_custom_call" | custom-call | flops 3221225472 | bytes 4194304 | tf_op jit(solution)/shard_map/attend0/pallas_call | solution.py:310
  35.5 7.4 %attend1.1 = (f32[32,512]{1,0:T(8,128)S(1)}, f32[32,512]{1,0:T(8,128)S(1)}, f32[1024,512]{1,0:T(8,128)S(1)}) custom-call(s32[2]{0:T(128)S(1)} %pad_add_fusion.where, s32[16]{0:T(128)S(1)} %select_reduce_fusion.live, bf16[264,1024]{1,0:T(8,128)(2,1)S(1)} %collective-permute-done.refs_3_.refs_0_, ...), custom_call_target="tpu_custom_call", output_to_operand_aliasing={{0}: (6, {}), {1}: (7, {}), {2}: (8, {})} | custom-call | flops 3221225472 | bytes 4194304 | tf_op jit(solution)/shard_map/attend1/pallas_call | solution.py:310
  42.9 0.0 collective-permute-done.6.nb_mate
  42.9 1.6 %collective-permute-start.9 = (bf16[128,1024]{1,0:T(8,128)(2,1)S(1)}, bf16[128,1024]{1,0:T(8,128)(2,1)S(1)}, u32[]{:S(2)}, u32[]{:S(2)}) collective-permute-start(bf16[128,1024]{1,0:T(8,128)(2,1)S(1)} %get-tuple-element.33), channel_id=1, source_target_pairs={{0,16},{8,24},{16,0},{24,8},{1,17},{9,25},{17,1},{25,9},{2,18},{10... | collective-permute-start | bytes 786440 | tf_op jit(solution)/shard_map/ppermute | solution.py:510
  44.5 0.0 collective-permute-done.8.refs_8_
  44.5 1.4 %collective-permute-start.10 = (bf16[128,1024]{1,0:T(8,128)(2,1)S(1)}, bf16[128,1024]{1,0:T(8,128)(2,1)S(1)}, u32[]{:S(2)}, u32[]{:S(2)}) collective-permute-start(bf16[128,1024]{1,0:T(8,128)(2,1)S(1)} %get-tuple-element.34), channel_id=1, source_target_pairs={{0,24},{8,16},{16,8},{24,0},{1,25},{9,17},{17,9},{25,1},{2,26},{10... | collective-permute-start | bytes 786440 | tf_op jit(solution)/shard_map/ppermute | solution.py:510
  45.9 0.0 collective-permute-done.1.refs_5_.refs_0_
  45.9 0.7 collective-permute-start.2
  46.6 0.0 collective-permute-done.4.refs_6_.refs_1_
  46.6 1.3 %collective-permute-start.5 = (bf16[264,1024]{1,0:T(8,128)(2,1)S(1)}, bf16[264,1024]{1,0:T(8,128)(2,1)S(1)}, u32[]{:S(2)}, u32[]{:S(2)}) collective-permute-start(bf16[264,1024]{1,0:T(8,128)(2,1)S(1)} %collective-permute-done.4.refs_6_.refs_1_), channel_id=1, source_target_pairs={{2,0},{3,1},{10,8},{11,9},{18,16},{19,17},{26,24},{27,25}} | collective-permute-start | bytes 1622024 | tf_op jit(solution)/shard_map/ppermute | solution.py:487
  47.9 0.0 copy-start.6
  48.0 0.0 copy-start.7
  48.0 0.8 attend1b.1
  48.8 6.7 %collective-permute-done.9.refs_9_ = bf16[128,1024]{1,0:T(8,128)(2,1)S(1)} collective-permute-done((bf16[128,1024]{1,0:T(8,128)(2,1)S(1)}, bf16[128,1024]{1,0:T(8,128)(2,1)S(1)}, u32[]{:S(2)}, u32[]{:S(2)}) %collective-permute-start.9) | collective-permute-done | bytes 262176 | tf_op jit(solution)/shard_map/ppermute | solution.py:510
  55.5 0.0 collective-permute-done.10.refs_10_
  55.5 0.0 collective-permute-done.7.refs_2_
  55.5 0.0 copy-done.6
  55.5 0.0 copy-done.7
  55.5 3.3 %gather.1 = (f32[256,1024]{1,0:T(8,128)S(1)}, f32[256,1024]{1,0:T(8,128)S(1)}, bf16[2,22,256,128]{3,2,1,0:T(8,128)(2,1)S(1)}) custom-call(s32[2]{0:T(128)S(1)} %pad_add_fusion.where, s32[2,16]{1,0:T(2,128)S(1)} %copy-done.7, s32[2,16]{1,0:T(2,128)S(1)} %collective-permute-done.6.nb_mate, bf16[264,1024]{1,0:T(8,128)(2,1)S(1)} %fusion.1.refs_0_, ...), custom_call_target="tpu_custom_call" | custom-call | flops 1073741824 | bytes 8388608 | tf_op jit(solution)/shard_map/gather/pallas_call | solution.py:569
  58.8 7.4 %attend2.1 = (f32[32,512]{1,0:T(8,128)S(1)}, f32[32,512]{1,0:T(8,128)S(1)}, f32[1024,512]{1,0:T(8,128)S(1)}) custom-call(s32[2]{0:T(128)S(1)} %pad_add_fusion.where, s32[16]{0:T(128)S(1)} %select_reduce_fusion.live, bf16[264,1024]{1,0:T(8,128)(2,1)S(1)} %collective-permute-done.1.refs_5_.refs_0_, ...), custom_call_target="tpu_custom_call", output_to_operand_aliasing={{0}: (6, {}), {1}: (7, {}), {2}: (8, {})} | custom-call | flops 3221225472 | bytes 4194304 | tf_op jit(solution)/shard_map/attend2/pallas_call | solution.py:310
  66.2 0.0 collective-permute-done.2.left.refs_0_
  66.2 0.0 collective-permute-done.5.right.refs_1_
  66.2 0.0 copy-start.5
  66.2 7.6 %attend3.1 = (f32[1088,256]{1,0:T(8,128)S(1)}, f32[32,512]{1,0:T(8,128)S(1)}, f32[32,512]{1,0:T(8,128)S(1)}, f32[1024,512]{1,0:T(8,128)S(1)}) custom-call(s32[2]{0:T(128)S(1)} %pad_add_fusion.where, s32[16]{0:T(128)S(1)} %select_reduce_fusion.live, ...), custom_call_target="tpu_custom_call", output_to_operand_aliasing={{1}: (6, {}), {2}: (7, {}), {3}: (8, {})} | custom-call | flops 3221225472 | bytes 4194304 | tf_op jit(solution)/shard_map/attend3/pallas_call | solution.py:310
  73.9 0.1 collective-permute-start.13
  74.0 0.0 copy-start.1
  74.0 0.0 copy-start.3
  74.0 0.0 copy-start.4
  74.0 1.4 %gather_more.1 = (f32[256,1024]{1,0:T(8,128)S(1)}, f32[256,1024]{1,0:T(8,128)S(1)}) custom-call(s32[2]{0:T(128)S(1)} %pad_add_fusion.where, bf16[264,1024]{1,0:T(8,128)(2,1)S(1)} %collective-permute-done.2.left.refs_0_, bf16[264,1024]{1,0:T(8,128)(2,1)S(1)} %collective-permute-done.5.right.refs_1_, ...), custom_call_target="tpu_custom_call", output_to_operand_aliasing={{0}: (4, {}), {1}: (5, {})} | custom-call | flops 268435456 | bytes 4194304 | tf_op jit(solution)/shard_map/gather_more/pallas_call | solution.py:584
  75.4 0.5 collective-permute-start.11
  75.9 2.3 %collective-permute-done.11.y_got = f32[256,1024]{1,0:T(8,128)S(1)} collective-permute-done((f32[256,1024]{1,0:T(8,128)S(1)}, f32[256,1024]{1,0:T(8,128)S(1)}, u32[]{:S(2)}, u32[]{:S(2)}) %collective-permute-start.11) | collective-permute-done | bytes 1048608 | tf_op jit(solution)/shard_map/ppermute | solution.py:529
  78.2 0.0 copy-done.5
  78.2 0.0 copy-done.1
  78.2 0.0 copy-start.2
  78.2 1.0 %local.1 = f32[256,1024]{1,0:T(8,128)S(1)} custom-call(bf16[256,1024]{1,0:T(8,128)(2,1)S(1)} %copy-done.1, f32[256,1024]{1,0:T(8,128)S(1)} %get-tuple-element.38.y_own, f32[256,1024]{1,0:T(8,128)S(1)} %collective-permute-done.11.y_got, bf16[1024,1024]{1,0:T(8,128)(2,1)S(1)} %copy-done.5), custom_call_target="tpu_custom_call" | custom-call | flops 536870912 | bytes 4194304 | tf_op jit(solution)/shard_map/local/pallas_call | solution.py:539
  79.2 0.0 collective-permute-done.13.got
  79.2 0.0 copy-done.3
  79.2 0.0 copy-done.4
  79.3 1.2 %copy-done.2 = bf16[1024,2048]{1,0:T(8,128)(2,1)S(1)} copy-done((bf16[1024,2048]{1,0:T(8,128)(2,1)S(1)}, bf16[1024,2048]{1,0:T(8,128)(2,1)}, u32[]{:S(2)}) %copy-start.2) | copy-done | bytes 4194328
  80.4 4.6 %tail.1 = bf16[256,1024]{1,0:T(8,128)(2,1)} custom-call(bf16[256,1024]{1,0:T(8,128)(2,1)S(1)} %copy-done.1, f32[256,1024]{1,0:T(8,128)S(1)} %local.1, f32[32,512]{1,0:T(8,128)S(1)} %get-tuple-element.53.top, f32[32,512]{1,0:T(8,128)S(1)} %get-tuple-element.54.total, f32[1024,512]{1,0:T(8,128)S(1)} %get-tuple-element.55.acc, ...), custom_call_target="tpu_custom_call" | custom-call | flops 2684354560 | bytes 12582912 | tf_op jit(solution)/shard_map/tail/pallas_call | solution.py:548
Async XLA Ops:
  0.0 11.6 %copy-start.10 = (s32[16,16]{1,0:T(8,128)S(1)}, s32[16,16]{1,0:T(8,128)}, u32[]{:S(2)}) copy-start(s32[16,16]{1,0:T(8,128)} %param.19) | copy-start | bytes 3076
  1.8 16.5 %collective-permute-start = (bf16[264,1024]{1,0:T(8,128)(2,1)S(1)}, bf16[264,1024]{1,0:T(8,128)(2,1)S(1)}, u32[]{:S(2)}, u32[]{:S(2)}) collective-permute-start(bf16[264,1024]{1,0:T(8,128)(2,1)S(1)} %fusion.1.refs_0_), channel_id=1, source_target_pairs={{0,2},{1,3},{2,4},{3,5},{4,6},{5,7},{8,10},{9,11},{10,12},{11,13},... | collective-permute-start | bytes 1622024 | tf_op jit(solution)/shard_map/ppermute | solution.py:487
  6.8 15.6 %collective-permute-start.3 = (bf16[264,1024]{1,0:T(8,128)(2,1)S(1)}, bf16[264,1024]{1,0:T(8,128)(2,1)S(1)}, u32[]{:S(2)}, u32[]{:S(2)}) collective-permute-start(bf16[264,1024]{1,0:T(8,128)(2,1)S(1)} %fusion.1.refs_0_), channel_id=1, source_target_pairs={{2,0},{3,1},{4,2},{5,3},{6,4},{7,5},{10,8},{11,9},{12,10},{13,11},... | collective-permute-start | bytes 1622024 | tf_op jit(solution)/shard_map/ppermute | solution.py:487
  8.1 15.0 %collective-permute-start.12 = (bf16[264,1024]{1,0:T(8,128)(2,1)S(1)}, bf16[264,1024]{1,0:T(8,128)(2,1)S(1)}, u32[]{:S(2)}, u32[]{:S(2)}) collective-permute-start(bf16[264,1024]{1,0:T(8,128)(2,1)S(1)} %fusion.1.refs_0_), channel_id=1, source_target_pairs={{0,1},{1,0},{2,3},{3,2},{4,5},{5,4},{6,7},{7,6},{8,9},{9,8},{10,11... | collective-permute-start | bytes 1622024 | tf_op jit(solution)/shard_map/ppermute | solution.py:492
  8.2 34.7 %collective-permute-start.6 = (s32[2,16]{1,0:T(2,128)}, s32[2,16]{1,0:T(2,128)S(1)}, u32[]{:S(2)}, u32[]{:S(2)}) collective-permute-start(s32[2,16]{1,0:T(2,128)} %nb_own.1), channel_id=1, source_target_pairs={{0,1},{1,0},{2,3},{3,2},{4,5},{5,4},{6,7},{7,6},{8,9},{9,8},{10,11... | collective-permute-start | bytes 392 | tf_op jit(solution)/shard_map/ppermute | solution.py:494
  8.7 46.8 %collective-permute-start.7 = (bf16[2,16,128,128]{3,2,1,0:T(8,128)(2,1)}, bf16[2,16,128,128]{3,2,1,0:T(8,128)(2,1)S(1)}, u32[]{:S(2)}, u32[]{:S(2)}) collective-permute-start(bf16[2,16,128,128]{3,2,1,0:T(8,128)(2,1)} %refs_1_.1), channel_id=1, source_target_pairs={{0,1},{1,0},{2,3},{3,2},{4,5},{5,4},{6,7},{7,6},{8,9},{9,8},{10,11... | collective-permute-start | bytes 3145736 | tf_op jit(solution)/shard_map/ppermute | solution.py:493
  8.8 1.0 %copy-start = (bf16[256,1024]{1,0:T(8,128)(2,1)S(1)}, bf16[256,1024]{1,0:T(8,128)(2,1)}, u32[]{:S(2)}) copy-start(bf16[256,1024]{1,0:T(8,128)(2,1)} %x.7) | copy-start | bytes 1572868
  9.9 0.7 copy-start.9
  18.3 26.2 %collective-permute-start.8 = (bf16[128,1024]{1,0:T(8,128)(2,1)S(1)}, bf16[128,1024]{1,0:T(8,128)(2,1)S(1)}, u32[]{:S(2)}, u32[]{:S(2)}) collective-permute-start(bf16[128,1024]{1,0:T(8,128)(2,1)S(1)} %get-tuple-element.32), channel_id=1, source_target_pairs={{0,8},{8,0},{16,24},{24,16},{1,9},{9,1},{17,25},{25,17},{2,10},{10... | collective-permute-start | bytes 786440 | tf_op jit(solution)/shard_map/ppermute | solution.py:510
  22.4 23.5 %collective-permute-start.1 = (bf16[264,1024]{1,0:T(8,128)(2,1)S(1)}, bf16[264,1024]{1,0:T(8,128)(2,1)S(1)}, u32[]{:S(2)}, u32[]{:S(2)}) collective-permute-start(bf16[264,1024]{1,0:T(8,128)(2,1)S(1)} %collective-permute-done.refs_3_.refs_0_), channel_id=1, source_target_pairs={{2,4},{3,5},{4,6},{5,7},{10,12},{11,13},{12,14},{13,15},{18,20},{1... | collective-permute-start | bytes 1622024 | tf_op jit(solution)/shard_map/ppermute | solution.py:487
  23.1 23.5 %collective-permute-start.4 = (bf16[264,1024]{1,0:T(8,128)(2,1)S(1)}, bf16[264,1024]{1,0:T(8,128)(2,1)S(1)}, u32[]{:S(2)}, u32[]{:S(2)}) collective-permute-start(bf16[264,1024]{1,0:T(8,128)(2,1)S(1)} %collective-permute-done.3.refs_4_.refs_1_), channel_id=1, source_target_pairs={{2,0},{3,1},{4,2},{5,3},{10,8},{11,9},{12,10},{13,11},{18,16},{19,... | collective-permute-start | bytes 1622024 | tf_op jit(solution)/shard_map/ppermute | solution.py:487
  24.4 2.8 %copy-start.8 = (bf16[1024,3072]{1,0:T(8,128)(2,1)S(1)}, bf16[1024,3072]{1,0:T(8,128)(2,1)}, u32[]{:S(2)}) copy-start(bf16[1024,3072]{1,0:T(8,128)(2,1)} %refs_2_.9) | copy-start | bytes 18874372
  42.9 12.6 %collective-permute-start.9 = (bf16[128,1024]{1,0:T(8,128)(2,1)S(1)}, bf16[128,1024]{1,0:T(8,128)(2,1)S(1)}, u32[]{:S(2)}, u32[]{:S(2)}) collective-permute-start(bf16[128,1024]{1,0:T(8,128)(2,1)S(1)} %get-tuple-element.33), channel_id=1, source_target_pairs={{0,16},{8,24},{16,0},{24,8},{1,17},{9,25},{17,1},{25,9},{2,18},{10... | collective-permute-start | bytes 786440 | tf_op jit(solution)/shard_map/ppermute | solution.py:510
  44.5 11.0 %collective-permute-start.10 = (bf16[128,1024]{1,0:T(8,128)(2,1)S(1)}, bf16[128,1024]{1,0:T(8,128)(2,1)S(1)}, u32[]{:S(2)}, u32[]{:S(2)}) collective-permute-start(bf16[128,1024]{1,0:T(8,128)(2,1)S(1)} %get-tuple-element.34), channel_id=1, source_target_pairs={{0,24},{8,16},{16,8},{24,0},{1,25},{9,17},{17,9},{25,1},{2,26},{10... | collective-permute-start | bytes 786440 | tf_op jit(solution)/shard_map/ppermute | solution.py:510
  45.9 20.3 %collective-permute-start.2 = (bf16[264,1024]{1,0:T(8,128)(2,1)S(1)}, bf16[264,1024]{1,0:T(8,128)(2,1)S(1)}, u32[]{:S(2)}, u32[]{:S(2)}) collective-permute-start(bf16[264,1024]{1,0:T(8,128)(2,1)S(1)} %collective-permute-done.1.refs_5_.refs_0_), channel_id=1, source_target_pairs={{4,6},{5,7},{12,14},{13,15},{20,22},{21,23},{28,30},{29,31}} | collective-permute-start | bytes 1622024 | tf_op jit(solution)/shard_map/ppermute | solution.py:487
  46.6 19.6 %collective-permute-start.5 = (bf16[264,1024]{1,0:T(8,128)(2,1)S(1)}, bf16[264,1024]{1,0:T(8,128)(2,1)S(1)}, u32[]{:S(2)}, u32[]{:S(2)}) collective-permute-start(bf16[264,1024]{1,0:T(8,128)(2,1)S(1)} %collective-permute-done.4.refs_6_.refs_1_), channel_id=1, source_target_pairs={{2,0},{3,1},{10,8},{11,9},{18,16},{19,17},{26,24},{27,25}} | collective-permute-start | bytes 1622024 | tf_op jit(solution)/shard_map/ppermute | solution.py:487
  47.9 7.6 %copy-start.6 = (bf16[2,16,128,128]{3,2,1,0:T(8,128)(2,1)S(1)}, bf16[2,16,128,128]{3,2,1,0:T(8,128)(2,1)}, u32[]{:S(2)}) copy-start(bf16[2,16,128,128]{3,2,1,0:T(8,128)(2,1)} %refs_1_.1) | copy-start | bytes 3145732
  48.0 7.6 %copy-start.7 = (s32[2,16]{1,0:T(2,128)S(1)}, s32[2,16]{1,0:T(2,128)}, u32[]{:S(2)}) copy-start(s32[2,16]{1,0:T(2,128)} %nb_own.1) | copy-start | bytes 388
  66.2 12.0 %copy-start.5 = (bf16[1024,1024]{1,0:T(8,128)(2,1)S(1)}, bf16[1024,1024]{1,0:T(8,128)(2,1)}, u32[]{:S(2)}) copy-start(bf16[1024,1024]{1,0:T(8,128)(2,1)} %w.1) | copy-start | bytes 6291460
  73.9 5.4 %collective-permute-start.13 = (f32[1088,256]{1,0:T(8,128)S(1)}, f32[1088,256]{1,0:T(8,128)S(1)}, u32[]{:S(2)}, u32[]{:S(2)}) collective-permute-start(f32[1088,256]{1,0:T(8,128)S(1)} %get-tuple-element.56), channel_id=1, source_target_pairs={{0,1},{1,0},{2,3},{3,2},{4,5},{5,4},{6,7},{7,6},{8,9},{9,8},{10,11... | collective-permute-start | bytes 3342344 | tf_op jit(solution)/shard_map/ppermute | solution.py:538
  74.0 4.3 %copy-start.1 = (bf16[256,1024]{1,0:T(8,128)(2,1)S(1)}, bf16[256,1024]{1,0:T(8,128)(2,1)}, u32[]{:S(2)}) copy-start(bf16[256,1024]{1,0:T(8,128)(2,1)} %x.7) | copy-start | bytes 1572868
  74.0 5.3 %copy-start.3 = (bf16[2048,1024]{1,0:T(8,128)(2,1)S(1)}, bf16[2048,1024]{1,0:T(8,128)(2,1)}, u32[]{:S(2)}) copy-start(bf16[2048,1024]{1,0:T(8,128)(2,1)} %w_down.1) | copy-start | bytes 12582916
  74.0 5.3 %copy-start.4 = (bf16[1024,1024]{1,0:T(8,128)(2,1)S(1)}, bf16[1024,1024]{1,0:T(8,128)(2,1)}, u32[]{:S(2)}) copy-start(bf16[1024,1024]{1,0:T(8,128)(2,1)} %w_out.1) | copy-start | bytes 6291460
  75.4 2.8 %collective-permute-start.11 = (f32[256,1024]{1,0:T(8,128)S(1)}, f32[256,1024]{1,0:T(8,128)S(1)}, u32[]{:S(2)}, u32[]{:S(2)}) collective-permute-start(f32[256,1024]{1,0:T(8,128)S(1)} %get-tuple-element.39), channel_id=1, source_target_pairs={{0,1},{1,0},{2,3},{3,2},{4,5},{5,4},{6,7},{7,6},{8,9},{9,8},{10,11... | collective-permute-start | bytes 3145736 | tf_op jit(solution)/shard_map/ppermute | solution.py:529
  78.2 2.2 %copy-start.2 = (bf16[1024,2048]{1,0:T(8,128)(2,1)S(1)}, bf16[1024,2048]{1,0:T(8,128)(2,1)}, u32[]{:S(2)}) copy-start(bf16[1024,2048]{1,0:T(8,128)(2,1)} %w_up.1) | copy-start | bytes 12582916

commit v3 on v2

--- a/solution.py
+++ b/solution.py
@@ -7,6 +7,7 @@
 from jax.experimental import pallas as pl
 from jax.experimental.pallas import tpu as pltpu
 from jax.sharding import PartitionSpec as P
+
 
 H = 32
 LOW = -1e30
@@ -153,6 +154,7 @@
 F32 = jnp.float32
 SMEM = pl.BlockSpec(memory_space=pltpu.SMEM)
 VMEM = pl.BlockSpec(memory_space=pltpu.VMEM)
+HBM = pl.BlockSpec(memory_space=pltpu.HBM)
 GROUP_COLS = 256
 DEPTH = 3
 
@@ -165,21 +167,30 @@
     return pltpu.CompilerParams(vmem_limit_bytes=mib << 20)
 
 
-def sources_of(step, me, peers):
-    left, right = me - CORES * step, me + CORES * step
-    return left, right, left >= 0, right < peers
-
-
-def attend_kernel(mode, step, rows, block, peers, where, live, *refs):
-    first, last, both = mode
+def source_of(step, me, peers):
+    chip = me // CORES
+    end = (chip == 0) | (chip == peers // CORES - 1)
+    if step == 0:
+        return me, end
+    if step == 1:
+        return me ^ CORES, end
+    near, across = 2 * CORES, 3 * CORES
+    if step == 2:
+        return me ^ jnp.where(end, near, across), end
+    return me ^ jnp.where(end, across, near), end
+
+
+def attend_kernel(mode, step, count, rows, block, peers, where, live, *refs):
+    first, last = mode
     if first:
-        own, mate_piece, w, qt_ref, max_ref, sum_ref, acc_ref, score_ref, prob_ref = refs
+        own, mate_piece, w_all, qt_ref, w, max_ref, sum_ref, acc_ref, score_ref, prob_ref, wq_ref, sems = refs
     else:
-        left_piece, right_piece, w, qt_ref, max_in, sum_in, acc_in, *refs = refs
+        arrived, refs = refs[:count], refs[count:]
+        qt_ref, w, max_in, sum_in, acc_in, *refs = refs
         if last:
             send_ref, *refs = refs
         max_ref, sum_ref, acc_ref, score_ref, prob_ref = refs
-    width = w.shape[0]
+    width = qt_ref.shape[0]
     head = width // H
     heads_step = GROUP_COLS // head
     per_dev = rows // block
@@ -187,22 +198,33 @@
     scale = math.log2(math.e) / math.sqrt(head)
     me = where[0]
     mate = me + 1 - 2 * (me % CORES)
-    if first:
-        source, needed = me, None
-    else:
-        left, right, has_left, has_right = sources_of(step, me, peers)
-        if both:
-            source, needed = right, has_left & has_right
-        else:
-            source, needed = jnp.where(has_left, left, right), has_left | has_right
+    source, end = source_of(step, me, peers)
+
+    def loads(g):
+        copies = []
+        for part in range(3):
+            at = part * width + g * GROUP_COLS
+            target = wq_ref if part == 0 else w
+            to = at if part == 0 else at - width
+            copies.append(
+                pltpu.make_async_copy(
+                    w_all.at[:, pl.ds(pl.multiple_of(at, GROUP_COLS), GROUP_COLS)],
+                    target.at[:, pl.ds(pl.multiple_of(to, GROUP_COLS), GROUP_COLS)],
+                    sems.at[g, part],
+                )
+            )
+        return copies
 
     def run():
         if first:
+            for g in range(width // GROUP_COLS):
+                for load in loads(g):
+                    load.start()
             x = own[0:rows, :]
-        elif both:
-            x = right_piece[0:rows, :]
+        elif count == 1:
+            x = arrived[0][0:rows, :]
         else:
-            x = jnp.where(has_left, left_piece[0:rows, :], right_piece[0:rows, :])
+            x = jnp.where(end, arrived[1][0:rows, :], arrived[0][0:rows, :])
         query_blocks = [dev * per_dev + b for dev in (me, mate) for b in range(per_dev)]
         alive = []
         for j in range(per_dev):
@@ -219,7 +241,9 @@
                 return w[:, pl.ds(pl.multiple_of(part * width + cols, GROUP_COLS), GROUP_COLS)]
 
             if first:
-                wq = weight(0)
+                for load in loads(g):
+                    load.wait()
+                wq = wq_ref[:, pl.ds(cols, GROUP_COLS)]
                 qt_ref[pl.ds(cols, GROUP_COLS), 0:rows] = mm(x, wq).astype(BF).T
                 mate_q = mm(mate_piece[0:rows, :], wq).astype(BF)
                 qt_ref[pl.ds(cols, GROUP_COLS), rows:queries] = mate_q.T
@@ -228,8 +252,8 @@
             else:
                 tops = max_in[pl.ds(heads_at, heads_step), :]
                 sums = sum_in[pl.ds(heads_at, heads_step), :]
-            keys = mm(x, weight(1)).astype(BF)
-            values = mm(x, weight(2)).astype(BF).T
+            keys = mm(x, weight(0)).astype(BF)
+            values = mm(x, weight(1)).astype(BF).T
             new_tops, new_sums = [], []
 
             def score(h):
@@ -274,17 +298,7 @@
 
         lax.fori_loop(0, width // GROUP_COLS, group, 0)
 
-    if needed is None:
-        run()
-    else:
-        pl.when(needed)(run)
-
-        @pl.when(jnp.logical_not(needed))
-        def _():
-            max_ref[...] = max_in[...]
-            sum_ref[...] = sum_in[...]
-            acc_ref[...] = acc_in[...]
-
+    run()
     if last:
         send_ref[0:width, :] = acc_ref[:, rows:queries]
         send_ref[width : width + H, :] = max_ref[:, rows:queries]
@@ -292,41 +306,49 @@
 
 
 def attend_call(mode, step, pieces, state, where, live, w_qkv, rows, block, peers):
-    first, last, both = mode
+    first, last = mode
     width = w_qkv.shape[0]
     queries = CORES * rows
     stats = jax.ShapeDtypeStruct((H, queries), F32)
     out_shape = [stats, stats, jax.ShapeDtypeStruct((width, queries), F32)]
-    args = [where, live, *pieces, w_qkv]
+    scratch = [pltpu.VMEM((DEPTH, rows, queries), F32), pltpu.VMEM((2, rows, queries), BF)]
+    args = [where, live, *pieces]
+    in_specs = [SMEM] * 2 + [VMEM] * len(pieces)
     aliases = {}
     if first:
-        out_shape = [jax.ShapeDtypeStruct((width, queries), BF), *out_shape]
+        args.append(w_qkv)
+        in_specs.append(HBM)
+        out_shape = [
+            jax.ShapeDtypeStruct((width, queries), BF), jax.ShapeDtypeStruct((width, 2 * width), BF), *out_shape
+        ]
+        scratch += [pltpu.VMEM((width, width), BF), pltpu.SemaphoreType.DMA((width // GROUP_COLS, 3))]
     else:
         args += state
+        in_specs += [VMEM] * len(state)
         extra = 1 if last else 0
-        aliases = {6: extra, 7: extra + 1, 8: extra + 2}
+        at = len(pieces) + 4
+        aliases = {at: extra, at + 1: extra + 1, at + 2: extra + 2}
     if last:
         out_shape = [jax.ShapeDtypeStruct((width + 2 * H, rows), F32), *out_shape]
     out = pl.pallas_call(
-        functools.partial(attend_kernel, mode, step, rows, block, peers),
-        in_specs=[SMEM, SMEM] + [VMEM] * (len(args) - 2),
+        functools.partial(attend_kernel, mode, step, len(pieces), rows, block, peers),
+        in_specs=in_specs,
         out_specs=[VMEM] * len(out_shape),
         out_shape=out_shape,
-        scratch_shapes=[pltpu.VMEM((DEPTH, rows, queries), F32), pltpu.VMEM((2, rows, queries), BF)],
+        scratch_shapes=scratch,
         input_output_aliases=aliases,
-        compiler_params=grant(24),
+        compiler_params=grant(42 if first else 24),
         cost_estimate=pl.CostEstimate(
             flops=4 * rows * width * width + 16 * rows * queries * width,
             transcendentals=H * rows * queries,
             bytes_accessed=4 << 20,
         ),
-        name=f"attend{step}{'b' if both else ''}",
     )(*args)
     if first:
         return list(out)
     if last:
         return out
-    return [state[0], *out]
+    return [*state[:2], *out]
 
 
 def pick_row(tile, at):
@@ -346,27 +368,25 @@
     y_mate[...] += both[rows:, :]
 
 
-def add_arrived(step, where, left_piece, right_piece, spread, y_own, y_mate, rows, slot, block, peers):
+def add_arrived(step, where, arrived, spread, y_own, y_mate, rows, slot, block, peers):
     me = where[0]
     mate = me + 1 - 2 * (me % CORES)
-    left, right, has_left, has_right = sources_of(step, me, peers)
-
-    def add(source, piece):
-        at = rows // block + source * (slot // block)
-        add_piece(
-            piece[rows:, 0:slot], piece[0:rows, :], (me, mate), lambda dest, j: spread[dest, at + j],
-            y_own, y_mate, rows, slot, block,
-        )
-
-    pl.when(has_left)(lambda: add(left, left_piece))
-    pl.when(has_right)(lambda: add(right, right_piece))
+    source, end = source_of(step, me, peers)
+    at = rows // block + source * (slot // block)
+    if len(arrived) == 1:
+        lists, x = arrived[0][rows:, 0:slot], arrived[0][0:rows, :]
+    else:
+        lists = jnp.where(end, arrived[1][rows:, 0:slot], arrived[0][rows:, 0:slot])
+        x = jnp.where(end, arrived[1][0:rows, :], arrived[0][0:rows, :])
+    add_piece(lists, x, (me, mate), lambda dest, j: spread[dest, at + j], y_own, y_mate, rows, slot, block)
 
 
 def gather_kernel(steps, far_count, rows, slot, far_slot, block, peers, where, nb_own, nb_mate, *refs):
     own, adj_own, adj_mate, *refs = refs
-    arrived = refs[: 2 * steps]
-    far = refs[2 * steps : 2 * steps + far_count]
-    y_own, y_mate, spread = refs[2 * steps + far_count :]
+    count = sum(steps)
+    arrived = refs[:count]
+    far = refs[count : count + far_count]
+    y_own, y_mate, spread = refs[count + far_count :]
     me, cluster = where[0], where[1]
     mate = me + 1 - 2 * (me % CORES)
     spread[...] = jnp.zeros(spread.shape, BF)
@@ -391,16 +411,18 @@
         for j in range(far_slot // block):
             tiles_far.append(spread[0, first_far + source * (far_slot // block) + j])
     y_own[...] += mm(jnp.concatenate(tiles_far, axis=1), jnp.concatenate([r[...] for r in far], axis=0))
-    for t in range(steps):
-        add_arrived(
-            t + 1, where, arrived[2 * t], arrived[2 * t + 1], spread, y_own, y_mate, rows, slot, block, peers
-        )
-
-
-def gather_more_kernel(step, rows, slot, block, peers, where, left, right, spread, own_in, mate_in, y_own, y_mate):
+    at = 0
+    for step, width in enumerate(steps):
+        add_arrived(step + 1, where, arrived[at : at + width], spread, y_own, y_mate, rows, slot, block, peers)
+        at += width
+
+
+def gather_more_kernel(step, count, rows, slot, block, peers, where, *refs):
+    arrived = refs[:count]
+    spread, own_in, mate_in, y_own, y_mate = refs[count:]
     y_own[...] = own_in[...]
     y_mate[...] = mate_in[...]
-    add_arrived(step, where, left, right, spread, y_own, y_mate, rows, slot, block, peers)
+    add_arrived(step, where, arrived, spread, y_own, y_mate, rows, slot, block, peers)
 
 
 def far_source(step, cluster, clusters):
@@ -415,13 +437,24 @@
     return (cluster + step) % clusters
 
 
-def pick_kernel(clusters, where, lists, x, *outs):
+def pack_kernel(lists, x, out, sem):
     rows = x.shape[0]
+    load = pltpu.make_async_copy(x, out.at[0:rows, :], sem)
+    load.start()
+    peers, slot = lists.shape[1:]
+    numbers = lists[0].astype(F32).astype(BF)
+    if slot < out.shape[1]:
+        numbers = jnp.concatenate([numbers, jnp.zeros((peers, out.shape[1] - slot), BF)], axis=1)
+    out[rows : rows + peers, :] = numbers
+    load.wait()
+
+
+def pick_kernel(clusters, rows, where, lists, x, *outs):
     numbers = lax.broadcasted_iota(jnp.int32, (rows, lists.shape[-1]), 0)
     for step, out in enumerate(outs):
         row = lists[0, pl.ds(far_target(step, where[1], clusters), 1), :]
         chosen = jnp.where(numbers == row, 1.0, 0.0).astype(BF)
-        out[...] = mm(chosen, x[...], ((0,), (0,))).astype(BF)
+        out[...] = mm(chosen, x[0:rows, :], ((0,), (0,))).astype(BF)
 
 
 def local_kernel(x, y_own, y_got, w, out):
@@ -430,7 +463,9 @@
     out[...] = layer_norm(x[...].astype(F32) + agg)
 
 
-def tail_kernel(rows, x, local, top, total, acc, got, w_out, w_up, w_down, out):
+def tail_kernel(rows, x, local, top, total, acc, got, w_out, w_up_all, w_down, out, w_up, sem):
+    load = pltpu.make_async_copy(w_up_all, w_up, sem)
+    load.start()
     heads = top.shape[0]
     width = acc.shape[0]
     head = width // heads
@@ -449,6 +484,7 @@
     attended = jnp.concatenate(pieces, axis=0)
     projected = mm(attended, w_out[...], ((0,), (0,)))
     summed = local[...] + layer_norm(x[...].astype(F32) + projected)
+    load.wait()
     activated = jax.nn.gelu(mm(summed.astype(BF), w_up[...])).astype(BF)
     out[...] = layer_norm(summed + mm(activated, w_down[...])).astype(BF)
 
@@ -478,23 +514,28 @@
     where = jnp.stack([lax.axis_index("dev"), cluster]).astype(jnp.int32)
     swap = [(CORES * c + k, CORES * c + 1 - k) for c in range(chips) for k in range(CORES)]
 
-    def hop(value, step, far):
-        pairs = []
-        for c in range(chips):
-            to = c + step
-            if 0 <= to < chips and 0 <= to - step * far < chips:
-                pairs += [(CORES * c + k, CORES * to + k) for k in range(CORES)]
-        return lax.ppermute(value, "dev", pairs)
-
-    lists = jnp.pad(inner_rows[0].astype(BF), ((0, 0), (0, width - slot)))
-    piece = jnp.concatenate([node_feats, lists], axis=0)
-    left, right = hop(piece, 1, 1), hop(piece, -1, 1)
+    def cross(value, pairs):
+        lanes = [(CORES * a + k, CORES * b + k) for a, b in pairs for k in range(CORES)]
+        return lax.ppermute(value, "dev", lanes)
+
+    piece = pl.pallas_call(
+        pack_kernel,
+        in_specs=[VMEM, HBM],
+        out_specs=VMEM,
+        out_shape=jax.ShapeDtypeStruct((rows + peers, width), BF),
+        scratch_shapes=[pltpu.SemaphoreType.DMA],
+        compiler_params=grant(4),
+        name="pack",
+    )(inner_rows, node_feats)
+    outer, middle = [(0, 1), (1, 0), (2, 3), (3, 2)], [(1, 2), (2, 1)]
+    outward = [(1, 0), (2, 3)]
+    near, mid = cross(piece, outer), cross(piece, middle)
     mate_piece = lax.ppermute(piece, "dev", swap)
     mate_adj = lax.ppermute(adj_tiles, "dev", swap)
     mate_nb = lax.ppermute(neighbor_blocks, "dev", swap)
 
     picked = pl.pallas_call(
-        functools.partial(pick_kernel, clusters),
+        functools.partial(pick_kernel, clusters, rows),
         in_specs=[SMEM, VMEM, VMEM],
         out_specs=[VMEM] * clusters,
         out_shape=[jax.ShapeDtypeStruct((far_slot, width), BF)] * clusters,
@@ -503,7 +544,7 @@
             flops=2 * rows * clusters * far_slot * width, transcendentals=0, bytes_accessed=1 << 20
         ),
         name="pick",
-    )(where, outer_rows, node_feats)
+    )(where, outer_rows, piece)
     far = [picked[0]]
     for s in range(1, clusters):
         pairs = [(c, far_target(s, c, clusters)) for c in range(clusters)]
@@ -513,28 +554,26 @@
     live = jnp.sum(jnp.where(slots < key_counts[:, None], jnp.left_shift(1, key_blocks), 0), axis=1)
     live = live.astype(jnp.int32)
 
-    attend = lambda mode, step, pieces, state: attend_call(
-        mode, step, pieces, state, where, live, w_qkv, rows, block, peers
-    )
-    state = attend((True, False, False), 0, [piece, mate_piece], None)
-    arrived = []
-    for step in range(1, chips):
-        pair = [left, right]
-        final = step + 1 == chips
-        if final:
-            sums = gather_call(
-                where, neighbor_blocks, mate_nb, piece, adj_tiles, mate_adj, arrived, far, rows, slot, far_slot, block, peers
-            )
-            sums = gather_more_call(step, where, pair, sums, rows, slot, block, peers)
-            y_got = lax.ppermute(sums[1], "dev", swap)
-        else:
-            left, right = hop(left, 1, step + 1), hop(right, -1, step + 1)
-        two = 2 * step <= chips - 1
-        state = attend((False, final and not two, False), step, pair, state)
-        if two:
-            state = attend((False, final, True), step, pair, state)
-        arrived += pair
-    send, top, total, acc = state
+    attend = lambda step, pieces, state, last=False: attend_call(
+        (step == 0, last), step, pieces, state, where, live, w_qkv, rows, block, peers
+    )
+    state = attend(0, [piece, mate_piece], None)
+    near, mid, state[2] = lax.optimization_barrier((near, mid, state[2]))
+    to_end = cross(mid, outward)
+    to_mid = cross(near, middle)
+    state = attend(1, [near], state)
+    to_mid, to_end, state[2] = lax.optimization_barrier((to_mid, to_end, state[2]))
+    across = cross(to_mid, outward)
+    state = attend(2, [mid, to_end], state)
+    arrived = [near, mid, to_end]
+    sums = gather_call(
+        where, neighbor_blocks, mate_nb, piece, adj_tiles, mate_adj, arrived, (1, 2), far,
+        rows, slot, far_slot, block, peers,
+    )
+    sums = gather_more_call(3, where, [to_mid, across], sums, rows, slot, block, peers)
+    y_send, state[2] = lax.optimization_barrier((sums[1], state[2]))
+    y_got = lax.ppermute(y_send, "dev", swap)
+    send, top, total, acc = attend(3, [to_mid, across], state, True)
     got = lax.ppermute(send, "dev", swap)
     local = pl.pallas_call(
         local_kernel,
@@ -547,9 +586,10 @@
     )(node_feats, sums[0], y_got, w_gcn)
     return pl.pallas_call(
         functools.partial(tail_kernel, rows),
-        in_specs=[VMEM] * 9,
+        in_specs=[VMEM] * 7 + [HBM, VMEM],
         out_specs=VMEM,
         out_shape=jax.ShapeDtypeStruct((rows, width), BF),
+        scratch_shapes=[pltpu.VMEM(w_up.shape, BF), pltpu.SemaphoreType.DMA],
         compiler_params=grant(32),
         cost_estimate=pl.CostEstimate(
             flops=2 * rows * width * (width + 2 * w_up.shape[1]), transcendentals=0, bytes_accessed=12 << 20
@@ -559,13 +599,12 @@
 
 
 def gather_call(
-    where, nb_own, nb_mate, own, adj_own, adj_mate, arrived, far, rows, slot, far_slot, block, peers
+    where, nb_own, nb_mate, own, adj_own, adj_mate, arrived, steps, far, rows, slot, far_slot, block, peers
 ):
     width = own.shape[1]
     table_blocks = (rows + peers * slot + len(far) * far_slot) // block
     y = jax.ShapeDtypeStruct((rows, width), F32)
     spread = jax.ShapeDtypeStruct((CORES, table_blocks, rows, block), BF)
-    steps = len(arrived) // 2
     return pl.pallas_call(
         functools.partial(gather_kernel, steps, len(far), rows, slot, far_slot, block, peers),
         in_specs=[SMEM] * 3 + [VMEM] * (3 + len(arrived) + len(far)),
@@ -573,7 +612,7 @@
         out_shape=[y, y, spread],
         compiler_params=grant(24),
         cost_estimate=pl.CostEstimate(
-            flops=4 * rows * rows * width * (2 + steps), transcendentals=0, bytes_accessed=8 << 20
+            flops=4 * rows * rows * width * (2 + len(steps)), transcendentals=0, bytes_accessed=8 << 20
         ),
         name="gather",
     )(where, nb_own, nb_mate, own, adj_own, adj_mate, *arrived, *far)
@@ -582,11 +621,11 @@
 def gather_more_call(step, where, pair, sums, rows, slot, block, peers):
     y_own, y_mate, spread = sums
     return pl.pallas_call(
-        functools.partial(gather_more_kernel, step, rows, slot, block, peers),
-        in_specs=[SMEM] + [VMEM] * 5,
+        functools.partial(gather_more_kernel, step, len(pair), rows, slot, block, peers),
+        in_specs=[SMEM] + [VMEM] * (len(pair) + 3),
         out_specs=[VMEM] * 2,
         out_shape=[jax.ShapeDtypeStruct(y_own.shape, F32)] * 2,
-        input_output_aliases={4: 0, 5: 1},
+        input_output_aliases={2 + len(pair): 0, 3 + len(pair): 1},
         compiler_params=grant(16),
         cost_estimate=pl.CostEstimate(
             flops=4 * rows * rows * y_own.shape[1], transcendentals=0, bytes_accessed=4 << 20
@@ -599,7 +638,7 @@
     inner, feats, tiles = args[4], args[0], args[2]
     whole_slots = inner.shape[-1] == feats.shape[0] and feats.shape[0] <= 256
     whole_slots = whole_slots and args[8].shape[0] <= 31
-    if whole_slots and lax.axis_size("dev") % CORES == 0 and inner.shape[-1] % tiles.shape[-1] == 0:
+    if whole_slots and lax.axis_size("dev") == 4 * CORES and inner.shape[-1] % tiles.shape[-1] == 0:
         return line_plan(*args)
     return gathered_plan(*args)
 
@@ -619,6 +658,4 @@
         P(),
         P(),
     )
-    return jax.shard_map(
-        per_device, mesh=mesh, in_specs=placed, out_specs=P(("group", "dev"), None), check_vma=False
-    )
+    return jax.shard_map(per_device, mesh=mesh, in_specs=placed, out_specs=P(("group", "dev"), None), check_vma=False)

time: 85.4 us -> 83.2 us (0.974)
  waiting for transfers between devices: 17.5 us -> 23.5 us
  starting transfers between devices: 16 us -> 11.7 us
  local copies, waits for them, and re-layouts: 5.71 us -> 2.91 us
  other arithmetic: 2.7 us -> 0.95 us
    ppermute x7 -> x6, waiting for transfers between devices: 10.8 us -> 22.3 us  [the longest x5 18.6 us: cross(): return lax.ppermute(value, 'dev', lanes)]
    ppermute x3, waiting for transfers between devices: 6.7 us -> 0.01 us  [line_plan(): far.append(lax.ppermute(picked[s], 'group', pairs))]
    ppermute x7 -> x6, starting transfers between devices: 10.8 us -> 7.26 us  [the longest x5 6.76 us: cross(): return lax.ppermute(value, 'dev', lanes)]
    unnamed x22 -> x20, local copies, waits for them, and re-layouts: 5.71 us -> 2.91 us
    ppermute x1, waiting for transfers between devices: 0.01 us -> 1.16 us  [line_plan(): mate_nb = lax.ppermute(neighbor_blocks, 'dev', swap)]
    concatenate x1 -> x0, other arithmetic: 1.08 us -> none  [line_plan(): piece = jnp.concatenate([node_feats, lists], axis=0)]
    ppermute x3, starting transfers between devices: 4.51 us -> 3.55 us  [line_plan(): far.append(lax.ppermute(picked[s], 'group', pairs))]
    pallas_call x8, Pallas kernels: 38.5 us -> 39.5 us  [the longest x4 32.2 us: attend_call(): pl.pallas_call(functools.partial(attend_kernel, mode, step, len(pieces),...]
  transfers between devices with their start and end apart: 14 -> 13, of which waited for: 4 -> 5; matrix products, arithmetic and copies ran while one was open for 1% -> 1% of each run, Pallas kernels for 36% -> 36%
where the time goes in v3:
time: 83.2 us; the launch traced here: 82.8 us
  Pallas kernels  43.4 us (52%)
  waiting for transfers between devices  23.5 us (28%)
  starting transfers between devices  11.7 us (14%)
  local copies, waits for them, and re-layouts  2.91 us (3%)
  other arithmetic  0.95 us (1%)
    pallas_call x4, Pallas kernels, attend_call(): pl.pallas_call(functools.partial(attend_kernel, mode, step, len(pieces),...  32.2 us
    ppermute x5, waiting for transfers between devices, cross(): return lax.ppermute(value, 'dev', lanes)  18.6 us
    ppermute x5, starting transfers between devices, cross(): return lax.ppermute(value, 'dev', lanes)  6.76 us
    pallas_call x1, Pallas kernels, line_plan(): pl.pallas_call(functools.partial(tail_kernel, rows), in_specs=[VMEM] * 7...  4.94 us
    ppermute x1, waiting for transfers between devices, line_plan(): y_got = lax.ppermute(y_send, 'dev', swap)  3.74 us
    ppermute x3, starting transfers between devices, line_plan(): far.append(lax.ppermute(picked[s], 'group', pairs))  3.55 us
    unnamed x20, local copies, waits for them, and re-layouts  2.91 us
    pallas_call x1, Pallas kernels, gather_call(): pl.pallas_call(functools.partial(gather_kernel, steps, len(far), rows, sl...  2.88 us
  transfers between devices with their start and end apart: 13, of which 5 were waited for; matrix products, arithmetic and copies ran while one was open for 1% of the time, Pallas kernels for 36%

profile of v3, /device:TPU:0, one launch (start us, length us, event | category | flops | bytes accessed | tf_op | source)
XLA Modules:
  0.0 82.8 jit_solution(10394766971744150801)
XLA Ops:
  0.0 0.0 copy-start
  0.0 1.0 %copy-done = bf16[256,1024]{1,0:T(8,128)(2,1)S(1)} copy-done((bf16[256,1024]{1,0:T(8,128)(2,1)S(1)}, bf16[256,1024]{1,0:T(8,128)(2,1)}, u32[]{:S(2)}) %copy-start) | copy-done | bytes 524312
  1.0 0.0 copy-start.7
  1.0 0.7 copy-done.7
  1.8 0.6 collective-permute-start.2
  2.4 2.6 %collective-permute-start = (bf16[264,1024]{1,0:T(8,128)(2,1)S(1)}, bf16[264,1024]{1,0:T(8,128)(2,1)S(1)}, u32[]{:S(2)}, u32[]{:S(2)}) collective-permute-start(bf16[264,1024]{1,0:T(8,128)(2,1)S(1)} %pack.1.refs_0_.x), channel_id=1, source_target_pairs={{0,2},{1,3},{2,0},{3,1},{4,6},{5,7},{6,4},{7,5},{8,10},{9,11},{10,... | collective-permute-start | bytes 1622024 | tf_op jit(solution)/shard_map/ppermute | solution.py:519
  5.0 0.7 collective-permute-start.1
  5.7 0.2 collective-permute-start.7
  5.9 0.1 pad_add_fusion.where
  6.0 0.9 %select_reduce_fusion.live = s32[16]{0:T(128)S(1)} fusion(s32[16,16]{1,0:T(8,128)} %param.19, s32[16]{0:T(128)} %param.20), kind=kLoop, calls=%fused_computation | loop fusion | flops 1008 | bytes 1152 | tf_op jit(solution)/shard_map/reduce_sum | solution.py:554
  6.9 0.0 copy-start.9
  6.9 0.0 collective-permute-done.2.refs_1_
  6.9 9.8 %shard_map.118 = (bf16[1024,512]{1,0:T(8,128)(2,1)S(1)}, bf16[1024,2048]{1,0:T(8,128)(2,1)S(1)}, f32[32,512]{1,0:T(8,128)S(1)}, f32[32,512]{1,0:T(8,128)S(1)}, f32[1024,512]{1,0:T(8,128)S(1)}) custom-call(s32[2]{0:T(128)S(1)} %pad_add_fusion.where, s32[16]{0:T(128)S(1)} %select_reduce_fusion.live, bf16[264,1024]{1,0:T(8,128)(2,1)S(1)} %pack.1.refs_0_.x, ...), custom_call_target="tpu_custom_call" | custom-call | flops 3221225472 | bytes 4194304 | tf_op jit(solution)/shard_map/pallas_call | solution.py:333
  16.7 1.2 %collective-permute-done.refs_0_.refs_3_ = bf16[264,1024]{1,0:T(8,128)(2,1)S(1)} collective-permute-done((bf16[264,1024]{1,0:T(8,128)(2,1)S(1)}, bf16[264,1024]{1,0:T(8,128)(2,1)S(1)}, u32[]{:S(2)}, u32[]{:S(2)}) %collective-permute-start) | collective-permute-done | bytes 540704 | tf_op jit(solution)/shard_map/ppermute | solution.py:519
  17.9 0.0 collective-permute-done.1.refs_4_.refs_0_
  17.9 0.7 collective-permute-start.3
  18.6 1.3 %collective-permute-start.4 = (bf16[264,1024]{1,0:T(8,128)(2,1)S(1)}, bf16[264,1024]{1,0:T(8,128)(2,1)S(1)}, u32[]{:S(2)}, u32[]{:S(2)}) collective-permute-start(bf16[264,1024]{1,0:T(8,128)(2,1)S(1)} %collective-permute-done.1.refs_4_.refs_0_), channel_id=1, source_target_pairs={{2,0},{3,1},{4,6},{5,7},{10,8},{11,9},{12,14},{13,15},{18,16},{19,... | collective-permute-start | bytes 1622024 | tf_op jit(solution)/shard_map/ppermute | solution.py:519
  19.9 0.0 copy-done.9
  19.9 1.0 %pick.1 = (bf16[128,1024]{1,0:T(8,128)(2,1)S(1)}, bf16[128,1024]{1,0:T(8,128)(2,1)S(1)}, bf16[128,1024]{1,0:T(8,128)(2,1)S(1)}, bf16[128,1024]{1,0:T(8,128)(2,1)S(1)}) custom-call(s32[2]{0:T(128)S(1)} %pad_add_fusion.where, s32[1,4,128]{2,1,0:T(4,128)S(1)} %copy-done.9, bf16[264,1024]{1,0:T(8,128)(2,1)S(1)} %pack.1.refs_0_.x), custom_call_target="tpu_custom_call" | custom-call | flops 268435456 | bytes 1048576 | tf_op jit(solution)/shard_map/pick/pallas_call | solution.py:537
  20.9 2.7 %collective-permute-start.10 = (bf16[128,1024]{1,0:T(8,128)(2,1)S(1)}, bf16[128,1024]{1,0:T(8,128)(2,1)S(1)}, u32[]{:S(2)}, u32[]{:S(2)}) collective-permute-start(bf16[128,1024]{1,0:T(8,128)(2,1)S(1)} %get-tuple-element.51), channel_id=1, source_target_pairs={{0,24},{8,16},{16,8},{24,0},{1,25},{9,17},{17,9},{25,1},{2,26},{10... | collective-permute-start | bytes 786440 | tf_op jit(solution)/shard_map/ppermute | solution.py:551
  23.6 0.5 collective-permute-start.8
  24.1 0.0 collective-permute-done.3.refs_0_
  24.1 0.3 collective-permute-start.9
  24.4 0.0 copy-start.8
  24.5 0.0 copy-start.6
  24.5 7.4 %shard_map.119 = (f32[32,512]{1,0:T(8,128)S(1)}, f32[32,512]{1,0:T(8,128)S(1)}, f32[1024,512]{1,0:T(8,128)S(1)}) custom-call(s32[2]{0:T(128)S(1)} %pad_add_fusion.where, s32[16]{0:T(128)S(1)} %select_reduce_fusion.live, bf16[264,1024]{1,0:T(8,128)(2,1)S(1)} %collective-permute-done.refs_0_.refs_3_, ...), custom_call_target="tpu_custom_call", output_to_operand_aliasing={{0}: (5, {}), {1}: (6, {}), {2}: (7, {})} | custom-call | flops 3221225472 | bytes 4194304 | tf_op jit(solution)/shard_map/pallas_call | solution.py:333
  31.9 7.1 %collective-permute-done.4.refs_5_.refs_1_ = bf16[264,1024]{1,0:T(8,128)(2,1)S(1)} collective-permute-done((bf16[264,1024]{1,0:T(8,128)(2,1)S(1)}, bf16[264,1024]{1,0:T(8,128)(2,1)S(1)}, u32[]{:S(2)}, u32[]{:S(2)}) %collective-permute-start.4) | collective-permute-done | bytes 540704 | tf_op jit(solution)/shard_map/ppermute | solution.py:519
  39.0 0.0 copy-done.8
  39.0 0.0 collective-permute-start.6
  39.0 1.2 %collective-permute-done.6.nb_mate = s32[2,16]{1,0:T(2,128)S(1)} collective-permute-done((s32[2,16]{1,0:T(2,128)S(1)}, s32[2,16]{1,0:T(2,128)S(1)}, u32[]{:S(2)}, u32[]{:S(2)}) %collective-permute-start.6) | collective-permute-done | bytes 160 | tf_op jit(solution)/shard_map/ppermute | solution.py:535
  40.2 1.5 %collective-permute-start.5 = (bf16[264,1024]{1,0:T(8,128)(2,1)S(1)}, bf16[264,1024]{1,0:T(8,128)(2,1)S(1)}, u32[]{:S(2)}, u32[]{:S(2)}) collective-permute-start(bf16[264,1024]{1,0:T(8,128)(2,1)S(1)} %collective-permute-done.3.refs_0_), channel_id=1, source_target_pairs={{2,0},{3,1},{4,6},{5,7},{10,8},{11,9},{12,14},{13,15},{18,16},{19,... | collective-permute-start | bytes 1622024 | tf_op jit(solution)/shard_map/ppermute | solution.py:519
  41.6 0.0 collective-permute-done.10.refs_9_
  41.6 0.0 collective-permute-done.8.refs_7_
  41.6 0.0 collective-permute-done.9.refs_8_
  41.7 0.0 collective-permute-done.7.refs_2_
  41.7 0.0 copy-done.6
  41.7 2.9 %gather.1 = (f32[256,1024]{1,0:T(8,128)S(1)}, f32[256,1024]{1,0:T(8,128)S(1)}, bf16[2,22,256,128]{3,2,1,0:T(8,128)(2,1)S(1)}) custom-call(s32[2]{0:T(128)S(1)} %pad_add_fusion.where, s32[2,16]{1,0:T(2,128)S(1)} %copy-done.8, s32[2,16]{1,0:T(2,128)S(1)} %collective-permute-done.6.nb_mate, bf16[264,1024]{1,0:T(8,128)(2,1)S(1)} %pack.1.refs_0_.x, ...), custom_call_target="tpu_custom_call" | custom-call | flops 1073741824 | bytes 8388608 | tf_op jit(solution)/shard_map/gather/pallas_call | solution.py:608
  44.6 7.5 %shard_map.120 = (f32[32,512]{1,0:T(8,128)S(1)}, f32[32,512]{1,0:T(8,128)S(1)}, f32[1024,512]{1,0:T(8,128)S(1)}) custom-call(s32[2]{0:T(128)S(1)} %pad_add_fusion.where, s32[16]{0:T(128)S(1)} %select_reduce_fusion.live, bf16[264,1024]{1,0:T(8,128)(2,1)S(1)} %collective-permute-done.1.refs_4_.refs_0_, ...), custom_call_target="tpu_custom_call", output_to_operand_aliasing={{0}: (6, {}), {1}: (7, {}), {2}: (8, {})} | custom-call | flops 3221225472 | bytes 4194304 | tf_op jit(solution)/shard_map/pallas_call | solution.py:333
  52.0 10.3 %collective-permute-done.5.refs_1_ = bf16[264,1024]{1,0:T(8,128)(2,1)S(1)} collective-permute-done((bf16[264,1024]{1,0:T(8,128)(2,1)S(1)}, bf16[264,1024]{1,0:T(8,128)(2,1)S(1)}, u32[]{:S(2)}, u32[]{:S(2)}) %collective-permute-start.5) | collective-permute-done | bytes 540704 | tf_op jit(solution)/shard_map/ppermute | solution.py:519
  62.3 1.2 %gather_more.1 = (f32[256,1024]{1,0:T(8,128)S(1)}, f32[256,1024]{1,0:T(8,128)S(1)}) custom-call(s32[2]{0:T(128)S(1)} %pad_add_fusion.where, bf16[264,1024]{1,0:T(8,128)(2,1)S(1)} %collective-permute-done.3.refs_0_, bf16[264,1024]{1,0:T(8,128)(2,1)S(1)} %collective-permute-done.5.refs_1_, ...), custom_call_target="tpu_custom_call", output_to_operand_aliasing={{0}: (4, {}), {1}: (5, {})} | custom-call | flops 268435456 | bytes 4194304 | tf_op jit(solution)/shard_map/gather_more/pallas_call | solution.py:623
  63.6 0.0 copy-start.1
  63.6 0.0 copy-start.5
  63.6 0.0 copy-start.3
  63.6 0.0 copy-start.4
  63.6 7.6 %shard_map.121 = (f32[1088,256]{1,0:T(8,128)S(1)}, f32[32,512]{1,0:T(8,128)S(1)}, f32[32,512]{1,0:T(8,128)S(1)}, f32[1024,512]{1,0:T(8,128)S(1)}) custom-call(s32[2]{0:T(128)S(1)} %pad_add_fusion.where, s32[16]{0:T(128)S(1)} %select_reduce_fusion.live, ...), custom_call_target="tpu_custom_call", output_to_operand_aliasing={{1}: (6, {}), {2}: (7, {}), {3}: (8, {})} | custom-call | flops 3221225472 | bytes 4194304 | tf_op jit(solution)/shard_map/pallas_call | solution.py:333
  71.2 0.1 collective-permute-start.12
  71.3 0.5 collective-permute-start.11
  71.8 3.7 %collective-permute-done.11.y_got = f32[256,1024]{1,0:T(8,128)S(1)} collective-permute-done((f32[256,1024]{1,0:T(8,128)S(1)}, f32[256,1024]{1,0:T(8,128)S(1)}, u32[]{:S(2)}, u32[]{:S(2)}) %collective-permute-start.11) | collective-permute-done | bytes 1048608 | tf_op jit(solution)/shard_map/ppermute | solution.py:575
  75.5 0.0 copy-done.1
  75.5 0.0 copy-done.5
  75.5 0.0 copy-start.2
  75.5 1.0 %local.1 = f32[256,1024]{1,0:T(8,128)S(1)} custom-call(bf16[256,1024]{1,0:T(8,128)(2,1)S(1)} %copy-done.1, f32[256,1024]{1,0:T(8,128)S(1)} %get-tuple-element.55.y_own, f32[256,1024]{1,0:T(8,128)S(1)} %collective-permute-done.11.y_got, bf16[1024,1024]{1,0:T(8,128)(2,1)S(1)} %copy-done.5), custom_call_target="tpu_custom_call" | custom-call | flops 536870912 | bytes 4194304 | tf_op jit(solution)/shard_map/local/pallas_call | solution.py:578
  76.6 0.0 collective-permute-done.12.got
  76.6 0.0 copy-done.3
  76.6 0.0 copy-done.4
  76.6 1.1 %copy-done.2 = bf16[1024,2048]{1,0:T(8,128)(2,1)S(1)} copy-done((bf16[1024,2048]{1,0:T(8,128)(2,1)S(1)}, bf16[1024,2048]{1,0:T(8,128)(2,1)}, u32[]{:S(2)}) %copy-start.2) | copy-done | bytes 4194328
  77.7 4.9 %tail.1 = bf16[256,1024]{1,0:T(8,128)(2,1)} custom-call(bf16[256,1024]{1,0:T(8,128)(2,1)S(1)} %copy-done.1, f32[256,1024]{1,0:T(8,128)S(1)} %local.1, f32[32,512]{1,0:T(8,128)S(1)} %get-tuple-element.65.top, f32[32,512]{1,0:T(8,128)S(1)} %get-tuple-element.66.total, f32[1024,512]{1,0:T(8,128)S(1)} %get-tuple-element.67.acc, ...), custom_call_target="tpu_custom_call" | custom-call | flops 2684354560 | bytes 12582912 | tf_op jit(solution)/shard_map/tail/pallas_call | solution.py:587
  (1 shorter events, 0.0 us)
Async XLA Ops:
  0.0 1.0 %copy-start = (bf16[256,1024]{1,0:T(8,128)(2,1)S(1)}, bf16[256,1024]{1,0:T(8,128)(2,1)}, u32[]{:S(2)}) copy-start(bf16[256,1024]{1,0:T(8,128)(2,1)} %x.5) | copy-start | bytes 1572868
  1.0 0.7 copy-start.7
  1.8 5.1 %collective-permute-start.2 = (bf16[264,1024]{1,0:T(8,128)(2,1)S(1)}, bf16[264,1024]{1,0:T(8,128)(2,1)S(1)}, u32[]{:S(2)}, u32[]{:S(2)}) collective-permute-start(bf16[264,1024]{1,0:T(8,128)(2,1)S(1)} %pack.1.refs_0_.x), channel_id=1, source_target_pairs={{0,1},{1,0},{2,3},{3,2},{4,5},{5,4},{6,7},{7,6},{8,9},{9,8},{10,11... | collective-permute-start | bytes 1622024 | tf_op jit(solution)/shard_map/ppermute | solution.py:533
  2.4 15.5 %collective-permute-start = (bf16[264,1024]{1,0:T(8,128)(2,1)S(1)}, bf16[264,1024]{1,0:T(8,128)(2,1)S(1)}, u32[]{:S(2)}, u32[]{:S(2)}) collective-permute-start(bf16[264,1024]{1,0:T(8,128)(2,1)S(1)} %pack.1.refs_0_.x), channel_id=1, source_target_pairs={{0,2},{1,3},{2,0},{3,1},{4,6},{5,7},{6,4},{7,5},{8,10},{9,11},{10,... | collective-permute-start | bytes 1622024 | tf_op jit(solution)/shard_map/ppermute | solution.py:519
  5.0 12.9 %collective-permute-start.1 = (bf16[264,1024]{1,0:T(8,128)(2,1)S(1)}, bf16[264,1024]{1,0:T(8,128)(2,1)S(1)}, u32[]{:S(2)}, u32[]{:S(2)}) collective-permute-start(bf16[264,1024]{1,0:T(8,128)(2,1)S(1)} %pack.1.refs_0_.x), channel_id=1, source_target_pairs={{2,4},{3,5},{4,2},{5,3},{10,12},{11,13},{12,10},{13,11},{18,20},{1... | collective-permute-start | bytes 1622024 | tf_op jit(solution)/shard_map/ppermute | solution.py:519
  5.7 36.0 %collective-permute-start.7 = (bf16[2,16,128,128]{3,2,1,0:T(8,128)(2,1)}, bf16[2,16,128,128]{3,2,1,0:T(8,128)(2,1)S(1)}, u32[]{:S(2)}, u32[]{:S(2)}) collective-permute-start(bf16[2,16,128,128]{3,2,1,0:T(8,128)(2,1)} %refs_1_.1), channel_id=1, source_target_pairs={{0,1},{1,0},{2,3},{3,2},{4,5},{5,4},{6,7},{7,6},{8,9},{9,8},{10,11... | collective-permute-start | bytes 3145736 | tf_op jit(solution)/shard_map/ppermute | solution.py:534
  6.9 13.0 %copy-start.9 = (s32[1,4,128]{2,1,0:T(4,128)S(1)}, s32[1,4,128]{2,1,0:T(4,128)}, u32[]{:S(2)}) copy-start(s32[1,4,128]{2,1,0:T(4,128)} %lists.3) | copy-start | bytes 6148
  17.9 6.3 %collective-permute-start.3 = (bf16[264,1024]{1,0:T(8,128)(2,1)S(1)}, bf16[264,1024]{1,0:T(8,128)(2,1)S(1)}, u32[]{:S(2)}, u32[]{:S(2)}) collective-permute-start(bf16[264,1024]{1,0:T(8,128)(2,1)S(1)} %collective-permute-done.refs_0_.refs_3_), channel_id=1, source_target_pairs={{2,4},{3,5},{4,2},{5,3},{10,12},{11,13},{12,10},{13,11},{18,20},{1... | collective-permute-start | bytes 1622024 | tf_op jit(solution)/shard_map/ppermute | solution.py:519
  18.6 20.4 %collective-permute-start.4 = (bf16[264,1024]{1,0:T(8,128)(2,1)S(1)}, bf16[264,1024]{1,0:T(8,128)(2,1)S(1)}, u32[]{:S(2)}, u32[]{:S(2)}) collective-permute-start(bf16[264,1024]{1,0:T(8,128)(2,1)S(1)} %collective-permute-done.1.refs_4_.refs_0_), channel_id=1, source_target_pairs={{2,0},{3,1},{4,6},{5,7},{10,8},{11,9},{12,14},{13,15},{18,16},{19,... | collective-permute-start | bytes 1622024 | tf_op jit(solution)/shard_map/ppermute | solution.py:519
  20.9 20.7 %collective-permute-start.10 = (bf16[128,1024]{1,0:T(8,128)(2,1)S(1)}, bf16[128,1024]{1,0:T(8,128)(2,1)S(1)}, u32[]{:S(2)}, u32[]{:S(2)}) collective-permute-start(bf16[128,1024]{1,0:T(8,128)(2,1)S(1)} %get-tuple-element.51), channel_id=1, source_target_pairs={{0,24},{8,16},{16,8},{24,0},{1,25},{9,17},{17,9},{25,1},{2,26},{10... | collective-permute-start | bytes 786440 | tf_op jit(solution)/shard_map/ppermute | solution.py:551
  23.6 18.1 %collective-permute-start.8 = (bf16[128,1024]{1,0:T(8,128)(2,1)S(1)}, bf16[128,1024]{1,0:T(8,128)(2,1)S(1)}, u32[]{:S(2)}, u32[]{:S(2)}) collective-permute-start(bf16[128,1024]{1,0:T(8,128)(2,1)S(1)} %get-tuple-element.49), channel_id=1, source_target_pairs={{0,8},{8,0},{16,24},{24,16},{1,9},{9,1},{17,25},{25,17},{2,10},{10... | collective-permute-start | bytes 786440 | tf_op jit(solution)/shard_map/ppermute | solution.py:551
  24.1 17.5 %collective-permute-start.9 = (bf16[128,1024]{1,0:T(8,128)(2,1)S(1)}, bf16[128,1024]{1,0:T(8,128)(2,1)S(1)}, u32[]{:S(2)}, u32[]{:S(2)}) collective-permute-start(bf16[128,1024]{1,0:T(8,128)(2,1)S(1)} %get-tuple-element.50), channel_id=1, source_target_pairs={{0,16},{8,24},{16,0},{24,8},{1,17},{9,25},{17,1},{25,9},{2,18},{10... | collective-permute-start | bytes 786440 | tf_op jit(solution)/shard_map/ppermute | solution.py:551
  24.4 14.5 %copy-start.8 = (s32[2,16]{1,0:T(2,128)S(1)}, s32[2,16]{1,0:T(2,128)}, u32[]{:S(2)}) copy-start(s32[2,16]{1,0:T(2,128)} %nb_own.1) | copy-start | bytes 388
  24.5 17.2 %copy-start.6 = (bf16[2,16,128,128]{3,2,1,0:T(8,128)(2,1)S(1)}, bf16[2,16,128,128]{3,2,1,0:T(8,128)(2,1)}, u32[]{:S(2)}) copy-start(bf16[2,16,128,128]{3,2,1,0:T(8,128)(2,1)} %refs_1_.1) | copy-start | bytes 3145732
  39.0 1.2 %collective-permute-start.6 = (s32[2,16]{1,0:T(2,128)S(1)}, s32[2,16]{1,0:T(2,128)S(1)}, u32[]{:S(2)}, u32[]{:S(2)}) collective-permute-start(s32[2,16]{1,0:T(2,128)S(1)} %copy-done.8), channel_id=1, source_target_pairs={{0,1},{1,0},{2,3},{3,2},{4,5},{5,4},{6,7},{7,6},{8,9},{9,8},{10,11... | collective-permute-start | bytes 392 | tf_op jit(solution)/shard_map/ppermute | solution.py:535
  40.2 22.2 %collective-permute-start.5 = (bf16[264,1024]{1,0:T(8,128)(2,1)S(1)}, bf16[264,1024]{1,0:T(8,128)(2,1)S(1)}, u32[]{:S(2)}, u32[]{:S(2)}) collective-permute-start(bf16[264,1024]{1,0:T(8,128)(2,1)S(1)} %collective-permute-done.3.refs_0_), channel_id=1, source_target_pairs={{2,0},{3,1},{4,6},{5,7},{10,8},{11,9},{12,14},{13,15},{18,16},{19,... | collective-permute-start | bytes 1622024 | tf_op jit(solution)/shard_map/ppermute | solution.py:519
  63.6 11.9 %copy-start.1 = (bf16[256,1024]{1,0:T(8,128)(2,1)S(1)}, bf16[256,1024]{1,0:T(8,128)(2,1)}, u32[]{:S(2)}) copy-start(bf16[256,1024]{1,0:T(8,128)(2,1)} %x.5) | copy-start | bytes 1572868
  63.6 11.9 %copy-start.5 = (bf16[1024,1024]{1,0:T(8,128)(2,1)S(1)}, bf16[1024,1024]{1,0:T(8,128)(2,1)}, u32[]{:S(2)}) copy-start(bf16[1024,1024]{1,0:T(8,128)(2,1)} %w.1) | copy-start | bytes 6291460
  63.6 13.0 %copy-start.3 = (bf16[2048,1024]{1,0:T(8,128)(2,1)S(1)}, bf16[2048,1024]{1,0:T(8,128)(2,1)}, u32[]{:S(2)}) copy-start(bf16[2048,1024]{1,0:T(8,128)(2,1)} %w_down.1) | copy-start | bytes 12582916
  63.6 13.0 %copy-start.4 = (bf16[1024,1024]{1,0:T(8,128)(2,1)S(1)}, bf16[1024,1024]{1,0:T(8,128)(2,1)}, u32[]{:S(2)}) copy-start(bf16[1024,1024]{1,0:T(8,128)(2,1)} %w_out.1) | copy-start | bytes 6291460
  71.2 5.4 %collective-permute-start.12 = (f32[1088,256]{1,0:T(8,128)S(1)}, f32[1088,256]{1,0:T(8,128)S(1)}, u32[]{:S(2)}, u32[]{:S(2)}) collective-permute-start(f32[1088,256]{1,0:T(8,128)S(1)} %get-tuple-element.68), channel_id=1, source_target_pairs={{0,1},{1,0},{2,3},{3,2},{4,5},{5,4},{6,7},{7,6},{8,9},{9,8},{10,11... | collective-permute-start | bytes 3342344 | tf_op jit(solution)/shard_map/ppermute | solution.py:577
  71.3 4.2 %collective-permute-start.11 = (f32[256,1024]{1,0:T(8,128)S(1)}, f32[256,1024]{1,0:T(8,128)S(1)}, u32[]{:S(2)}, u32[]{:S(2)}) collective-permute-start(f32[256,1024]{1,0:T(8,128)S(1)} %get-tuple-element.61), channel_id=1, source_target_pairs={{0,1},{1,0},{2,3},{3,2},{4,5},{5,4},{6,7},{7,6},{8,9},{9,8},{10,11... | collective-permute-start | bytes 3145736 | tf_op jit(solution)/shard_map/ppermute | solution.py:575
  75.5 2.2 %copy-start.2 = (bf16[1024,2048]{1,0:T(8,128)(2,1)S(1)}, bf16[1024,2048]{1,0:T(8,128)(2,1)}, u32[]{:S(2)}) copy-start(bf16[1024,2048]{1,0:T(8,128)(2,1)} %w_up_all.1) | copy-start | bytes 12582916

commit v4 on v3

--- a/solution.py
+++ b/solution.py
@@ -172,12 +172,7 @@
     end = (chip == 0) | (chip == peers // CORES - 1)
     if step == 0:
         return me, end
-    if step == 1:
-        return me ^ CORES, end
-    near, across = 2 * CORES, 3 * CORES
-    if step == 2:
-        return me ^ jnp.where(end, near, across), end
-    return me ^ jnp.where(end, across, near), end
+    return me ^ (CORES * (1, 3, 2)[step - 1]), end
 
 
 def attend_kernel(mode, step, count, rows, block, peers, where, live, *refs):
@@ -558,22 +553,20 @@
         (step == 0, last), step, pieces, state, where, live, w_qkv, rows, block, peers
     )
     state = attend(0, [piece, mate_piece], None)
-    near, mid, state[2] = lax.optimization_barrier((near, mid, state[2]))
+    near, mid, to_far, state[2] = lax.optimization_barrier((near, mid, piece, state[2]))
+    ends = cross(to_far, [(0, 3), (3, 0)])
     to_end = cross(mid, outward)
     to_mid = cross(near, middle)
     state = attend(1, [near], state)
-    to_mid, to_end, state[2] = lax.optimization_barrier((to_mid, to_end, state[2]))
-    across = cross(to_mid, outward)
-    state = attend(2, [mid, to_end], state)
-    arrived = [near, mid, to_end]
+    state = attend(2, [mid, ends], state)
     sums = gather_call(
-        where, neighbor_blocks, mate_nb, piece, adj_tiles, mate_adj, arrived, (1, 2), far,
+        where, neighbor_blocks, mate_nb, piece, adj_tiles, mate_adj, [near, mid, ends], (1, 2), far,
         rows, slot, far_slot, block, peers,
     )
-    sums = gather_more_call(3, where, [to_mid, across], sums, rows, slot, block, peers)
+    sums = gather_more_call(3, where, [to_mid, to_end], sums, rows, slot, block, peers)
     y_send, state[2] = lax.optimization_barrier((sums[1], state[2]))
     y_got = lax.ppermute(y_send, "dev", swap)
-    send, top, total, acc = attend(3, [to_mid, across], state, True)
+    send, top, total, acc = attend(3, [to_mid, to_end], state, True)
     got = lax.ppermute(send, "dev", swap)
     local = pl.pallas_call(
         local_kernel,

time: 83.2 us -> 71.7 us (0.86)
  waiting for transfers between devices: 23.5 us -> 8.04 us
  starting transfers between devices: 11.7 us -> 14.9 us
    ppermute x5, waiting for transfers between devices: 18.6 us -> 3.13 us  [cross(): return lax.ppermute(value, 'dev', lanes)]
    ppermute x5, starting transfers between devices: 6.76 us -> 9.85 us  [cross(): return lax.ppermute(value, 'dev', lanes)]
  transfers between devices with their start and end apart: 13 -> 13, of which waited for: 5 -> 4; matrix products, arithmetic and copies ran while one was open for 1% -> 1% of each run, Pallas kernels for 36% -> 42%
where the time goes in v4:
time: 71.7 us; the launch traced here: 71.3 us
  Pallas kernels  43.4 us (61%)
  starting transfers between devices  14.9 us (21%)
  waiting for transfers between devices  8.04 us (11%)
  local copies, waits for them, and re-layouts  3.59 us (5%)
  other arithmetic  0.95 us (1%)
    pallas_call x4, Pallas kernels, attend_call(): pl.pallas_call(functools.partial(attend_kernel, mode, step, len(pieces),...  32.2 us
    ppermute x5, starting transfers between devices, cross(): return lax.ppermute(value, 'dev', lanes)  9.85 us
    pallas_call x1, Pallas kernels, line_plan(): pl.pallas_call(functools.partial(tail_kernel, rows), in_specs=[VMEM] * 7...  4.94 us
    ppermute x1, waiting for transfers between devices, line_plan(): y_got = lax.ppermute(y_send, 'dev', swap)  3.74 us
    ppermute x3, starting transfers between devices, line_plan(): far.append(lax.ppermute(picked[s], 'group', pairs))  3.63 us
    unnamed x20, local copies, waits for them, and re-layouts  3.59 us
    ppermute x5, waiting for transfers between devices, cross(): return lax.ppermute(value, 'dev', lanes)  3.13 us
    pallas_call x1, Pallas kernels, gather_call(): pl.pallas_call(functools.partial(gather_kernel, steps, len(far), rows, sl...  2.88 us
  transfers between devices with their start and end apart: 13, of which 4 were waited for; matrix products, arithmetic and copies ran while one was open for 1% of the time, Pallas kernels for 42%

profile of v4, /device:TPU:0, one launch (start us, length us, event | category | flops | bytes accessed | tf_op | source)
XLA Modules:
  0.0 71.3 jit_solution(1695287904716681650)
XLA Ops:
  0.0 0.0 copy-start
  0.0 1.0 %copy-done = bf16[256,1024]{1,0:T(8,128)(2,1)S(1)} copy-done((bf16[256,1024]{1,0:T(8,128)(2,1)S(1)}, bf16[256,1024]{1,0:T(8,128)(2,1)}, u32[]{:S(2)}) %copy-start) | copy-done | bytes 524312
  1.0 0.0 copy-start.7
  1.0 0.7 copy-done.7
  1.8 0.6 collective-permute-start.2
  2.4 2.6 %collective-permute-start = (bf16[264,1024]{1,0:T(8,128)(2,1)S(1)}, bf16[264,1024]{1,0:T(8,128)(2,1)S(1)}, u32[]{:S(2)}, u32[]{:S(2)}) collective-permute-start(bf16[264,1024]{1,0:T(8,128)(2,1)S(1)} %pack.1.refs_0_.x), channel_id=1, source_target_pairs={{0,2},{1,3},{2,0},{3,1},{4,6},{5,7},{6,4},{7,5},{8,10},{9,11},{10,... | collective-permute-start | bytes 1622024 | tf_op jit(solution)/shard_map/ppermute | solution.py:514
  5.0 0.7 collective-permute-start.1
  5.7 0.2 collective-permute-start.6
  5.9 0.1 pad_add_fusion.where
  6.0 0.0 copy-start.9
  6.0 0.7 copy-done.9
  6.7 1.0 %pick.1 = (bf16[128,1024]{1,0:T(8,128)(2,1)S(1)}, bf16[128,1024]{1,0:T(8,128)(2,1)S(1)}, bf16[128,1024]{1,0:T(8,128)(2,1)S(1)}, bf16[128,1024]{1,0:T(8,128)(2,1)S(1)}) custom-call(s32[2]{0:T(128)S(1)} %pad_add_fusion.where, s32[1,4,128]{2,1,0:T(4,128)S(1)} %copy-done.9, bf16[264,1024]{1,0:T(8,128)(2,1)S(1)} %pack.1.refs_0_.x), custom_call_target="tpu_custom_call" | custom-call | flops 268435456 | bytes 1048576 | tf_op jit(solution)/shard_map/pick/pallas_call | solution.py:532
  7.7 2.5 %collective-permute-start.10 = (bf16[128,1024]{1,0:T(8,128)(2,1)S(1)}, bf16[128,1024]{1,0:T(8,128)(2,1)S(1)}, u32[]{:S(2)}, u32[]{:S(2)}) collective-permute-start(bf16[128,1024]{1,0:T(8,128)(2,1)S(1)} %get-tuple-element.42), channel_id=1, source_target_pairs={{0,24},{8,16},{16,8},{24,0},{1,25},{9,17},{17,9},{25,1},{2,26},{10... | collective-permute-start | bytes 786440 | tf_op jit(solution)/shard_map/ppermute | solution.py:546
  10.2 0.9 %select_reduce_fusion.live = s32[16]{0:T(128)S(1)} fusion(s32[16,16]{1,0:T(8,128)} %param.19, s32[16]{0:T(128)} %param.20), kind=kLoop, calls=%fused_computation | loop fusion | flops 1008 | bytes 1152 | tf_op jit(solution)/shard_map/reduce_sum | solution.py:549
  11.1 0.0 collective-permute-done.2.refs_1_
  11.1 0.0 copy-start.8
  11.1 0.6 collective-permute-start.8
  11.7 9.8 %shard_map.118 = (bf16[1024,512]{1,0:T(8,128)(2,1)S(1)}, bf16[1024,2048]{1,0:T(8,128)(2,1)S(1)}, f32[32,512]{1,0:T(8,128)S(1)}, f32[32,512]{1,0:T(8,128)S(1)}, f32[1024,512]{1,0:T(8,128)S(1)}) custom-call(s32[2]{0:T(128)S(1)} %pad_add_fusion.where, s32[16]{0:T(128)S(1)} %select_reduce_fusion.live, bf16[264,1024]{1,0:T(8,128)(2,1)S(1)} %pack.1.refs_0_.x, ...), custom_call_target="tpu_custom_call" | custom-call | flops 3221225472 | bytes 4194304 | tf_op jit(solution)/shard_map/pallas_call | solution.py:328
  21.5 0.0 collective-permute-done.refs_3_.refs_0_
  21.5 0.0 collective-permute-done.1.refs_4_.refs_0_
  21.5 4.4 %collective-permute-start.7 = (bf16[264,1024]{1,0:T(8,128)(2,1)S(1)}, bf16[264,1024]{1,0:T(8,128)(2,1)S(1)}, u32[]{:S(2)}, u32[]{:S(2)}) collective-permute-start(bf16[264,1024]{1,0:T(8,128)(2,1)S(1)} %pack.1.refs_0_.x), channel_id=1, source_target_pairs={{0,6},{1,7},{6,0},{7,1},{8,14},{9,15},{14,8},{15,9},{16,22},{17,23... | collective-permute-start | bytes 1622024 | tf_op jit(solution)/shard_map/ppermute | solution.py:514
  25.9 0.0 copy-done.8
  25.9 0.1 collective-permute-start.5
  26.0 1.1 %collective-permute-done.5.nb_mate = s32[2,16]{1,0:T(2,128)S(1)} collective-permute-done((s32[2,16]{1,0:T(2,128)S(1)}, s32[2,16]{1,0:T(2,128)S(1)}, u32[]{:S(2)}, u32[]{:S(2)}) %collective-permute-start.5) | collective-permute-done | bytes 160 | tf_op jit(solution)/shard_map/ppermute | solution.py:530
  27.1 0.5 collective-permute-start.9
  27.6 0.0 collective-permute-done.10.refs_9_
  27.6 0.7 collective-permute-start.3
  28.3 0.0 collective-permute-done.8.refs_7_
  28.3 1.5 %collective-permute-start.4 = (bf16[264,1024]{1,0:T(8,128)(2,1)S(1)}, bf16[264,1024]{1,0:T(8,128)(2,1)S(1)}, u32[]{:S(2)}, u32[]{:S(2)}) collective-permute-start(bf16[264,1024]{1,0:T(8,128)(2,1)S(1)} %collective-permute-done.1.refs_4_.refs_0_), channel_id=1, source_target_pairs={{2,0},{3,1},{4,6},{5,7},{10,8},{11,9},{12,14},{13,15},{18,16},{19,... | collective-permute-start | bytes 1622024 | tf_op jit(solution)/shard_map/ppermute | solution.py:514
  29.8 0.0 copy-start.6
  29.8 7.4 %shard_map.119 = (f32[32,512]{1,0:T(8,128)S(1)}, f32[32,512]{1,0:T(8,128)S(1)}, f32[1024,512]{1,0:T(8,128)S(1)}) custom-call(s32[2]{0:T(128)S(1)} %pad_add_fusion.where, s32[16]{0:T(128)S(1)} %select_reduce_fusion.live, bf16[264,1024]{1,0:T(8,128)(2,1)S(1)} %collective-permute-done.refs_3_.refs_0_, ...), custom_call_target="tpu_custom_call", output_to_operand_aliasing={{0}: (5, {}), {1}: (6, {}), {2}: (7, {})} | custom-call | flops 3221225472 | bytes 4194304 | tf_op jit(solution)/shard_map/pallas_call | solution.py:328
  37.3 0.0 collective-permute-done.9.refs_8_
  37.3 0.0 collective-permute-done.6.refs_2_
  37.3 2.0 %collective-permute-done.7.refs_5_.refs_1_ = bf16[264,1024]{1,0:T(8,128)(2,1)S(1)} collective-permute-done((bf16[264,1024]{1,0:T(8,128)(2,1)S(1)}, bf16[264,1024]{1,0:T(8,128)(2,1)S(1)}, u32[]{:S(2)}, u32[]{:S(2)}) %collective-permute-start.7) | collective-permute-done | bytes 540704 | tf_op jit(solution)/shard_map/ppermute | solution.py:514
  39.3 0.0 copy-done.6
  39.3 2.9 %gather.1 = (f32[256,1024]{1,0:T(8,128)S(1)}, f32[256,1024]{1,0:T(8,128)S(1)}, bf16[2,22,256,128]{3,2,1,0:T(8,128)(2,1)S(1)}) custom-call(s32[2]{0:T(128)S(1)} %pad_add_fusion.where, s32[2,16]{1,0:T(2,128)S(1)} %copy-done.8, s32[2,16]{1,0:T(2,128)S(1)} %collective-permute-done.5.nb_mate, bf16[264,1024]{1,0:T(8,128)(2,1)S(1)} %pack.1.refs_0_.x, ...), custom_call_target="tpu_custom_call" | custom-call | flops 1073741824 | bytes 8388608 | tf_op jit(solution)/shard_map/gather/pallas_call | solution.py:601
  42.2 7.5 %shard_map.120 = (f32[32,512]{1,0:T(8,128)S(1)}, f32[32,512]{1,0:T(8,128)S(1)}, f32[1024,512]{1,0:T(8,128)S(1)}) custom-call(s32[2]{0:T(128)S(1)} %pad_add_fusion.where, s32[16]{0:T(128)S(1)} %select_reduce_fusion.live, bf16[264,1024]{1,0:T(8,128)(2,1)S(1)} %collective-permute-done.1.refs_4_.refs_0_, ...), custom_call_target="tpu_custom_call", output_to_operand_aliasing={{0}: (6, {}), {1}: (7, {}), {2}: (8, {})} | custom-call | flops 3221225472 | bytes 4194304 | tf_op jit(solution)/shard_map/pallas_call | solution.py:328
  49.7 0.0 collective-permute-done.3.refs_0_
  49.7 1.1 %collective-permute-done.4.refs_1_ = bf16[264,1024]{1,0:T(8,128)(2,1)S(1)} collective-permute-done((bf16[264,1024]{1,0:T(8,128)(2,1)S(1)}, bf16[264,1024]{1,0:T(8,128)(2,1)S(1)}, u32[]{:S(2)}, u32[]{:S(2)}) %collective-permute-start.4) | collective-permute-done | bytes 540704 | tf_op jit(solution)/shard_map/ppermute | solution.py:514
  50.8 1.2 %gather_more.1 = (f32[256,1024]{1,0:T(8,128)S(1)}, f32[256,1024]{1,0:T(8,128)S(1)}) custom-call(s32[2]{0:T(128)S(1)} %pad_add_fusion.where, bf16[264,1024]{1,0:T(8,128)(2,1)S(1)} %collective-permute-done.3.refs_0_, bf16[264,1024]{1,0:T(8,128)(2,1)S(1)} %collective-permute-done.4.refs_1_, ...), custom_call_target="tpu_custom_call", output_to_operand_aliasing={{0}: (4, {}), {1}: (5, {})} | custom-call | flops 268435456 | bytes 4194304 | tf_op jit(solution)/shard_map/gather_more/pallas_call | solution.py:616
  52.1 0.0 copy-start.1
  52.1 0.0 copy-start.5
  52.1 0.0 copy-start.3
  52.1 0.0 copy-start.4
  52.1 7.5 %shard_map.121 = (f32[1088,256]{1,0:T(8,128)S(1)}, f32[32,512]{1,0:T(8,128)S(1)}, f32[32,512]{1,0:T(8,128)S(1)}, f32[1024,512]{1,0:T(8,128)S(1)}) custom-call(s32[2]{0:T(128)S(1)} %pad_add_fusion.where, s32[16]{0:T(128)S(1)} %select_reduce_fusion.live, ...), custom_call_target="tpu_custom_call", output_to_operand_aliasing={{1}: (6, {}), {2}: (7, {}), {3}: (8, {})} | custom-call | flops 3221225472 | bytes 4194304 | tf_op jit(solution)/shard_map/pallas_call | solution.py:328
  59.6 0.1 collective-permute-start.12
  59.7 0.5 collective-permute-start.11
  60.2 3.7 %collective-permute-done.11.y_got = f32[256,1024]{1,0:T(8,128)S(1)} collective-permute-done((f32[256,1024]{1,0:T(8,128)S(1)}, f32[256,1024]{1,0:T(8,128)S(1)}, u32[]{:S(2)}, u32[]{:S(2)}) %collective-permute-start.11) | collective-permute-done | bytes 1048608 | tf_op jit(solution)/shard_map/ppermute | solution.py:568
  64.0 0.0 copy-done.1
  64.0 0.0 copy-done.5
  64.0 0.0 copy-start.2
  64.0 1.0 %local.1 = f32[256,1024]{1,0:T(8,128)S(1)} custom-call(bf16[256,1024]{1,0:T(8,128)(2,1)S(1)} %copy-done.1, f32[256,1024]{1,0:T(8,128)S(1)} %get-tuple-element.46.y_own, f32[256,1024]{1,0:T(8,128)S(1)} %collective-permute-done.11.y_got, bf16[1024,1024]{1,0:T(8,128)(2,1)S(1)} %copy-done.5), custom_call_target="tpu_custom_call" | custom-call | flops 536870912 | bytes 4194304 | tf_op jit(solution)/shard_map/local/pallas_call | solution.py:571
  65.0 0.0 collective-permute-done.12.got
  65.0 0.0 copy-done.3
  65.0 0.0 copy-done.4
  65.0 1.1 %copy-done.2 = bf16[1024,2048]{1,0:T(8,128)(2,1)S(1)} copy-done((bf16[1024,2048]{1,0:T(8,128)(2,1)S(1)}, bf16[1024,2048]{1,0:T(8,128)(2,1)}, u32[]{:S(2)}) %copy-start.2) | copy-done | bytes 4194328
  66.2 4.9 %tail.1 = bf16[256,1024]{1,0:T(8,128)(2,1)} custom-call(bf16[256,1024]{1,0:T(8,128)(2,1)S(1)} %copy-done.1, f32[256,1024]{1,0:T(8,128)S(1)} %local.1, f32[32,512]{1,0:T(8,128)S(1)} %get-tuple-element.61.top, f32[32,512]{1,0:T(8,128)S(1)} %get-tuple-element.62.total, f32[1024,512]{1,0:T(8,128)S(1)} %get-tuple-element.63.acc, ...), custom_call_target="tpu_custom_call" | custom-call | flops 2684354560 | bytes 12582912 | tf_op jit(solution)/shard_map/tail/pallas_call | solution.py:580
  (1 shorter events, 0.0 us)
Async XLA Ops:
  0.0 1.0 %copy-start = (bf16[256,1024]{1,0:T(8,128)(2,1)S(1)}, bf16[256,1024]{1,0:T(8,128)(2,1)}, u32[]{:S(2)}) copy-start(bf16[256,1024]{1,0:T(8,128)(2,1)} %x.5) | copy-start | bytes 1572868
  1.0 0.7 copy-start.7
  1.8 9.3 %collective-permute-start.2 = (bf16[264,1024]{1,0:T(8,128)(2,1)S(1)}, bf16[264,1024]{1,0:T(8,128)(2,1)S(1)}, u32[]{:S(2)}, u32[]{:S(2)}) collective-permute-start(bf16[264,1024]{1,0:T(8,128)(2,1)S(1)} %pack.1.refs_0_.x), channel_id=1, source_target_pairs={{0,1},{1,0},{2,3},{3,2},{4,5},{5,4},{6,7},{7,6},{8,9},{9,8},{10,11... | collective-permute-start | bytes 1622024 | tf_op jit(solution)/shard_map/ppermute | solution.py:528
  2.4 19.1 %collective-permute-start = (bf16[264,1024]{1,0:T(8,128)(2,1)S(1)}, bf16[264,1024]{1,0:T(8,128)(2,1)S(1)}, u32[]{:S(2)}, u32[]{:S(2)}) collective-permute-start(bf16[264,1024]{1,0:T(8,128)(2,1)S(1)} %pack.1.refs_0_.x), channel_id=1, source_target_pairs={{0,2},{1,3},{2,0},{3,1},{4,6},{5,7},{6,4},{7,5},{8,10},{9,11},{10,... | collective-permute-start | bytes 1622024 | tf_op jit(solution)/shard_map/ppermute | solution.py:514
  5.0 16.5 %collective-permute-start.1 = (bf16[264,1024]{1,0:T(8,128)(2,1)S(1)}, bf16[264,1024]{1,0:T(8,128)(2,1)S(1)}, u32[]{:S(2)}, u32[]{:S(2)}) collective-permute-start(bf16[264,1024]{1,0:T(8,128)(2,1)S(1)} %pack.1.refs_0_.x), channel_id=1, source_target_pairs={{2,4},{3,5},{4,2},{5,3},{10,12},{11,13},{12,10},{13,11},{18,20},{1... | collective-permute-start | bytes 1622024 | tf_op jit(solution)/shard_map/ppermute | solution.py:514
  5.7 31.6 %collective-permute-start.6 = (bf16[2,16,128,128]{3,2,1,0:T(8,128)(2,1)}, bf16[2,16,128,128]{3,2,1,0:T(8,128)(2,1)S(1)}, u32[]{:S(2)}, u32[]{:S(2)}) collective-permute-start(bf16[2,16,128,128]{3,2,1,0:T(8,128)(2,1)} %refs_1_.1), channel_id=1, source_target_pairs={{0,1},{1,0},{2,3},{3,2},{4,5},{5,4},{6,7},{7,6},{8,9},{9,8},{10,11... | collective-permute-start | bytes 3145736 | tf_op jit(solution)/shard_map/ppermute | solution.py:529
  6.0 0.7 copy-start.9
  7.7 20.0 %collective-permute-start.10 = (bf16[128,1024]{1,0:T(8,128)(2,1)S(1)}, bf16[128,1024]{1,0:T(8,128)(2,1)S(1)}, u32[]{:S(2)}, u32[]{:S(2)}) collective-permute-start(bf16[128,1024]{1,0:T(8,128)(2,1)S(1)} %get-tuple-element.42), channel_id=1, source_target_pairs={{0,24},{8,16},{16,8},{24,0},{1,25},{9,17},{17,9},{25,1},{2,26},{10... | collective-permute-start | bytes 786440 | tf_op jit(solution)/shard_map/ppermute | solution.py:546
  11.1 14.8 %copy-start.8 = (s32[2,16]{1,0:T(2,128)S(1)}, s32[2,16]{1,0:T(2,128)}, u32[]{:S(2)}) copy-start(s32[2,16]{1,0:T(2,128)} %nb_own.1) | copy-start | bytes 388
  11.1 17.2 %collective-permute-start.8 = (bf16[128,1024]{1,0:T(8,128)(2,1)S(1)}, bf16[128,1024]{1,0:T(8,128)(2,1)S(1)}, u32[]{:S(2)}, u32[]{:S(2)}) collective-permute-start(bf16[128,1024]{1,0:T(8,128)(2,1)S(1)} %get-tuple-element.40), channel_id=1, source_target_pairs={{0,8},{8,0},{16,24},{24,16},{1,9},{9,1},{17,25},{25,17},{2,10},{10... | collective-permute-start | bytes 786440 | tf_op jit(solution)/shard_map/ppermute | solution.py:546
  21.5 17.8 %collective-permute-start.7 = (bf16[264,1024]{1,0:T(8,128)(2,1)S(1)}, bf16[264,1024]{1,0:T(8,128)(2,1)S(1)}, u32[]{:S(2)}, u32[]{:S(2)}) collective-permute-start(bf16[264,1024]{1,0:T(8,128)(2,1)S(1)} %pack.1.refs_0_.x), channel_id=1, source_target_pairs={{0,6},{1,7},{6,0},{7,1},{8,14},{9,15},{14,8},{15,9},{16,22},{17,23... | collective-permute-start | bytes 1622024 | tf_op jit(solution)/shard_map/ppermute | solution.py:514
  25.9 1.2 %collective-permute-start.5 = (s32[2,16]{1,0:T(2,128)S(1)}, s32[2,16]{1,0:T(2,128)S(1)}, u32[]{:S(2)}, u32[]{:S(2)}) collective-permute-start(s32[2,16]{1,0:T(2,128)S(1)} %copy-done.8), channel_id=1, source_target_pairs={{0,1},{1,0},{2,3},{3,2},{4,5},{5,4},{6,7},{7,6},{8,9},{9,8},{10,11... | collective-permute-start | bytes 392 | tf_op jit(solution)/shard_map/ppermute | solution.py:530
  27.1 10.2 %collective-permute-start.9 = (bf16[128,1024]{1,0:T(8,128)(2,1)S(1)}, bf16[128,1024]{1,0:T(8,128)(2,1)S(1)}, u32[]{:S(2)}, u32[]{:S(2)}) collective-permute-start(bf16[128,1024]{1,0:T(8,128)(2,1)S(1)} %get-tuple-element.41), channel_id=1, source_target_pairs={{0,16},{8,24},{16,0},{24,8},{1,17},{9,25},{17,1},{25,9},{2,18},{10... | collective-permute-start | bytes 786440 | tf_op jit(solution)/shard_map/ppermute | solution.py:546
  27.6 22.1 %collective-permute-start.3 = (bf16[264,1024]{1,0:T(8,128)(2,1)S(1)}, bf16[264,1024]{1,0:T(8,128)(2,1)S(1)}, u32[]{:S(2)}, u32[]{:S(2)}) collective-permute-start(bf16[264,1024]{1,0:T(8,128)(2,1)S(1)} %collective-permute-done.refs_3_.refs_0_), channel_id=1, source_target_pairs={{2,4},{3,5},{4,2},{5,3},{10,12},{11,13},{12,10},{13,11},{18,20},{1... | collective-permute-start | bytes 1622024 | tf_op jit(solution)/shard_map/ppermute | solution.py:514
  28.3 22.5 %collective-permute-start.4 = (bf16[264,1024]{1,0:T(8,128)(2,1)S(1)}, bf16[264,1024]{1,0:T(8,128)(2,1)S(1)}, u32[]{:S(2)}, u32[]{:S(2)}) collective-permute-start(bf16[264,1024]{1,0:T(8,128)(2,1)S(1)} %collective-permute-done.1.refs_4_.refs_0_), channel_id=1, source_target_pairs={{2,0},{3,1},{4,6},{5,7},{10,8},{11,9},{12,14},{13,15},{18,16},{19,... | collective-permute-start | bytes 1622024 | tf_op jit(solution)/shard_map/ppermute | solution.py:514
  29.8 9.5 %copy-start.6 = (bf16[2,16,128,128]{3,2,1,0:T(8,128)(2,1)S(1)}, bf16[2,16,128,128]{3,2,1,0:T(8,128)(2,1)}, u32[]{:S(2)}) copy-start(bf16[2,16,128,128]{3,2,1,0:T(8,128)(2,1)} %refs_1_.1) | copy-start | bytes 3145732
  52.1 11.9 %copy-start.1 = (bf16[256,1024]{1,0:T(8,128)(2,1)S(1)}, bf16[256,1024]{1,0:T(8,128)(2,1)}, u32[]{:S(2)}) copy-start(bf16[256,1024]{1,0:T(8,128)(2,1)} %x.5) | copy-start | bytes 1572868
  52.1 11.9 %copy-start.5 = (bf16[1024,1024]{1,0:T(8,128)(2,1)S(1)}, bf16[1024,1024]{1,0:T(8,128)(2,1)}, u32[]{:S(2)}) copy-start(bf16[1024,1024]{1,0:T(8,128)(2,1)} %w.1) | copy-start | bytes 6291460
  52.1 12.9 %copy-start.3 = (bf16[2048,1024]{1,0:T(8,128)(2,1)S(1)}, bf16[2048,1024]{1,0:T(8,128)(2,1)}, u32[]{:S(2)}) copy-start(bf16[2048,1024]{1,0:T(8,128)(2,1)} %w_down.1) | copy-start | bytes 12582916
  52.1 12.9 %copy-start.4 = (bf16[1024,1024]{1,0:T(8,128)(2,1)S(1)}, bf16[1024,1024]{1,0:T(8,128)(2,1)}, u32[]{:S(2)}) copy-start(bf16[1024,1024]{1,0:T(8,128)(2,1)} %w_out.1) | copy-start | bytes 6291460
  59.6 5.4 %collective-permute-start.12 = (f32[1088,256]{1,0:T(8,128)S(1)}, f32[1088,256]{1,0:T(8,128)S(1)}, u32[]{:S(2)}, u32[]{:S(2)}) collective-permute-start(f32[1088,256]{1,0:T(8,128)S(1)} %get-tuple-element.64), channel_id=1, source_target_pairs={{0,1},{1,0},{2,3},{3,2},{4,5},{5,4},{6,7},{7,6},{8,9},{9,8},{10,11... | collective-permute-start | bytes 3342344 | tf_op jit(solution)/shard_map/ppermute | solution.py:570
  59.7 4.2 %collective-permute-start.11 = (f32[256,1024]{1,0:T(8,128)S(1)}, f32[256,1024]{1,0:T(8,128)S(1)}, u32[]{:S(2)}, u32[]{:S(2)}) collective-permute-start(f32[256,1024]{1,0:T(8,128)S(1)} %get-tuple-element.57), channel_id=1, source_target_pairs={{0,1},{1,0},{2,3},{3,2},{4,5},{5,4},{6,7},{7,6},{8,9},{9,8},{10,11... | collective-permute-start | bytes 3145736 | tf_op jit(solution)/shard_map/ppermute | solution.py:568
  64.0 2.2 %copy-start.2 = (bf16[1024,2048]{1,0:T(8,128)(2,1)S(1)}, bf16[1024,2048]{1,0:T(8,128)(2,1)}, u32[]{:S(2)}) copy-start(bf16[1024,2048]{1,0:T(8,128)(2,1)} %w_up_all.1) | copy-start | bytes 12582916
